TPU v7x, 512 devices: a whole 4x4x16 slice. The times are simulated.
512 devices in a mesh: gx: 16 (over z), gy: 16 (over x, y_hi, core), gz: 2 (over y_lo).
Axes of the slice: x: 4, y: 4 (y_hi: 2, y_lo: 2; y = y_hi * 2 + y_lo), z: 16, core: 2. Of those that a mesh axis runs over, the one named last changes fastest.
Arguments:
- displacement: float32 [3, 16, 512, 2048], P(None, 'gz', 'gx', 'gy'), may hold values from -6 to 6
- load: float32 [3, 16, 512, 2048], P(None, 'gz', 'gx', 'gy'), may hold values from -6 to 6
- density_code: int32 [16, 512, 2048], P('gz', 'gx', 'gy'), may hold values from 0 to 15
- fixed_mask: int32 [3, 16, 512, 2048], P(None, 'gz', 'gx', 'gy'), may hold values from 0 to 1, as said below
Outputs:
- improved: float32 [3, 16, 512, 2048], P(None, 'gz', 'gx', 'gy')
Inputs may be any that keep to these rules, and one draw needn't show every extreme that they name: `fixed_mask`: 1 on all three components of the nodes of a few rectangular support patches in the first layer along the first dimension, and on a few scattered components elsewhere.
All inputs are finite; a program needn't handle non-finite values.
Results may differ from a plain program's by a relative error of at most 0.0001.
Values sent between devices are 32-bit elements; how exact they have to be, the bound alone decides.
No kernel may reach another device: no remote copies, remote signals or barrier semaphores. Data moves between devices by JAX's collectives and lax.ppermute only.
A program may use at most 128 MiB of HBM per device.

v0:
```python
import functools

import jax
import jax.numpy as jnp
import numpy as np
from jax import lax
from jax.sharding import PartitionSpec as P

NU = 2
COARSE = 4
LEVELS = 16


EMIN = 0.001
OMEGA = 0.5


def padded_2(block, sides, width):
    for axis, dim in sides:
        count = lax.axis_size(axis)
        forward = [(i, i + 1) for i in range(count - 1)]
        backward = [(target, source) for source, target in forward]
        low = lax.ppermute(
            lax.slice_in_dim(block, block.shape[dim] - width, None, axis=dim), axis, forward
        )
        high = lax.ppermute(lax.slice_in_dim(block, 0, width, axis=dim), axis, backward)
        block = jnp.concatenate([low, block, high], axis=dim)
    return block


def shifted(value, axis, steps):
    count = lax.axis_size(axis)
    leading, last = (max(0, -steps), min(count, count - steps))
    return lax.ppermute(value, axis, [(source, source + steps) for source in range(leading, last)])


def partner_2(block, axis, stride):
    count = lax.axis_size(axis)
    route = []
    for low in range(count):
        high = low | 1 << stride
        if high != low and high < count:
            route += [(low, high), (high, low)]
    return lax.ppermute(block, axis, route)


def corner(index):
    return (index >> 2 & 1, index >> 1 & 1, index & 1)


def element_matrix():
    poisson = 0.3
    lame_first = poisson / ((1 + poisson) * (1 - 2 * poisson))
    shear = 1 / (2 * (1 + poisson))
    elastic = np.zeros((6, 6))
    elastic[:3, :3] = lame_first
    for d in range(3):
        elastic[d, d] = lame_first + 2 * shear
        elastic[3 + d, 3 + d] = shear
    offset_gauss = 0.5 / np.sqrt(3.0)
    points = (0.5 - offset_gauss, 0.5 + offset_gauss)
    stiffness = np.zeros((24, 24))
    for px in points:
        for py in points:
            for pz in points:
                place = (px, py, pz)
                strain = np.zeros((6, 24))
                for a in range(8):
                    o = corner(a)
                    shapes = [place[d] if o[d] else 1 - place[d] for d in range(3)]
                    slopes = [1.0 if o[d] else -1.0 for d in range(3)]
                    gradient = [
                        slopes[0] * shapes[1] * shapes[2],
                        shapes[0] * slopes[1] * shapes[2],
                        shapes[0] * shapes[1] * slopes[2],
                    ]
                    c = 3 * a
                    strain[0, c] = gradient[0]
                    strain[1, c + 1] = gradient[1]
                    strain[2, c + 2] = gradient[2]
                    strain[3, c] = gradient[1]
                    strain[3, c + 1] = gradient[0]
                    strain[4, c + 1] = gradient[2]
                    strain[4, c + 2] = gradient[1]
                    strain[5, c] = gradient[2]
                    strain[5, c + 2] = gradient[0]
                stiffness += strain.T @ elastic @ strain / 8.0
    return stiffness


def stencil(padded_u, padded_s, spacing):
    stiffness = element_matrix()
    extent = (padded_s.shape[0] - 2, padded_s.shape[1] - 2, padded_s.shape[2] - 2)

    def window(array, start):
        return array[
            ...,
            start[0] : start[0] + extent[0],
            start[1] : start[1] + extent[1],
            start[2] : start[2] + extent[2],
        ]

    forces = [None, None, None]
    diagonal = [None, None, None]
    for a in range(8):
        oa = corner(a)
        weight = window(padded_s, tuple((1 - oa[d] for d in range(3))))
        for i in range(3):
            terms = []
            for b in range(8):
                ob = corner(b)
                moved = tuple((1 - oa[d] + ob[d] for d in range(3)))
                for j in range(3):
                    coeff = float(stiffness[3 * a + i, 3 * b + j])
                    if abs(coeff) > 1e-12:
                        terms.append(coeff * window(padded_u[j], moved))
            part = weight * functools.reduce(jnp.add, terms)
            forces[i] = part if forces[i] is None else forces[i] + part
            piece = float(stiffness[3 * a + i, 3 * a + i]) * weight
            diagonal[i] = piece if diagonal[i] is None else diagonal[i] + piece
    return (spacing * jnp.stack(forces), spacing * jnp.stack(diagonal))


def pad_faces(stacked):
    return padded_2(stacked, (("gx", 2), ("gy", 3), ("gz", 1)), 1)


def level_apply(scales, spacing):

    def apply(field):
        padded = pad_faces(jnp.concatenate([field, scales[None]], 0))
        return stencil(padded[:3], padded[3], spacing)

    return apply


def pad_group(stacked):
    lower = shifted(stacked[:, :, -1:], "gx", 2)
    upper = shifted(stacked[:, :, :1], "gx", -2)
    stacked = jnp.concatenate([lower, stacked, upper], 2)
    lower = shifted(stacked[:, :, :, -1:], "gy", 2)
    upper = shifted(stacked[:, :, :, :1], "gy", -2)
    stacked = jnp.concatenate([lower, stacked, upper], 3)
    return jnp.pad(stacked, ((0, 0), (1, 1), (0, 0), (0, 0)))


def smooth(field, rhs, free, apply, sweeps):
    for sweep in range(sweeps):
        product, diagonal = apply(field)
        field = field + OMEGA * free * (rhs - product) / diagonal
    return field


def residual(field, rhs, free, apply):
    product, diagonal = apply(field)
    return free * (rhs - product)


def coarsen(array, reducer):
    lead = array.shape[:-3]
    ex, ey, ez = array.shape[-3:]
    shaped = array.reshape(lead + (ex // 2, 2, ey // 2, 2, ez // 2, 2))
    return reducer(shaped, axis=(-5, -3, -1))


def refine(array):
    return jnp.repeat(jnp.repeat(jnp.repeat(array, 2, -3), 2, -2), 2, -1)


def coarse_grouped(rhs2, scales2, free2):
    depth, ex, ey = scales2.shape
    stacked = jnp.concatenate([rhs2, scales2[None], free2], 0)
    block = lax.all_gather(stacked, "gz", axis=1, tiled=True)
    partner = partner_2(block, "gx", 0)
    odd_x = lax.axis_index("gx") % 2 == 1
    block = jnp.where(
        odd_x, jnp.concatenate([partner, block], 2), jnp.concatenate([block, partner], 2)
    )
    partner = partner_2(block, "gy", 0)
    odd_y = lax.axis_index("gy") % 2 == 1
    block = jnp.where(
        odd_y, jnp.concatenate([partner, block], 3), jnp.concatenate([block, partner], 3)
    )
    group_rhs = block[:3]
    group_scales = block[3]
    group_free = block[4:]

    def apply(field):
        padded = pad_group(jnp.concatenate([field, group_scales[None]], 0))
        return stencil(padded[:3], padded[3], 4.0)

    settled = smooth(jnp.zeros_like(group_rhs), group_rhs, group_free, apply, COARSE)
    start_z = (lax.axis_index("gz") * depth).astype(jnp.int32)
    start_x = (lax.axis_index("gx") % 2 * ex).astype(jnp.int32)
    start_y = (lax.axis_index("gy") % 2 * ey).astype(jnp.int32)
    return lax.dynamic_slice(settled, (jnp.int32(0), start_z, start_x, start_y), (3, depth, ex, ey))


def on_device(displacement, load, density_code, fixed_mask):
    free0 = 1.0 - fixed_mask.astype(jnp.float32)
    level = density_code.astype(jnp.float32) / (LEVELS - 1)
    scales0 = EMIN + (1.0 - EMIN) * level * level * level
    apply0 = level_apply(scales0, 1.0)
    state = smooth(free0 * displacement, load, free0, apply0, NU)
    rhs1 = coarsen(residual(state, load, free0, apply0), jnp.sum)
    scales1 = coarsen(scales0, jnp.mean)
    free1 = coarsen(free0, jnp.min)
    apply1 = level_apply(scales1, 2.0)
    corr1 = smooth(jnp.zeros_like(rhs1), rhs1, free1, apply1, NU)
    rhs2 = coarsen(residual(corr1, rhs1, free1, apply1), jnp.sum)
    scales2 = coarsen(scales1, jnp.mean)
    free2 = coarsen(free1, jnp.min)
    corr2 = coarse_grouped(rhs2, scales2, free2)
    corr1 = smooth(corr1 + free1 * refine(corr2), rhs1, free1, apply1, NU)
    return smooth(state + free0 * refine(corr1), load, free0, apply0, NU)


def solution(mesh):
    return jax.shard_map(
        on_device,
        mesh=mesh,
        in_specs=(
            P(None, "gz", "gx", "gy"),
            P(None, "gz", "gx", "gy"),
            P("gz", "gx", "gy"),
            P(None, "gz", "gx", "gy"),
        ),
        out_specs=P(None, "gz", "gx", "gy"),
        check_vma=False,
    )
```

profile of v0, /device:TPU:398, one launch (start us, length us, event | category | flops | bytes accessed | tf_op | source)
XLA Modules:
  0.0 562.7 jit_solution(11012801677518508346)
XLA Ops:
  0.9 9.8 %reshape.85 = f32[4,2,16,2,64,2]{5,4,3,2,1,0:T(8,128)} reshape(f32[8,32,128]{2,1,0:T(8,128)S(1)} %get-tuple-element.142) | data formatting | bytes 262144 | tf_op jit(solution)/shard_map/reshape | solution.py:162
  10.7 4.1 reduce_sum.39
  15.4 4.1 collective-permute-start.19
  21.7 4.6 collective-permute-done.18
  32.9 3.9 collective-permute-start
  36.8 26.5 %reshape.83 = f32[3,4,2,16,2,64,2]{6,5,4,3,2,1,0:T(8,128)} reshape(f32[3,8,32,128]{3,2,1,0:T(8,128)S(1)} %get-tuple-element.53) | data formatting | bytes 786432 | tf_op jit(solution)/shard_map/reshape | solution.py:162
  63.4 9.4 %reduce_min.20 = f32[3,4,16,64]{3,2,1,0:T(8,128)S(1)} reduce(f32[3,4,2,16,2,64,2]{6,5,4,3,2,1,0:T(8,128)} %reshape.83, f32[]{:T(128)} %constant.54.clone.1), dimensions={2,4,6}, to_apply=%region_0.0 | reduce | flops 86016 | bytes 442372 | tf_op jit(solution)/shard_map/reduce_min | solution.py:163
  73.7 5.5 collective-permute-start.3
  82.8 4.5 collective-permute-start.23
  94.4 4.1 collective-permute-done.4
  114.5 4.4 collective-permute-done.6
  124.6 4.7 collective-permute-done.8
  135.3 4.4 collective-permute-done.10
  151.7 3.9 collective-permute-start.12
  174.2 4.4 collective-permute-done.16
  188.3 26.5 %reshape.84 = f32[3,4,2,16,2,64,2]{6,5,4,3,2,1,0:T(8,128)} reshape(f32[3,8,32,128]{3,2,1,0:T(8,128)S(1)} %fusion.66) | data formatting | bytes 786432 | tf_op jit(solution)/shard_map/reshape | solution.py:162
  214.9 9.4 %reduce_sum.38 = f32[3,4,16,64]{3,2,1,0:T(8,128)S(1)} reduce(f32[3,4,2,16,2,64,2]{6,5,4,3,2,1,0:T(8,128)} %reshape.84, f32[]{:T(128)} %constant.25.clone.1), dimensions={2,4,6}, to_apply=%region_1.0 | reduce | flops 86016 | bytes 442372 | tf_op jit(solution)/shard_map/reduce_sum | solution.py:163
  226.4 3.9 collective-permute-start.24
  237.9 6.2 %collective-permute-done.26 = f32[4,4,18,1]{3,1,2,0:T(4,128)S(1)} collective-permute-done((f32[4,4,18,1]{3,1,2,0:T(4,128)S(1)}, f32[4,4,18,1]{3,1,2,0:T(4,128)S(1)}, u32[]{:S(2)}, u32[]{:S(2)}) %collective-permute-start.26) | collective-permute-done | bytes 1184 | tf_op jit(solution)/shard_map/ppermute | solution.py:23
  245.7 4.5 collective-permute-start.29
  256.3 3.9 collective-permute-start.30
  268.8 5.2 collective-permute-done.32
  288.9 5.1 collective-permute-start.35
  302.6 5.1 all_gather.3
  310.4 4.0 collective-permute-done.36
  320.2 4.5 collective-permute-start.38
  330.2 5.4 collective-permute-start.40
  335.6 4.1 collective-permute-done.41
  344.9 4.2 collective-permute-start.42
  352.8 4.2 collective-permute-start.45
  370.8 4.8 collective-permute-start.46
  381.0 5.1 collective-permute-start.48
  394.9 4.8 collective-permute-start.50
  402.7 4.2 collective-permute-start.53
  411.3 5.1 collective-permute-done.52
  421.6 4.3 collective-permute-start.54
  433.1 6.2 %collective-permute-done.56 = f32[4,4,18,1]{3,1,2,0:T(4,128)S(1)} collective-permute-done((f32[4,4,18,1]{3,1,2,0:T(4,128)S(1)}, f32[4,4,18,1]{3,1,2,0:T(4,128)S(1)}, u32[]{:S(2)}, u32[]{:S(2)}) %collective-permute-start.56) | collective-permute-done | bytes 1184 | tf_op jit(solution)/shard_map/ppermute | solution.py:23
  440.9 4.5 collective-permute-start.59
  451.5 3.9 collective-permute-start.60
  463.0 6.2 %collective-permute-done.62 = f32[4,4,18,1]{3,1,2,0:T(4,128)S(1)} collective-permute-done((f32[4,4,18,1]{3,1,2,0:T(4,128)S(1)}, f32[4,4,18,1]{3,1,2,0:T(4,128)S(1)}, u32[]{:S(2)}, u32[]{:S(2)}) %collective-permute-start.62) | collective-permute-done | bytes 1184 | tf_op jit(solution)/shard_map/ppermute | solution.py:23
  470.8 4.5 collective-permute-start.65
  483.1 3.9 collective-permute-start.66
  495.6 4.7 collective-permute-done.68
  501.3 4.3 collective-permute-start.71
  508.4 4.4 collective-permute-done.70
  524.8 3.9 collective-permute-start.72
  537.3 4.8 collective-permute-done.74
  547.3 4.4 collective-permute-done.76
  (410 shorter events, 281.2 us)
Async XLA Ops:
  19.6 6.8 %collective-permute-start.18 = (f32[4,4,1,64]{3,2,1,0:T(1,128)S(1)}, f32[4,4,1,64]{3,2,1,0:T(1,128)S(1)}, u32[]{:S(2)}, u32[]{:S(2)}) collective-permute-start(f32[4,4,1,64]{3,2,1,0:T(1,128)S(1)} %get-tuple-element.148), channel_id=1, source_target_pairs={{0,32},{32,64},{64,96},{96,128},{128,160},{160,192},{192,224},{224... | collective-permute-start | bytes 12296 | tf_op jit(solution)/shard_map/ppermute | solution.py:23
  26.5 46.3 %collective-permute-start.21 = (f32[4,4,18,1]{3,1,2,0:T(4,128)S(1)}, f32[4,4,18,1]{3,1,2,0:T(4,128)S(1)}, u32[]{:S(2)}, u32[]{:S(2)}) collective-permute-start(f32[4,4,18,1]{3,1,2,0:T(4,128)S(1)} %get-tuple-element.127), channel_id=1, source_target_pairs={{2,0},{4,2},{6,4},{8,6},{10,8},{12,10},{14,12},{16,14},{18,16},{20... | collective-permute-start | bytes 3464 | tf_op jit(solution)/shard_map/ppermute | solution.py:26
  29.0 43.8 %collective-permute-start.20 = (f32[4,4,18,1]{3,1,2,0:T(4,128)S(1)}, f32[4,4,18,1]{3,1,2,0:T(4,128)S(1)}, u32[]{:S(2)}, u32[]{:S(2)}) collective-permute-start(f32[4,4,18,1]{3,1,2,0:T(4,128)S(1)} %get-tuple-element.126), channel_id=1, source_target_pairs={{0,2},{2,4},{4,6},{6,8},{8,10},{10,12},{12,14},{14,16},{16,18},{18... | collective-permute-start | bytes 3464 | tf_op jit(solution)/shard_map/ppermute | solution.py:23
  31.0 42.1 %collective-permute-start.1 = (f32[4,8,1,128]{3,1,2,0:T(8,128)S(1)}, f32[4,8,1,128]{3,1,2,0:T(8,128)S(1)}, u32[]{:S(2)}, u32[]{:S(2)}) collective-permute-start(f32[4,8,1,128]{3,1,2,0:T(8,128)S(1)} %bitcast.321), channel_id=1, source_target_pairs={{32,0},{64,32},{96,64},{128,96},{160,128},{192,160},{224,192},{256... | collective-permute-start | bytes 49160 | tf_op jit(solution)/shard_map/ppermute | solution.py:26
  32.9 40.1 %collective-permute-start = (f32[4,8,1,128]{3,1,2,0:T(8,128)S(1)}, f32[4,8,1,128]{3,1,2,0:T(8,128)S(1)}, u32[]{:S(2)}, u32[]{:S(2)}) collective-permute-start(f32[4,8,1,128]{3,1,2,0:T(8,128)S(1)} %bitcast.320), channel_id=1, source_target_pairs={{0,32},{32,64},{64,96},{96,128},{128,160},{160,192},{192,224},{224... | collective-permute-start | bytes 49160 | tf_op jit(solution)/shard_map/ppermute | solution.py:23
  73.7 13.7 %collective-permute-start.3 = (f32[4,8,34,1]{2,1,3,0:T(8,128)S(1)}, f32[4,8,34,1]{2,1,3,0:T(8,128)S(1)}, u32[]{:S(2)}, u32[]{:S(2)}) collective-permute-start(f32[4,8,34,1]{2,1,3,0:T(8,128)S(1)} %copy.591), channel_id=1, source_target_pairs={{2,0},{4,2},{6,4},{8,6},{10,8},{12,10},{14,12},{16,14},{18,16},{20... | collective-permute-start | bytes 13064 | tf_op jit(solution)/shard_map/ppermute | solution.py:26
  79.5 8.2 %collective-permute-start.2 = (f32[4,8,34,1]{2,1,3,0:T(8,128)S(1)}, f32[4,8,34,1]{2,1,3,0:T(8,128)S(1)}, u32[]{:S(2)}, u32[]{:S(2)}) collective-permute-start(f32[4,8,34,1]{2,1,3,0:T(8,128)S(1)} %copy.590), channel_id=1, source_target_pairs={{0,2},{2,4},{4,6},{6,8},{8,10},{10,12},{12,14},{14,16},{16,18},{18... | collective-permute-start | bytes 13064 | tf_op jit(solution)/shard_map/ppermute | solution.py:23
  81.5 11.4 %collective-permute-start.22 = (f32[4,1,18,66]{3,2,1,0:T(8,128)S(1)}, f32[4,1,18,66]{3,2,1,0:T(8,128)S(1)}, u32[]{:S(2)}, u32[]{:S(2)}) collective-permute-start(f32[4,1,18,66]{3,2,1,0:T(8,128)S(1)} %copy.689), channel_id=1, source_target_pairs={{0,1},{2,3},{4,5},{6,7},{8,9},{10,11},{12,13},{14,15},{16,17},{18,... | collective-permute-start | bytes 57032 | tf_op jit(solution)/shard_map/ppermute | solution.py:23
  82.8 31.7 %collective-permute-start.23 = (f32[4,1,18,66]{3,2,1,0:T(8,128)S(1)}, f32[4,1,18,66]{3,2,1,0:T(8,128)S(1)}, u32[]{:S(2)}, u32[]{:S(2)}) collective-permute-start(f32[4,1,18,66]{3,2,1,0:T(8,128)S(1)} %copy.690), channel_id=1, source_target_pairs={{1,0},{3,2},{5,4},{7,6},{9,8},{11,10},{13,12},{15,14},{17,16},{19,... | collective-permute-start | bytes 57032 | tf_op jit(solution)/shard_map/ppermute | solution.py:26
  91.4 7.2 %collective-permute-start.4 = (f32[4,1,34,130]{3,2,1,0:T(8,128)S(1)}, f32[4,1,34,130]{3,2,1,0:T(8,128)S(1)}, u32[]{:S(2)}, u32[]{:S(2)}) collective-permute-start(f32[4,1,34,130]{3,2,1,0:T(8,128)S(1)} %get-tuple-element.37), channel_id=1, source_target_pairs={{0,1},{2,3},{4,5},{6,7},{8,9},{10,11},{12,13},{14,15},{16,17},{18,... | collective-permute-start | bytes 212168 | tf_op jit(solution)/shard_map/ppermute | solution.py:23
  112.1 6.8 %collective-permute-start.6 = (f32[4,8,1,128]{3,1,2,0:T(8,128)S(1)}, f32[4,8,1,128]{3,1,2,0:T(8,128)S(1)}, u32[]{:S(2)}, u32[]{:S(2)}) collective-permute-start(f32[4,8,1,128]{3,1,2,0:T(8,128)S(1)} %bitcast.322), channel_id=1, source_target_pairs={{0,32},{32,64},{64,96},{96,128},{128,160},{160,192},{192,224},{224... | collective-permute-start | bytes 49160 | tf_op jit(solution)/shard_map/ppermute | solution.py:23
  121.8 7.6 %collective-permute-start.8 = (f32[4,8,34,1]{2,1,3,0:T(8,128)S(1)}, f32[4,8,34,1]{2,1,3,0:T(8,128)S(1)}, u32[]{:S(2)}, u32[]{:S(2)}) collective-permute-start(f32[4,8,34,1]{2,1,3,0:T(8,128)S(1)} %copy.598), channel_id=1, source_target_pairs={{0,2},{2,4},{4,6},{6,8},{8,10},{10,12},{12,14},{14,16},{16,18},{18... | collective-permute-start | bytes 13064 | tf_op jit(solution)/shard_map/ppermute | solution.py:23
  132.5 7.2 %collective-permute-start.10 = (f32[4,1,34,130]{3,2,1,0:T(8,128)S(1)}, f32[4,1,34,130]{3,2,1,0:T(8,128)S(1)}, u32[]{:S(2)}, u32[]{:S(2)}) collective-permute-start(f32[4,1,34,130]{3,2,1,0:T(8,128)S(1)} %get-tuple-element.35), channel_id=1, source_target_pairs={{0,1},{2,3},{4,5},{6,7},{8,9},{10,11},{12,13},{14,15},{16,17},{18,... | collective-permute-start | bytes 212168 | tf_op jit(solution)/shard_map/ppermute | solution.py:23
  149.8 7.1 %collective-permute-start.13 = (f32[4,8,1,128]{3,1,2,0:T(8,128)S(1)}, f32[4,8,1,128]{3,1,2,0:T(8,128)S(1)}, u32[]{:S(2)}, u32[]{:S(2)}) collective-permute-start(f32[4,8,1,128]{3,1,2,0:T(8,128)S(1)} %bitcast.328), channel_id=1, source_target_pairs={{32,0},{64,32},{96,64},{128,96},{160,128},{192,160},{224,192},{256... | collective-permute-start | bytes 49160 | tf_op jit(solution)/shard_map/ppermute | solution.py:26
  151.7 6.8 %collective-permute-start.12 = (f32[4,8,1,128]{3,1,2,0:T(8,128)S(1)}, f32[4,8,1,128]{3,1,2,0:T(8,128)S(1)}, u32[]{:S(2)}, u32[]{:S(2)}) collective-permute-start(f32[4,8,1,128]{3,1,2,0:T(8,128)S(1)} %bitcast.325), channel_id=1, source_target_pairs={{0,32},{32,64},{64,96},{96,128},{128,160},{160,192},{192,224},{224... | collective-permute-start | bytes 49160 | tf_op jit(solution)/shard_map/ppermute | solution.py:23
  161.4 7.5 %collective-permute-start.14 = (f32[4,8,34,1]{2,1,3,0:T(8,128)S(1)}, f32[4,8,34,1]{2,1,3,0:T(8,128)S(1)}, u32[]{:S(2)}, u32[]{:S(2)}) collective-permute-start(f32[4,8,34,1]{2,1,3,0:T(8,128)S(1)} %copy.606), channel_id=1, source_target_pairs={{0,2},{2,4},{4,6},{6,8},{8,10},{10,12},{12,14},{14,16},{16,18},{18... | collective-permute-start | bytes 13064 | tf_op jit(solution)/shard_map/ppermute | solution.py:23
  171.4 7.2 %collective-permute-start.16 = (f32[4,1,34,130]{3,2,1,0:T(8,128)S(1)}, f32[4,1,34,130]{3,2,1,0:T(8,128)S(1)}, u32[]{:S(2)}, u32[]{:S(2)}) collective-permute-start(f32[4,1,34,130]{3,2,1,0:T(8,128)S(1)} %get-tuple-element.33), channel_id=1, source_target_pairs={{0,1},{2,3},{4,5},{6,7},{8,9},{10,11},{12,13},{14,15},{16,17},{18,... | collective-permute-start | bytes 212168 | tf_op jit(solution)/shard_map/ppermute | solution.py:23
  226.4 6.8 %collective-permute-start.24 = (f32[4,4,1,64]{3,2,1,0:T(1,128)S(1)}, f32[4,4,1,64]{3,2,1,0:T(1,128)S(1)}, u32[]{:S(2)}, u32[]{:S(2)}) collective-permute-start(f32[4,4,1,64]{3,2,1,0:T(1,128)S(1)} %get-tuple-element.140), channel_id=1, source_target_pairs={{0,32},{32,64},{64,96},{96,128},{128,160},{160,192},{192,224},{224... | collective-permute-start | bytes 12296 | tf_op jit(solution)/shard_map/ppermute | solution.py:23
  235.2 8.9 %collective-permute-start.26 = (f32[4,4,18,1]{3,1,2,0:T(4,128)S(1)}, f32[4,4,18,1]{3,1,2,0:T(4,128)S(1)}, u32[]{:S(2)}, u32[]{:S(2)}) collective-permute-start(f32[4,4,18,1]{3,1,2,0:T(4,128)S(1)} %get-tuple-element.122), channel_id=1, source_target_pairs={{0,2},{2,4},{4,6},{6,8},{8,10},{10,12},{12,14},{14,16},{16,18},{18... | collective-permute-start | bytes 3464 | tf_op jit(solution)/shard_map/ppermute | solution.py:23
  256.3 6.8 %collective-permute-start.30 = (f32[4,4,1,64]{3,2,1,0:T(1,128)S(1)}, f32[4,4,1,64]{3,2,1,0:T(1,128)S(1)}, u32[]{:S(2)}, u32[]{:S(2)}) collective-permute-start(f32[4,4,1,64]{3,2,1,0:T(1,128)S(1)} %get-tuple-element.138), channel_id=1, source_target_pairs={{0,32},{32,64},{64,96},{96,128},{128,160},{160,192},{192,224},{224... | collective-permute-start | bytes 12296 | tf_op jit(solution)/shard_map/ppermute | solution.py:23
  265.1 8.9 %collective-permute-start.32 = (f32[4,4,18,1]{3,1,2,0:T(4,128)S(1)}, f32[4,4,18,1]{3,1,2,0:T(4,128)S(1)}, u32[]{:S(2)}, u32[]{:S(2)}) collective-permute-start(f32[4,4,18,1]{3,1,2,0:T(4,128)S(1)} %get-tuple-element.118), channel_id=1, source_target_pairs={{0,2},{2,4},{4,6},{6,8},{8,10},{10,12},{12,14},{14,16},{16,18},{18... | collective-permute-start | bytes 3464 | tf_op jit(solution)/shard_map/ppermute | solution.py:23
  275.5 18.5 %collective-permute-start.34 = (f32[4,1,18,66]{3,2,1,0:T(8,128)}, f32[4,1,18,66]{3,2,1,0:T(8,128)}, u32[]{:S(2)}, u32[]{:S(2)}) collective-permute-start(f32[4,1,18,66]{3,2,1,0:T(8,128)} %copy.693), channel_id=1, source_target_pairs={{0,1},{2,3},{4,5},{6,7},{8,9},{10,11},{12,13},{14,15},{16,17},{18,... | collective-permute-start | bytes 57032 | tf_op jit(solution)/shard_map/ppermute | solution.py:23
  288.9 6.9 %collective-permute-start.35 = (f32[4,1,18,66]{3,2,1,0:T(8,128)S(1)}, f32[4,1,18,66]{3,2,1,0:T(8,128)S(1)}, u32[]{:S(2)}, u32[]{:S(2)}) collective-permute-start(f32[4,1,18,66]{3,2,1,0:T(8,128)S(1)} %copy.694), channel_id=1, source_target_pairs={{1,0},{3,2},{5,4},{7,6},{9,8},{11,10},{13,12},{15,14},{17,16},{19,... | collective-permute-start | bytes 57032 | tf_op jit(solution)/shard_map/ppermute | solution.py:26
  318.0 6.8 %collective-permute-start.39 = (f32[4,4,1,64]{3,2,1,0:T(1,128)S(1)}, f32[4,4,1,64]{3,2,1,0:T(1,128)S(1)}, u32[]{:S(2)}, u32[]{:S(2)}) collective-permute-start(f32[4,4,1,64]{3,2,1,0:T(1,128)S(1)} %get-tuple-element.145), channel_id=1, source_target_pairs={{64,0},{96,32},{128,64},{160,96},{192,128},{224,160},{256,192},{28... | collective-permute-start | bytes 12296 | tf_op jit(solution)/shard_map/ppermute | solution.py:34
  320.2 7.7 %collective-permute-start.38 = (f32[4,4,1,64]{3,2,1,0:T(1,128)S(1)}, f32[4,4,1,64]{3,2,1,0:T(1,128)S(1)}, u32[]{:S(2)}, u32[]{:S(2)}) collective-permute-start(f32[4,4,1,64]{3,2,1,0:T(1,128)S(1)} %get-tuple-element.144), channel_id=1, source_target_pairs={{0,64},{32,96},{64,128},{96,160},{128,192},{160,224},{192,256},{22... | collective-permute-start | bytes 12296 | tf_op jit(solution)/shard_map/ppermute | solution.py:34
  328.1 11.7 %collective-permute-start.41 = (f32[4,4,18,1]{3,1,2,0:T(4,128)S(1)}, f32[4,4,18,1]{3,1,2,0:T(4,128)S(1)}, u32[]{:S(2)}, u32[]{:S(2)}) collective-permute-start(f32[4,4,18,1]{3,1,2,0:T(4,128)S(1)} %get-tuple-element.115), channel_id=1, source_target_pairs={{4,0},{6,2},{8,4},{10,6},{12,8},{14,10},{16,12},{18,14},{20,16},{2... | collective-permute-start | bytes 3464 | tf_op jit(solution)/shard_map/ppermute | solution.py:34
  330.2 9.5 %collective-permute-start.40 = (f32[4,4,18,1]{3,1,2,0:T(4,128)S(1)}, f32[4,4,18,1]{3,1,2,0:T(4,128)S(1)}, u32[]{:S(2)}, u32[]{:S(2)}) collective-permute-start(f32[4,4,18,1]{3,1,2,0:T(4,128)S(1)} %get-tuple-element.114), channel_id=1, source_target_pairs={{0,4},{2,6},{4,8},{6,10},{8,12},{10,14},{12,16},{14,18},{16,20},{1... | collective-permute-start | bytes 3464 | tf_op jit(solution)/shard_map/ppermute | solution.py:34
  342.3 6.8 %collective-permute-start.43 = (f32[4,4,1,64]{3,2,1,0:T(1,128)S(1)}, f32[4,4,1,64]{3,2,1,0:T(1,128)S(1)}, u32[]{:S(2)}, u32[]{:S(2)}) collective-permute-start(f32[4,4,1,64]{3,2,1,0:T(1,128)S(1)} %get-tuple-element.137), channel_id=1, source_target_pairs={{64,0},{96,32},{128,64},{160,96},{192,128},{224,160},{256,192},{28... | collective-permute-start | bytes 12296 | tf_op jit(solution)/shard_map/ppermute | solution.py:34
  344.9 7.7 %collective-permute-start.42 = (f32[4,4,1,64]{3,2,1,0:T(1,128)S(1)}, f32[4,4,1,64]{3,2,1,0:T(1,128)S(1)}, u32[]{:S(2)}, u32[]{:S(2)}) collective-permute-start(f32[4,4,1,64]{3,2,1,0:T(1,128)S(1)} %get-tuple-element.136), channel_id=1, source_target_pairs={{0,64},{32,96},{64,128},{96,160},{128,192},{160,224},{192,256},{22... | collective-permute-start | bytes 12296 | tf_op jit(solution)/shard_map/ppermute | solution.py:34
  352.8 9.8 %collective-permute-start.45 = (f32[4,4,18,1]{3,1,2,0:T(4,128)S(1)}, f32[4,4,18,1]{3,1,2,0:T(4,128)S(1)}, u32[]{:S(2)}, u32[]{:S(2)}) collective-permute-start(f32[4,4,18,1]{3,1,2,0:T(4,128)S(1)} %get-tuple-element.113), channel_id=1, source_target_pairs={{4,0},{6,2},{8,4},{10,6},{12,8},{14,10},{16,12},{18,14},{20,16},{2... | collective-permute-start | bytes 3464 | tf_op jit(solution)/shard_map/ppermute | solution.py:34
  356.9 9.4 %collective-permute-start.44 = (f32[4,4,18,1]{3,1,2,0:T(4,128)S(1)}, f32[4,4,18,1]{3,1,2,0:T(4,128)S(1)}, u32[]{:S(2)}, u32[]{:S(2)}) collective-permute-start(f32[4,4,18,1]{3,1,2,0:T(4,128)S(1)} %get-tuple-element.112), channel_id=1, source_target_pairs={{0,4},{2,6},{4,8},{6,10},{8,12},{10,14},{12,16},{14,18},{16,20},{1... | collective-permute-start | bytes 3464 | tf_op jit(solution)/shard_map/ppermute | solution.py:34
  368.9 6.8 %collective-permute-start.47 = (f32[4,4,1,64]{3,2,1,0:T(1,128)S(1)}, f32[4,4,1,64]{3,2,1,0:T(1,128)S(1)}, u32[]{:S(2)}, u32[]{:S(2)}) collective-permute-start(f32[4,4,1,64]{3,2,1,0:T(1,128)S(1)} %get-tuple-element.135), channel_id=1, source_target_pairs={{64,0},{96,32},{128,64},{160,96},{192,128},{224,160},{256,192},{28... | collective-permute-start | bytes 12296 | tf_op jit(solution)/shard_map/ppermute | solution.py:34
  370.8 7.7 %collective-permute-start.46 = (f32[4,4,1,64]{3,2,1,0:T(1,128)S(1)}, f32[4,4,1,64]{3,2,1,0:T(1,128)S(1)}, u32[]{:S(2)}, u32[]{:S(2)}) collective-permute-start(f32[4,4,1,64]{3,2,1,0:T(1,128)S(1)} %get-tuple-element.134), channel_id=1, source_target_pairs={{0,64},{32,96},{64,128},{96,160},{128,192},{160,224},{192,256},{22... | collective-permute-start | bytes 12296 | tf_op jit(solution)/shard_map/ppermute | solution.py:34
  378.7 8.5 %collective-permute-start.49 = (f32[4,4,18,1]{3,1,2,0:T(4,128)S(1)}, f32[4,4,18,1]{3,1,2,0:T(4,128)S(1)}, u32[]{:S(2)}, u32[]{:S(2)}) collective-permute-start(f32[4,4,18,1]{3,1,2,0:T(4,128)S(1)} %get-tuple-element.111), channel_id=1, source_target_pairs={{4,0},{6,2},{8,4},{10,6},{12,8},{14,10},{16,12},{18,14},{20,16},{2... | collective-permute-start | bytes 3464 | tf_op jit(solution)/shard_map/ppermute | solution.py:34
  381.0 9.4 %collective-permute-start.48 = (f32[4,4,18,1]{3,1,2,0:T(4,128)S(1)}, f32[4,4,18,1]{3,1,2,0:T(4,128)S(1)}, u32[]{:S(2)}, u32[]{:S(2)}) collective-permute-start(f32[4,4,18,1]{3,1,2,0:T(4,128)S(1)} %get-tuple-element.110), channel_id=1, source_target_pairs={{0,4},{2,6},{4,8},{6,10},{8,12},{10,14},{12,16},{14,18},{16,20},{1... | collective-permute-start | bytes 3464 | tf_op jit(solution)/shard_map/ppermute | solution.py:34
  393.0 6.8 %collective-permute-start.51 = (f32[4,4,1,64]{3,2,1,0:T(1,128)S(1)}, f32[4,4,1,64]{3,2,1,0:T(1,128)S(1)}, u32[]{:S(2)}, u32[]{:S(2)}) collective-permute-start(f32[4,4,1,64]{3,2,1,0:T(1,128)S(1)} %get-tuple-element.133), channel_id=1, source_target_pairs={{64,0},{96,32},{128,64},{160,96},{192,128},{224,160},{256,192},{28... | collective-permute-start | bytes 12296 | tf_op jit(solution)/shard_map/ppermute | solution.py:34
  394.9 7.7 %collective-permute-start.50 = (f32[4,4,1,64]{3,2,1,0:T(1,128)S(1)}, f32[4,4,1,64]{3,2,1,0:T(1,128)S(1)}, u32[]{:S(2)}, u32[]{:S(2)}) collective-permute-start(f32[4,4,1,64]{3,2,1,0:T(1,128)S(1)} %get-tuple-element.132), channel_id=1, source_target_pairs={{0,64},{32,96},{64,128},{96,160},{128,192},{160,224},{192,256},{22... | collective-permute-start | bytes 12296 | tf_op jit(solution)/shard_map/ppermute | solution.py:34
  402.7 8.5 %collective-permute-start.53 = (f32[4,4,18,1]{3,1,2,0:T(4,128)S(1)}, f32[4,4,18,1]{3,1,2,0:T(4,128)S(1)}, u32[]{:S(2)}, u32[]{:S(2)}) collective-permute-start(f32[4,4,18,1]{3,1,2,0:T(4,128)S(1)} %get-tuple-element.109), channel_id=1, source_target_pairs={{4,0},{6,2},{8,4},{10,6},{12,8},{14,10},{16,12},{18,14},{20,16},{2... | collective-permute-start | bytes 3464 | tf_op jit(solution)/shard_map/ppermute | solution.py:34
  406.9 9.4 %collective-permute-start.52 = (f32[4,4,18,1]{3,1,2,0:T(4,128)S(1)}, f32[4,4,18,1]{3,1,2,0:T(4,128)S(1)}, u32[]{:S(2)}, u32[]{:S(2)}) collective-permute-start(f32[4,4,18,1]{3,1,2,0:T(4,128)S(1)} %get-tuple-element.108), channel_id=1, source_target_pairs={{0,4},{2,6},{4,8},{6,10},{8,12},{10,14},{12,16},{14,18},{16,20},{1... | collective-permute-start | bytes 3464 | tf_op jit(solution)/shard_map/ppermute | solution.py:34
  430.5 8.9 %collective-permute-start.56 = (f32[4,4,18,1]{3,1,2,0:T(4,128)S(1)}, f32[4,4,18,1]{3,1,2,0:T(4,128)S(1)}, u32[]{:S(2)}, u32[]{:S(2)}) collective-permute-start(f32[4,4,18,1]{3,1,2,0:T(4,128)S(1)} %get-tuple-element.106), channel_id=1, source_target_pairs={{0,2},{2,4},{4,6},{6,8},{8,10},{10,12},{12,14},{14,16},{16,18},{18... | collective-permute-start | bytes 3464 | tf_op jit(solution)/shard_map/ppermute | solution.py:23
  460.3 8.9 %collective-permute-start.62 = (f32[4,4,18,1]{3,1,2,0:T(4,128)S(1)}, f32[4,4,18,1]{3,1,2,0:T(4,128)S(1)}, u32[]{:S(2)}, u32[]{:S(2)}) collective-permute-start(f32[4,4,18,1]{3,1,2,0:T(4,128)S(1)} %get-tuple-element.102), channel_id=1, source_target_pairs={{0,2},{2,4},{4,6},{6,8},{8,10},{10,12},{12,14},{14,16},{16,18},{18... | collective-permute-start | bytes 3464 | tf_op jit(solution)/shard_map/ppermute | solution.py:23
  483.1 6.8 %collective-permute-start.66 = (f32[4,8,1,128]{3,1,2,0:T(8,128)S(1)}, f32[4,8,1,128]{3,1,2,0:T(8,128)S(1)}, u32[]{:S(2)}, u32[]{:S(2)}) collective-permute-start(f32[4,8,1,128]{3,1,2,0:T(8,128)S(1)} %bitcast.326), channel_id=1, source_target_pairs={{0,32},{32,64},{64,96},{96,128},{128,160},{160,192},{192,224},{224... | collective-permute-start | bytes 49160 | tf_op jit(solution)/shard_map/ppermute | solution.py:23
  492.8 7.5 %collective-permute-start.68 = (f32[4,8,34,1]{2,1,3,0:T(8,128)S(1)}, f32[4,8,34,1]{2,1,3,0:T(8,128)S(1)}, u32[]{:S(2)}, u32[]{:S(2)}) collective-permute-start(f32[4,8,34,1]{2,1,3,0:T(8,128)S(1)} %copy.671), channel_id=1, source_target_pairs={{0,2},{2,4},{4,6},{6,8},{8,10},{10,12},{12,14},{14,16},{16,18},{18... | collective-permute-start | bytes 13064 | tf_op jit(solution)/shard_map/ppermute | solution.py:23
  501.3 7.1 %collective-permute-start.71 = (f32[4,1,34,130]{3,2,1,0:T(8,128)S(1)}, f32[4,1,34,130]{3,2,1,0:T(8,128)S(1)}, u32[]{:S(2)}, u32[]{:S(2)}) collective-permute-start(f32[4,1,34,130]{3,2,1,0:T(8,128)S(1)} %get-tuple-element.32), channel_id=1, source_target_pairs={{1,0},{3,2},{5,4},{7,6},{9,8},{11,10},{13,12},{15,14},{17,16},{19,... | collective-permute-start | bytes 212168 | tf_op jit(solution)/shard_map/ppermute | solution.py:26
  505.6 7.2 %collective-permute-start.70 = (f32[4,1,34,130]{3,2,1,0:T(8,128)S(1)}, f32[4,1,34,130]{3,2,1,0:T(8,128)S(1)}, u32[]{:S(2)}, u32[]{:S(2)}) collective-permute-start(f32[4,1,34,130]{3,2,1,0:T(8,128)S(1)} %get-tuple-element.31), channel_id=1, source_target_pairs={{0,1},{2,3},{4,5},{6,7},{8,9},{10,11},{12,13},{14,15},{16,17},{18,... | collective-permute-start | bytes 212168 | tf_op jit(solution)/shard_map/ppermute | solution.py:23
  524.8 6.8 %collective-permute-start.72 = (f32[4,8,1,128]{3,1,2,0:T(8,128)S(1)}, f32[4,8,1,128]{3,1,2,0:T(8,128)S(1)}, u32[]{:S(2)}, u32[]{:S(2)}) collective-permute-start(f32[4,8,1,128]{3,1,2,0:T(8,128)S(1)} %bitcast.324), channel_id=1, source_target_pairs={{0,32},{32,64},{64,96},{96,128},{128,160},{160,192},{192,224},{224... | collective-permute-start | bytes 49160 | tf_op jit(solution)/shard_map/ppermute | solution.py:23
  534.5 7.6 %collective-permute-start.74 = (f32[4,8,34,1]{2,1,3,0:T(8,128)S(1)}, f32[4,8,34,1]{2,1,3,0:T(8,128)S(1)}, u32[]{:S(2)}, u32[]{:S(2)}) collective-permute-start(f32[4,8,34,1]{2,1,3,0:T(8,128)S(1)} %copy.679), channel_id=1, source_target_pairs={{0,2},{2,4},{4,6},{6,8},{8,10},{10,12},{12,14},{14,16},{16,18},{18... | collective-permute-start | bytes 13064 | tf_op jit(solution)/shard_map/ppermute | solution.py:23
  544.5 7.2 %collective-permute-start.76 = (f32[4,1,34,130]{3,2,1,0:T(8,128)S(1)}, f32[4,1,34,130]{3,2,1,0:T(8,128)S(1)}, u32[]{:S(2)}, u32[]{:S(2)}) collective-permute-start(f32[4,1,34,130]{3,2,1,0:T(8,128)S(1)} %get-tuple-element.29), channel_id=1, source_target_pairs={{0,1},{2,3},{4,5},{6,7},{8,9},{10,11},{12,13},{14,15},{16,17},{18,... | collective-permute-start | bytes 212168 | tf_op jit(solution)/shard_map/ppermute | solution.py:23
  (50 other events, 417.8 us)
where the time goes:
time: 570 us; the launch traced here: 563 us
  starting transfers between devices  216 us (38%)
  waiting for transfers between devices  139 us (24%)
  other arithmetic  103 us (18%)
  local copies, waits for them, and re-layouts  96.2 us (17%)
    ppermute x30, waiting for transfers between devices, padded_2(): lax.ppermute(lax.slice_in_dim(block, block.shape[dim] - width, None, axis...  90.5 us
    ppermute x30, starting transfers between devices, padded_2(): lax.ppermute(lax.slice_in_dim(block, 0, width, axis=dim), axis, backward)  81.2 us
    ppermute x30, starting transfers between devices, padded_2(): lax.ppermute(lax.slice_in_dim(block, block.shape[dim] - width, None, axis...  73.5 us
    reshape x3, local copies, waits for them, and re-layouts, coarsen(): shaped = array.reshape(lead + (ex // 2, 2, ey // 2, 2, ez // 2, 2))  62.8 us
    another operation x39, other arithmetic, stencil(): return (spacing * jnp.stack(forces), spacing * jnp.stack(diagonal))  62 us
    ppermute x16, starting transfers between devices, shifted(): lax.ppermute(value, axis, [(source, source + steps) for source in range(l...  56.6 us
    ppermute x16, waiting for transfers between devices, shifted(): lax.ppermute(value, axis, [(source, source + steps) for source in range(l...  32.9 us
    reduce_sum x4, other arithmetic, coarsen(): return reducer(shaped, axis=(-5, -3, -1))  13.7 us
  transfers between devices with their start and end apart: 78, of which 48 were waited for; matrix products, arithmetic and copies ran while one was open for 12% of the time, Pallas kernels for 0%

commit v1 on v0

v1 whole, which is shorter than its diff:
```python
import jax
import jax.numpy as jnp
from jax import lax
from jax.experimental import pallas as pl
from jax.experimental.pallas import tpu as pltpu
from jax.sharding import PartitionSpec as P

LEVELS = 16
COARSE = 4
EMIN = 0.001
OMEGA = 0.5

POISSON = 0.3
LAME = POISSON / ((1 + POISSON) * (1 - 2 * POISSON))
SHEAR = 1 / (2 * (1 + POISSON))
KDIAG = (LAME + 4 * SHEAR) / 16 + 2 * (LAME + 3 * SHEAR) / 48 + 2 * SHEAR / 48 + (LAME + 4 * SHEAR) / 144

PLANES, ROWS, LANES = 14, 40, 256
OWN = 3
EDGE = 4
EDGE1 = 12

F32 = jnp.float32


def element(c, s):
    s16l, s16m = s * (LAME / 16), s * (SHEAR / 16)
    s16n = s * (2 * SHEAR / 16)
    s48l, s48m, s48n = s * (LAME / 48), s * (SHEAR / 48), s * ((LAME + 3 * SHEAR) / 48)
    s144 = s * ((LAME + 4 * SHEAR) / 144)

    def at(*dims):
        return tuple(1 if d in dims else 0 for d in range(3))

    g = {}
    trace = s16l * (c[0, at(0)] + c[1, at(1)] + c[2, at(2)])
    for i in range(3):
        g[i, at(i)] = s16n * c[i, at(i)] + trace
    for i, j in ((0, 1), (0, 2), (1, 2)):
        force = s16m * (c[i, at(j)] + c[j, at(i)])
        g[i, at(j)] = force
        g[j, at(i)] = force
    for j in range(3):
        i, k = [d for d in range(3) if d != j]
        first, second = c[i, at(i, j)], c[k, at(k, j)]
        g[i, at(i, j)] = s48n * first + s48l * second
        g[k, at(k, j)] = s48n * second + s48l * first
    twists = [c[i, at(*[d for d in range(3) if d != i])] for i in range(3)]
    total = twists[0] + twists[1] + twists[2]
    for i in range(3):
        g[i, at(*[d for d in range(3) if d != i])] = s48m * (twists[i] + total)
        g[i, (1, 1, 1)] = s144 * c[i, (1, 1, 1)]
    return g


def stencil(u_ref, s_ref, emit, first, count, tiles, y_ref, x_ref, hi_ref, q_ref):
    width = u_ref.shape[-1]
    parts = width // 128

    def lanes(part):
        return pl.ds(128 * part, 128)

    def spread_y(z):
        for t in tiles:
            rows = pl.ds(8 * t, 8)
            for c in range(3):
                u = u_ref[c, z, rows, :]
                after = pltpu.roll(u, width - 1, 1)
                for k, value in enumerate((u + after, after - u)):
                    for part in range(parts):
                        y_ref[2 * c + k, part, rows, :] = value[:, 128 * part: 128 * part + 128]

    def spread_x(t, part):
        out = []
        for k in range(6):
            here = y_ref[k, part, pl.ds(8 * t, 8), :]
            after = y_ref[k, part, pl.ds(8 * t + 1, 8), :]
            out += [here + after, after - here]
        return out

    spread_y(first - 1)
    for t in tiles:
        for part in range(parts):
            for i, value in enumerate(spread_x(t, part)):
                x_ref[i, part, pl.ds(8 * t, 8), :] = value

    def layer(step, carry):
        e = first - 1 + step
        spread_y(e + 1)
        for t in tiles:
            rows = pl.ds(8 * t, 8)
            sums = [[], [], []]
            for part in range(parts):
                here = lanes(part)
                c = {}
                for i, now in enumerate(spread_x(t, part)):
                    comp, yt, xt = i // 4, i // 2 % 2, i % 2
                    before = x_ref[i, part, rows, :]
                    x_ref[i, part, rows, :] = now
                    c[comp, (0, xt, yt)] = now + before
                    c[comp, (1, xt, yt)] = now - before
                g = element(c, s_ref[e, rows, here])
                for comp in range(3):
                    ends = []
                    for yt in range(2):
                        node = []
                        for xt in range(2):
                            i = 4 * comp + 2 * yt + xt
                            d = g[comp, (1, xt, yt)]
                            a = g.get((comp, (0, xt, yt)))
                            low = hi_ref[i, part, rows, :]
                            if a is None:
                                node.append(low - d)
                                hi_ref[i, part, rows, :] = d
                            else:
                                node.append(low + (a - d))
                                hi_ref[i, part, rows, :] = a + d
                        k = 2 * comp + yt
                        q_ref[k, part, pl.ds(8 * t + 1, 8), :] = node[0] + node[1]
                        ends.append(node[0] - node[1] + q_ref[k, part, rows, :])
                    sums[comp].append(ends)
            forces = []
            for comp in range(3):
                low = jnp.concatenate([a - d for a, d in sums[comp]], 1) if parts > 1 else sums[comp][0][0] - sums[comp][0][1]
                high = jnp.concatenate([a + d for a, d in sums[comp]], 1) if parts > 1 else sums[comp][0][0] + sums[comp][0][1]
                forces.append(low + pltpu.roll(high, 1, 1))
            emit(e, t, forces)
        return carry

    lax.fori_loop(0, count + 1, layer, 0)


def box_inverse(total, factor):
    positive = total > 0
    return jnp.where(positive, OMEGA / (factor * jnp.where(positive, total, 1.0)), 0.0)


def lane_index(shape):
    return lax.broadcasted_iota(jnp.int32, shape, len(shape) - 1)


def call(body, outs, args, scratch=(), in_specs=None, out_specs=None):
    whole = pl.BlockSpec(memory_space=pltpu.VMEM)
    specs = [pl.BlockSpec(memory_space=pltpu.SMEM)] + [whole] * (len(args) - 1)
    return pl.pallas_call(
        body,
        out_shape=tuple(
            jax.ShapeDtypeStruct(shape, F32) if body is coarse else pltpu.VMEM(shape, F32) for shape in outs
        ),
        in_specs=in_specs or specs,
        out_specs=out_specs or tuple(whole for _ in outs),
        scratch_shapes=list(scratch),
        compiler_params=pltpu.CompilerParams(vmem_limit_bytes=24 * 1024 * 1024),
    )(args[0], *(value if body is prepare else pltpu.with_memory_space_constraint(value, pltpu.VMEM) for value in args[1:]))


def prepare(gz_ref, disp_ref, load_ref, code_ref, fixed_ref, base_ref, send_ref):
    gz = gz_ref[0]
    for z in range(8):
        level = code_ref[z].astype(F32) / (LEVELS - 1)
        base_ref[9, z] = EMIN + (1.0 - EMIN) * level * level * level
        for c in range(3):
            free = 1.0 - fixed_ref[c, z].astype(F32)
            base_ref[c, z] = free * disp_ref[c, z]
            base_ref[3 + c, z] = load_ref[c, z]
            base_ref[6 + c, z] = free
    three, two = 5 * (1 - gz), 6 * (1 - gz)
    for c in range(3):
        for j in range(3):
            send_ref[3 * c + j] = base_ref[c, three + j]
        for j in range(2):
            send_ref[9 + 2 * c + j] = base_ref[3 + c, two + j]
            send_ref[15 + 2 * c + j] = base_ref[6 + c, two + j]
    for j in range(3):
        send_ref[21 + j] = base_ref[9, three + j]


def edge_rows(gz_ref, base_ref, zrecv_ref, right_ref, left_ref):
    for k in range(104):
        if k < 80:
            f, z = divmod(k, 8)
            right_ref[pl.ds(4 * k, 4)] = base_ref[f, z, pl.ds(28, 4)]
            left_ref[pl.ds(4 * k, 4)] = base_ref[f, z, pl.ds(0, 4)]
        else:
            right_ref[pl.ds(4 * k, 4)] = zrecv_ref[k - 80, pl.ds(28, 4)]
            left_ref[pl.ds(4 * k, 4)] = zrecv_ref[k - 80, pl.ds(0, 4)]


def fine_places(gz):
    places = [(f, OWN + z) for f in range(10) for z in range(8)]
    three, two = 11 * (1 - gz), 11 - 10 * gz
    places += [(c, three + j) for c in range(3) for j in range(3)]
    places += [(3 + c, two + j) for c in range(3) for j in range(2)]
    places += [(6 + c, two + j) for c in range(3) for j in range(2)]
    places += [(9, three + j) for j in range(3)]
    return places


def edge_lanes(gz_ref, base_ref, zrecv_ref, low_ref, high_ref, ext_ref, send_ref):
    gz = gz_ref[0]
    blank = jnp.zeros((ROWS, 128), F32)
    for f in range(10):
        for z in list(range(OWN)) + list(range(OWN + 8, PLANES)):
            ext_ref[f, z] = blank
    lane = lane_index((ROWS, 128))
    packed = None
    for k, (f, z) in enumerate(fine_places(gz)):
        ext_ref[f, z, pl.ds(0, 4)] = low_ref[pl.ds(4 * k, 4)]
        ext_ref[f, z, pl.ds(4, 32)] = base_ref[k // 8, k % 8] if k < 80 else zrecv_ref[k - 80]
        ext_ref[f, z, pl.ds(36, 4)] = high_ref[pl.ds(4 * k, 4)]
        group = k % 16
        value = ext_ref[f, z]
        if group == 0:
            packed = value
        else:
            packed = jnp.where((lane >= 8 * group - 4) & (lane < 8 * group + 4), pltpu.roll(value, 8 * group, 1), packed)
        if group == 15 or k == 103:
            send_ref[k // 16] = packed


def fine_down(gz_ref, ext_ref, low_ref, high_ref,
              main_ref, send_ref, plane_ref,
              y_ref, x_ref, hi_ref, q_ref, r_ref, pair_ref, rows_ref):
    gz = gz_ref[0]
    blank = jnp.zeros((ROWS, 128), F32)
    for f in range(10):
        for z in range(PLANES):
            main_ref[f, z, :, pl.ds(0, 128)] = ext_ref[f, z]
        for z in list(range(OWN)) + list(range(OWN + 8, PLANES)):
            main_ref[f, z, :, pl.ds(128, 128)] = blank
    lane = lane_index((ROWS, 128))
    merged = None
    for k, (f, z) in enumerate(fine_places(gz)):
        group = k % 16
        if group == 0:
            merged = jnp.where(lane % 8 < 4, high_ref[k // 16], low_ref[k // 16])
        value = merged if group == 0 else pltpu.roll(merged, 128 - 8 * group, 1)
        main_ref[f, z, :, pl.ds(128, 128)] = jnp.where((lane < EDGE) | (lane >= 128 - EDGE), value, 0.0)
    for ref in (hi_ref, q_ref, y_ref):
        for k in range(ref.shape[0]):
            ref[k] = jnp.zeros(ref.shape[1:], F32)

    for c in range(3):
        for z1 in range(4):
            z = OWN + 2 * z1
            pair_ref[0] = jnp.minimum(
                main_ref[6 + c, z, :, pl.ds(0, 128)], main_ref[6 + c, z + 1, :, pl.ds(0, 128)]
            )
            least = jnp.minimum(pair_ref[0, pl.ds(4, 16, 2), :], pair_ref[0, pl.ds(5, 16, 2), :])
            rows_ref[pl.ds(32 * (4 + c) + 16 * (z1 // 2), 16), pl.ds(128 * (z1 % 2), 128)] = least

    def weigh(z, carry):
        for t in range(5):
            rows = pl.ds(8 * t, 8)
            s = main_ref[9, z, rows, :] + main_ref[9, z - 1, rows, :]
            for part in range(2):
                q_ref[0, part, pl.ds(8 * t + 1, 8), :] = s[:, 128 * part: 128 * part + 128]
            s = s + jnp.concatenate([q_ref[0, part, rows, :] for part in range(2)], 1)
            inverse = box_inverse(s + pltpu.roll(s, 1, 1), KDIAG)
            for c in range(3):
                main_ref[6 + c, z, rows, :] = main_ref[6 + c, z, rows, :] * inverse
        return carry

    lax.fori_loop(1, PLANES, weigh, 0)

    def sweep(z, t, forces):
        rows = pl.ds(8 * t, 8)
        for c in range(3):
            u = main_ref[c, z, rows, :]
            main_ref[c, z, rows, :] = u + main_ref[6 + c, z, rows, :] * (main_ref[3 + c, z, rows, :] - forces[c])

    u_ref, s_ref = main_ref, main_ref.at[9]
    tiles = range(5)

    def one(k, carry):
        stencil(u_ref, s_ref, sweep, 3 - 2 * gz + k * gz, 10 - k, tiles, y_ref, x_ref, hi_ref, q_ref)
        return carry

    lax.fori_loop(0, 2, one, 0)

    def remain(z, t, forces):
        rows = pl.ds(8 * t, 8)
        here = pl.ds(0, 128)
        for c in range(3):
            rest = main_ref[3 + c, z, rows, here] - forces[c][:, :128]
            r_ref[c, z - OWN + 1, rows, :] = jnp.where(main_ref[6 + c, z, rows, here] > 0, rest, 0.0)

    stencil(u_ref, s_ref, remain, OWN, 8, tiles, y_ref, x_ref, hi_ref, q_ref)

    for c in range(3):
        for z1 in range(4):
            pair_ref[0] = r_ref[c, 1 + 2 * z1] + r_ref[c, 2 + 2 * z1]
            total = pair_ref[0, pl.ds(4, 16, 2), :] + pair_ref[0, pl.ds(5, 16, 2), :]
            rows_ref[pl.ds(32 * c + 16 * (z1 // 2), 16), pl.ds(128 * (z1 % 2), 128)] = total
    for z1 in range(4):
        z = OWN + 2 * z1
        pair_ref[0] = main_ref[9, z, :, pl.ds(0, 128)] + main_ref[9, z + 1, :, pl.ds(0, 128)]
        total = pair_ref[0, pl.ds(4, 16, 2), :] + pair_ref[0, pl.ds(5, 16, 2), :]
        rows_ref[pl.ds(32 * 3 + 16 * (z1 // 2), 16), pl.ds(128 * (z1 % 2), 128)] = total
        box = []
        for k in range(2):
            here = pl.ds(128 * k, 128)
            pair_ref[k] = (main_ref[9, z - 2, :, here] + main_ref[9, z - 1, :, here]) + (
                main_ref[9, z, :, here] + main_ref[9, z + 1, :, here]
            )
            box.append(
                (pair_ref[k, pl.ds(2, 16, 2), :] + pair_ref[k, pl.ds(3, 16, 2), :])
                + (pair_ref[k, pl.ds(4, 16, 2), :] + pair_ref[k, pl.ds(5, 16, 2), :])
            )
        lane16 = lane_index((16, 128))
        back = jnp.where(lane16 < 2, pltpu.roll(box[1], 2, 1), pltpu.roll(box[0], 2, 1))
        rows_ref[pl.ds(32 * 7 + 16 * (z1 // 2), 16), pl.ds(128 * (z1 % 2), 128)] = box[0] + back

    source = lax.broadcasted_iota(jnp.int32, (256, 128), 0)
    target = lax.broadcasted_iota(jnp.int32, (256, 128), 1)
    join = jnp.where(source // 2 == target, 1.0, 0.0).astype(F32)
    level1 = jnp.dot(rows_ref[...], join, precision=lax.Precision.HIGHEST, preferred_element_type=F32)

    def part(k):
        return level1[32 * k: 32 * k + 32]

    inverse = box_inverse(part(7), 2.0 * KDIAG / 8)
    results = [part(0), part(1), part(2), part(3) * (2.0 / 8)]
    results += [jnp.where(part(4 + c) > 1.5, inverse, 0.0) for c in range(3)]
    for k in range(7):
        for pair in range(2):
            send_ref[k, pair] = results[k][16 * pair: 16 * pair + 16]
    away = OWN + 6 - 5 * gz
    for c in range(3):
        plane_ref[c] = main_ref[c, away]


def edge_rows1(gz_ref, own_ref, other_ref, full_ref, right_ref, left_ref):
    gz = gz_ref[0]
    for f in range(7):
        full_ref[f, pl.ds(2 * gz, 2)] = own_ref[f]
        full_ref[f, pl.ds(2 - 2 * gz, 2)] = other_ref[f]
    for f in range(7):
        for pair in range(4):
            k = 4 * f + pair
            right_ref[pl.ds(12 * k, 12)] = full_ref[f, pair, pl.ds(4, 12)]
            left_ref[pl.ds(12 * k, 12)] = full_ref[f, pair, pl.ds(0, 12)]


def edge_lanes1(gz_ref, full_ref, low_ref, high_ref, ext_ref, right_ref, left_ref):
    lane = lane_index((ROWS, 128))
    for f in range(7):
        right = left = None
        for pair in range(4):
            k = 4 * f + pair
            ext_ref[f, pair, pl.ds(0, 12)] = low_ref[pl.ds(12 * k, 12)]
            ext_ref[f, pair, pl.ds(12, 16)] = full_ref[f, pair]
            ext_ref[f, pair, pl.ds(28, 12)] = high_ref[pl.ds(12 * k, 12)]
            value = ext_ref[f, pair]
            moved = pltpu.roll(value, 16 * pair, 1) if pair else value
            place = (lane + (128 - 16 * pair)) % 64
            right = moved if right is None else jnp.where(place >= 52, moved, right)
            left = moved if left is None else jnp.where(place < 12, moved, left)
        right_ref[f] = right
        left_ref[f] = left


def coarse(gz_ref, ext_ref, low_ref, high_ref, main_ref, other_ref, out_ref,
           v1_ref, v2_ref, state_ref, y_ref, x_ref, hi_ref, q_ref, r_ref, rows_ref, pair_ref,
           fy_ref, fx_ref, fhi_ref, fq_ref):
    gz = gz_ref[0]
    lane = lane_index((ROWS, 128))
    slots = (3, 4, 5, 6, 7, 8, 9)
    for ref in (y_ref, x_ref, hi_ref, q_ref, fy_ref, fhi_ref, fq_ref):
        for k in range(ref.shape[0]):
            ref[k] = jnp.zeros(ref.shape[1:], F32)
    for f in range(10):
        for z in (0, 9):
            v1_ref[f, z] = jnp.zeros((ROWS, 128), F32)
        for z in range(6):
            v2_ref[f, z] = jnp.zeros((24, 128), F32)
    for f in range(7):
        low, high = low_ref[f], high_ref[f]
        for pair in range(4):
            value = ext_ref[f, pair]
            for half in range(2):
                own = value if half == 0 else pltpu.roll(value, 64, 1)
                turn = (64 - 16 * pair - 64 * half) % 128
                below = pltpu.roll(low, turn, 1) if turn else low
                above = pltpu.roll(high, turn, 1) if turn else high
                whole = jnp.where(
                    lane < 64, own, jnp.where(lane < 64 + EDGE1, above, jnp.where(lane >= 128 - EDGE1, below, 0.0))
                )
                v1_ref[slots[f], 1 + 2 * pair + half] = whole
    for c in range(3):
        for z in range(10):
            v1_ref[c, z] = v1_ref[7 + c, z] * v1_ref[3 + c, z]

    def smooth(v_ref):
        def sweep(z, t, forces):
            rows = pl.ds(8 * t, 8)
            for c in range(3):
                u = v_ref[c, z, rows, :]
                v_ref[c, z, rows, :] = u + v_ref[7 + c, z, rows, :] * (v_ref[3 + c, z, rows, :] - forces[c])
        return sweep

    s1_ref = v1_ref.at[6]
    stencil(v1_ref, s1_ref, smooth(v1_ref), 1, 8, range(5), y_ref, x_ref, hi_ref, q_ref)

    def remain(z, t, forces):
        rows = pl.ds(8 * t, 8)
        for c in range(3):
            rest = v1_ref[3 + c, z, rows, :] - forces[c]
            r_ref[c, z, rows, :] = jnp.where(v1_ref[7 + c, z, rows, :] > 0, rest, 0.0)

    stencil(v1_ref, s1_ref, remain, 1, 8, range(5), y_ref, x_ref, hi_ref, q_ref)

    for z2 in range(4):
        z = 1 + 2 * z2
        for c in range(3):
            r_ref[c, z] = r_ref[c, z] + r_ref[c, z + 1]
            rows_ref[pl.ds(24 * (4 * c + z2), 20)] = r_ref[c, z, pl.ds(0, 20, 2), :] + r_ref[c, z, pl.ds(1, 20, 2), :]
            r_ref[c, 9] = jnp.where((v1_ref[7 + c, z] > 0) & (v1_ref[7 + c, z + 1] > 0), 1.0, 0.0)
            rows_ref[pl.ds(24 * (16 + 4 * c + z2), 20)] = jnp.minimum(
                r_ref[c, 9, pl.ds(0, 20, 2), :], r_ref[c, 9, pl.ds(1, 20, 2), :]
            )
        r_ref[0, 9] = v1_ref[6, z] + v1_ref[6, z + 1]
        rows_ref[pl.ds(24 * (12 + z2), 20)] = r_ref[0, 9, pl.ds(0, 20, 2), :] + r_ref[0, 9, pl.ds(1, 20, 2), :]
    for k in range(28):
        rows_ref[pl.ds(24 * k + 20, 4)] = jnp.zeros((4, 128), F32)
    source = lax.broadcasted_iota(jnp.int32, (128, 128), 0)
    target = lax.broadcasted_iota(jnp.int32, (128, 128), 1)
    used = (target < 40) | (target >= 120)
    fold = (source // 2 + jnp.where(target < 64, 0, 64) == target) & used
    join = jnp.where(fold, 1.0, 0.0).astype(F32)
    level2 = jnp.dot(rows_ref[...], join, precision=lax.Precision.HIGHEST, preferred_element_type=F32)

    def part(k, z2):
        return level2[24 * (4 * k + z2): 24 * (4 * k + z2) + 24]

    for z2 in range(4):
        for c in range(3):
            v2_ref[3 + c, 1 + z2] = part(c, z2)
            v2_ref[7 + c, 1 + z2] = jnp.where(part(4 + c, z2) > 1.5, 1.0, 0.0)
        v2_ref[6, 1 + z2] = part(3, z2) * (4.0 / 2.0 / 8.0)
    for z in range(1, 5):
        for t in range(3):
            rows = pl.ds(8 * t, 8)
            s = v2_ref[6, z, rows, :] + v2_ref[6, z - 1, rows, :]
            q_ref[0, 0, pl.ds(8 * t + 1, 8), :] = s
            s = s + q_ref[0, 0, rows, :]
            inverse = box_inverse(s + pltpu.roll(s, 1, 1), KDIAG)
            for c in range(3):
                weight = v2_ref[7 + c, z, rows, :] * inverse
                v2_ref[7 + c, z, rows, :] = weight
                v2_ref[c, z, rows, :] = weight * v2_ref[3 + c, z, rows, :]

    def again(k, carry):
        stencil(v2_ref, v2_ref.at[6], smooth(v2_ref), 1, 4, range(3), y_ref, x_ref, hi_ref, q_ref)
        return carry

    lax.fori_loop(0, COARSE - 1, again, 0)

    part_of = jnp.where(
        (source == jnp.where(target < 96, target // 2, target // 2 + 64)), 1.0, 0.0
    ).astype(F32)
    for c in range(3):
        for z2 in range(4):
            rows_ref[pl.ds(24 * (4 * c + z2), 24)] = v2_ref[c, 1 + z2]
    spread = jnp.dot(rows_ref[pl.ds(0, 288)], part_of, precision=lax.Precision.HIGHEST, preferred_element_type=F32)
    for c in range(3):
        for z2 in range(4):
            k = 24 * (4 * c + z2)
            value = spread[k: k + 24][:20]
            r_ref[c, 9, pl.ds(0, 20, 2), :] = value
            r_ref[c, 9, pl.ds(1, 20, 2), :] = value
            for z in (1 + 2 * z2, 2 + 2 * z2):
                v1_ref[c, z] = v1_ref[c, z] + jnp.where(v1_ref[7 + c, z] > 0, r_ref[c, 9], 0.0)

    def second(k, carry):
        stencil(v1_ref, s1_ref, smooth(v1_ref), 1 + 2 * gz + k * gz, 6 - k, range(1, 4), y_ref, x_ref, hi_ref, q_ref)
        return carry

    lax.fori_loop(0, 2, second, 0)

    start = 4 * gz
    for c in range(3):
        for j in range(6):
            rows_ref[pl.ds(24 * (6 * c + j), 24)] = v1_ref[c, start + j, pl.ds(8, 24), :]
    target2 = lax.broadcasted_iota(jnp.int32, (128, 256), 1)
    source2 = lax.broadcasted_iota(jnp.int32, (128, 256), 0)
    copies = jnp.where(source2 == target2 // 2, 1.0, 0.0).astype(F32)
    fine = jnp.dot(rows_ref[pl.ds(0, 432)], copies, precision=lax.Precision.HIGHEST, preferred_element_type=F32)
    for c in range(3):
        for z in range(PLANES):
            state_ref[c, z] = main_ref[c, z]
        state_ref[c, 12 - 11 * gz] = other_ref[c]
        for j in range(6):
            k = 24 * (6 * c + j)
            value = fine[k: k + 24][2:22]
            for k in range(2):
                here = pl.ds(128 * k, 128)
                pair_ref[k, pl.ds(0, 20, 2), :] = value[:, 128 * k: 128 * k + 128]
                pair_ref[k, pl.ds(1, 20, 2), :] = value[:, 128 * k: 128 * k + 128]
                for half in range(2):
                    z = 1 + 2 * j + half
                    state_ref[c, z, :, here] = state_ref[c, z, :, here] + jnp.where(
                        main_ref[6 + c, z, :, here] > 0, pair_ref[k], 0.0
                    )

    def sweep(z, t, forces):
        rows = pl.ds(8 * t, 8)
        for c in range(3):
            u = state_ref[c, z, rows, :]
            state_ref[c, z, rows, :] = u + main_ref[6 + c, z, rows, :] * (main_ref[3 + c, z, rows, :] - forces[c])

    def last(k, carry):
        stencil(state_ref, main_ref.at[9], sweep, 3 - gz + k * gz, 9 - k, range(5), fy_ref, fx_ref, fhi_ref, fq_ref)
        return carry

    lax.fori_loop(0, 2, last, 0)
    for c in range(3):
        for z in range(8):
            out_ref[c, z] = state_ref[c, OWN + z, pl.ds(4, 32), pl.ds(0, 128)]


def up(value, axis):
    return lax.ppermute(value, axis, [(i, i + 1) for i in range(lax.axis_size(axis) - 1)])


def down(value, axis):
    return lax.ppermute(value, axis, [(i + 1, i) for i in range(lax.axis_size(axis) - 1)])


def swap(value):
    return lax.ppermute(value, "gz", [(0, 1), (1, 0)])


def scratch_of(rows, width):
    return [
        pltpu.VMEM((6, width // 128, rows + 8, 128), F32),
        pltpu.VMEM((12, width // 128, rows, 128), F32),
        pltpu.VMEM((12, width // 128, rows, 128), F32),
        pltpu.VMEM((6, width // 128, rows + 8, 128), F32),
    ]


def on_device(displacement, load, density_code, fixed_mask):
    gz = lax.axis_index("gz").astype(jnp.int32).reshape(1)
    base, zsend = call(
        prepare, [(10, 8, 32, 128), (24, 32, 128)], [gz, displacement, load, density_code, fixed_mask]
    )
    zrecv = swap(zsend)
    right, left = call(edge_rows, [(416, 128)] * 2, [gz, base, zrecv])
    low, high = up(right, "gx"), down(left, "gx")
    ext, ysend = call(
        edge_lanes, [(10, PLANES, ROWS, 128), (7, ROWS, 128)], [gz, base, zrecv, low, high]
    )
    low, high = up(ysend, "gy"), down(ysend, "gy")
    main, send1, plane = call(
        fine_down,
        [(10, PLANES, ROWS, LANES), (7, 2, 16, 128), (3, ROWS, LANES)],
        [gz, ext, low, high],
        scratch_of(ROWS, LANES)
        + [pltpu.VMEM((3, 9, ROWS, 128), F32), pltpu.VMEM((2, ROWS, 128), F32), pltpu.VMEM((256, 256), F32)],
    )
    other1 = swap(send1)
    other_plane = swap(plane)
    full, right, left = call(edge_rows1, [(7, 4, 16, 128), (336, 128), (336, 128)], [gz, send1, other1])
    low, high = up(right, "gx"), down(left, "gx")
    ext1, right, left = call(
        edge_lanes1, [(7, 4, ROWS, 128), (7, ROWS, 128), (7, ROWS, 128)], [gz, full, low, high]
    )
    low, high = up(right, "gy"), down(left, "gy")
    (out,) = call(
        coarse,
        [(3, 8, 32, 128)],
        [gz, ext1, low, high, main, other_plane],
        [
            pltpu.VMEM((10, 10, ROWS, 128), F32),
            pltpu.VMEM((10, 6, 24, 128), F32),
            pltpu.VMEM((3, PLANES, ROWS, LANES), F32),
        ]
        + scratch_of(ROWS, 128)
        + [pltpu.VMEM((3, 10, ROWS, 128), F32), pltpu.VMEM((672, 128), F32), pltpu.VMEM((2, ROWS, 128), F32)]
        + scratch_of(ROWS, LANES),
    )
    return out


def solution(mesh):
    return jax.shard_map(
        on_device,
        mesh=mesh,
        in_specs=(
            P(None, "gz", "gx", "gy"),
            P(None, "gz", "gx", "gy"),
            P("gz", "gx", "gy"),
            P(None, "gz", "gx", "gy"),
        ),
        out_specs=P(None, "gz", "gx", "gy"),
        check_vma=False,
    )
```

time: 570 us -> 122 us (0.21)
  the two profiles are of different devices: /device:TPU:398 before, /device:TPU:102 now
where the time goes in v1:
time: 122 us
  Pallas kernels  46.6 us (38%)
  waiting for transfers between devices  37.1 us (30%)
  starting transfers between devices  34.2 us (28%)
  local copies, waits for them, and re-layouts  3.89 us (3%)
    pallas_call x7, Pallas kernels, call(): pl.pallas_call(body, out_shape=tuple((jax.ShapeDtypeStruct(shape, F32) if...  46.6 us
    ppermute x3, waiting for transfers between devices, swap(): return lax.ppermute(value, 'gz', [(0, 1), (1, 0)])  17.5 us
    ppermute x4, starting transfers between devices, down(): lax.ppermute(value, axis, [(i + 1, i) for i in range(lax.axis_size(axis)...  13.6 us
    ppermute x4, starting transfers between devices, up(): lax.ppermute(value, axis, [(i, i + 1) for i in range(lax.axis_size(axis)...  11.9 us
    ppermute x4, waiting for transfers between devices, down(): lax.ppermute(value, axis, [(i + 1, i) for i in range(lax.axis_size(axis)...  10.2 us
    ppermute x4, waiting for transfers between devices, up(): lax.ppermute(value, axis, [(i, i + 1) for i in range(lax.axis_size(axis)...  9.36 us
    ppermute x3, starting transfers between devices, swap(): return lax.ppermute(value, 'gz', [(0, 1), (1, 0)])  8.67 us
    unnamed x8, local copies, waits for them, and re-layouts  3.89 us
  transfers between devices with their start and end apart: 11, of which 9 were waited for; matrix products, arithmetic and copies ran while one was open for 0% of the time, Pallas kernels for 0%

profile of v1, /device:TPU:102, one launch (start us, length us, event | category | flops | bytes accessed | tf_op | source)
XLA Modules:
  0.0 121.9 jit_solution(8852448366948055908)
XLA Ops:
  0.0 0.0 copy-start
  0.0 1.0 copy-done
  1.0 0.0 copy-start.1
  1.0 1.0 copy-done.1
  2.0 0.0 copy-start.2
  2.0 1.0 copy-done.2
  3.0 0.0 copy-start.3
  3.0 0.9 copy-done.3
  3.9 0.1 shard_map.46
  4.0 3.5 %collective-permute-start = (f32[24,32,128]{2,1,0:T(8,128)S(1)}, f32[24,32,128]{2,1,0:T(8,128)S(1)}, u32[]{:S(2)}, u32[]{:S(2)}) collective-permute-start(f32[24,32,128]{2,1,0:T(8,128)S(1)} %get-tuple-element.21), channel_id=1, source_target_pairs={{0,1},{1,0},{2,3},{3,2},{4,5},{5,4},{6,7},{7,6},{8,9},{9,8},{10,11... | collective-permute-start | bytes 1179656 | tf_op jit(solution)/shard_map/ppermute | solution.py:531
  7.5 9.3 %collective-permute-done.zrecv_ref = f32[24,32,128]{2,1,0:T(8,128)S(1)} collective-permute-done((f32[24,32,128]{2,1,0:T(8,128)S(1)}, f32[24,32,128]{2,1,0:T(8,128)S(1)}, u32[]{:S(2)}, u32[]{:S(2)}) %collective-permute-start) | collective-permute-done | bytes 393248 | tf_op jit(solution)/shard_map/ppermute | solution.py:531
  16.8 0.1 shard_map.47
  16.8 5.0 %collective-permute-start.1 = (f32[416,128]{1,0:T(8,128)S(1)}, f32[416,128]{1,0:T(8,128)S(1)}, u32[]{:S(2)}, u32[]{:S(2)}) collective-permute-start(f32[416,128]{1,0:T(8,128)S(1)} %get-tuple-element.22), channel_id=1, source_target_pairs={{0,32},{32,64},{64,96},{96,128},{128,160},{160,192},{192,224},{224... | collective-permute-start | bytes 638984 | tf_op jit(solution)/shard_map/ppermute | solution.py:523
  21.9 1.9 %collective-permute-start.2 = (f32[416,128]{1,0:T(8,128)S(1)}, f32[416,128]{1,0:T(8,128)S(1)}, u32[]{:S(2)}, u32[]{:S(2)}) collective-permute-start(f32[416,128]{1,0:T(8,128)S(1)} %get-tuple-element.23), channel_id=1, source_target_pairs={{32,0},{64,32},{96,64},{128,96},{160,128},{192,160},{224,192},{256... | collective-permute-start | bytes 638984 | tf_op jit(solution)/shard_map/ppermute | solution.py:527
  23.8 1.7 %collective-permute-done.1.low_ref = f32[416,128]{1,0:T(8,128)S(1)} collective-permute-done((f32[416,128]{1,0:T(8,128)S(1)}, f32[416,128]{1,0:T(8,128)S(1)}, u32[]{:S(2)}, u32[]{:S(2)}) %collective-permute-start.1) | collective-permute-done | bytes 213024 | tf_op jit(solution)/shard_map/ppermute | solution.py:523
  25.5 5.3 %collective-permute-done.2.high_ref = f32[416,128]{1,0:T(8,128)S(1)} collective-permute-done((f32[416,128]{1,0:T(8,128)S(1)}, f32[416,128]{1,0:T(8,128)S(1)}, u32[]{:S(2)}, u32[]{:S(2)}) %collective-permute-start.2) | collective-permute-done | bytes 213024 | tf_op jit(solution)/shard_map/ppermute | solution.py:527
  30.9 0.7 shard_map.48
  31.6 2.8 %collective-permute-start.4 = (f32[7,40,128]{2,1,0:T(8,128)S(1)}, f32[7,40,128]{2,1,0:T(8,128)S(1)}, u32[]{:S(2)}, u32[]{:S(2)}) collective-permute-start(f32[7,40,128]{2,1,0:T(8,128)S(1)} %get-tuple-element.25), channel_id=1, source_target_pairs={{2,0},{4,2},{6,4},{8,6},{10,8},{12,10},{14,12},{16,14},{18,16},{20... | collective-permute-start | bytes 430088 | tf_op jit(solution)/shard_map/ppermute | solution.py:527
  34.4 1.9 %collective-permute-start.3 = (f32[7,40,128]{2,1,0:T(8,128)S(1)}, f32[7,40,128]{2,1,0:T(8,128)S(1)}, u32[]{:S(2)}, u32[]{:S(2)}) collective-permute-start(f32[7,40,128]{2,1,0:T(8,128)S(1)} %get-tuple-element.25), channel_id=1, source_target_pairs={{0,2},{2,4},{4,6},{6,8},{8,10},{10,12},{12,14},{14,16},{16,18},{18... | collective-permute-start | bytes 430088 | tf_op jit(solution)/shard_map/ppermute | solution.py:523
  36.4 0.7 collective-permute-done.4.high_ref
  37.0 6.2 %collective-permute-done.3.low_ref = f32[7,40,128]{2,1,0:T(8,128)S(1)} collective-permute-done((f32[7,40,128]{2,1,0:T(8,128)S(1)}, f32[7,40,128]{2,1,0:T(8,128)S(1)}, u32[]{:S(2)}, u32[]{:S(2)}) %collective-permute-start.3) | collective-permute-done | bytes 143392 | tf_op jit(solution)/shard_map/ppermute | solution.py:523
  43.3 20.8 %shard_map.49 = (f32[10,14,40,256]{3,2,1,0:T(8,128)S(1)}, f32[7,2,16,128]{3,2,1,0:T(8,128)S(1)}, f32[3,40,256]{2,1,0:T(8,128)S(1)}) custom-call(s32[1]{0:T(128)} %bitcast.gz_ref, f32[10,14,40,128]{3,2,1,0:T(8,128)S(1)} %get-tuple-element.24.ext_ref, f32[7,40,128]{2,1,0:T(8,128)S(1)} %collective-permute-done.3.low_ref, ...), custom_call_target="tpu_custom_call" | custom-call | tf_op jit(solution)/shard_map/pallas_call | solution.py:145
  64.1 2.6 %collective-permute-start.5 = (f32[7,2,16,128]{3,2,1,0:T(8,128)S(1)}, f32[7,2,16,128]{3,2,1,0:T(8,128)S(1)}, u32[]{:S(2)}, u32[]{:S(2)}) collective-permute-start(f32[7,2,16,128]{3,2,1,0:T(8,128)S(1)} %get-tuple-element.26.own_ref), channel_id=1, source_target_pairs={{0,1},{1,0},{2,3},{3,2},{4,5},{5,4},{6,7},{7,6},{8,9},{9,8},{10,11... | collective-permute-start | bytes 344072 | tf_op jit(solution)/shard_map/ppermute | solution.py:531
  66.7 4.1 %collective-permute-done.5.other_ref = f32[7,2,16,128]{3,2,1,0:T(8,128)S(1)} collective-permute-done((f32[7,2,16,128]{3,2,1,0:T(8,128)S(1)}, f32[7,2,16,128]{3,2,1,0:T(8,128)S(1)}, u32[]{:S(2)}, u32[]{:S(2)}) %collective-permute-start.5) | collective-permute-done | bytes 114720 | tf_op jit(solution)/shard_map/ppermute | solution.py:531
  70.8 3.0 %collective-permute-start.6 = (f32[336,128]{1,0:T(8,128)S(1)}, f32[336,128]{1,0:T(8,128)S(1)}, u32[]{:S(2)}, u32[]{:S(2)}) collective-permute-start(f32[336,128]{1,0:T(8,128)S(1)} %get-tuple-element.28), channel_id=1, source_target_pairs={{0,32},{32,64},{64,96},{96,128},{128,160},{160,192},{192,224},{224... | collective-permute-start | bytes 516104 | tf_op jit(solution)/shard_map/ppermute | solution.py:523
  73.8 2.9 %collective-permute-start.7 = (f32[336,128]{1,0:T(8,128)S(1)}, f32[336,128]{1,0:T(8,128)S(1)}, u32[]{:S(2)}, u32[]{:S(2)}) collective-permute-start(f32[336,128]{1,0:T(8,128)S(1)} %get-tuple-element.29), channel_id=1, source_target_pairs={{32,0},{64,32},{96,64},{128,96},{160,128},{192,160},{224,192},{256... | collective-permute-start | bytes 516104 | tf_op jit(solution)/shard_map/ppermute | solution.py:527
  76.7 1.4 %collective-permute-done.6.low_ref = f32[336,128]{1,0:T(8,128)S(1)} collective-permute-done((f32[336,128]{1,0:T(8,128)S(1)}, f32[336,128]{1,0:T(8,128)S(1)}, u32[]{:S(2)}, u32[]{:S(2)}) %collective-permute-start.6) | collective-permute-done | bytes 172064 | tf_op jit(solution)/shard_map/ppermute | solution.py:523
  78.1 4.2 %collective-permute-done.7.high_ref = f32[336,128]{1,0:T(8,128)S(1)} collective-permute-done((f32[336,128]{1,0:T(8,128)S(1)}, f32[336,128]{1,0:T(8,128)S(1)}, u32[]{:S(2)}, u32[]{:S(2)}) %collective-permute-start.7) | collective-permute-done | bytes 172064 | tf_op jit(solution)/shard_map/ppermute | solution.py:527
  82.3 0.2 shard_map.51
  82.5 1.9 %collective-permute-start.8 = (f32[7,40,128]{2,1,0:T(8,128)S(1)}, f32[7,40,128]{2,1,0:T(8,128)S(1)}, u32[]{:S(2)}, u32[]{:S(2)}) collective-permute-start(f32[7,40,128]{2,1,0:T(8,128)S(1)} %get-tuple-element.31), channel_id=1, source_target_pairs={{0,2},{2,4},{4,6},{6,8},{8,10},{10,12},{12,14},{14,16},{16,18},{18... | collective-permute-start | bytes 430088 | tf_op jit(solution)/shard_map/ppermute | solution.py:523
  84.4 6.0 %collective-permute-start.9 = (f32[7,40,128]{2,1,0:T(8,128)S(1)}, f32[7,40,128]{2,1,0:T(8,128)S(1)}, u32[]{:S(2)}, u32[]{:S(2)}) collective-permute-start(f32[7,40,128]{2,1,0:T(8,128)S(1)} %get-tuple-element.32), channel_id=1, source_target_pairs={{2,0},{4,2},{6,4},{8,6},{10,8},{12,10},{14,12},{16,14},{18,16},{20... | collective-permute-start | bytes 430088 | tf_op jit(solution)/shard_map/ppermute | solution.py:527
  90.5 2.6 %collective-permute-start.10 = (f32[3,40,256]{2,1,0:T(8,128)S(1)}, f32[3,40,256]{2,1,0:T(8,128)S(1)}, u32[]{:S(2)}, u32[]{:S(2)}) collective-permute-start(f32[3,40,256]{2,1,0:T(8,128)S(1)} %get-tuple-element.34), channel_id=1, source_target_pairs={{0,1},{1,0},{2,3},{3,2},{4,5},{5,4},{6,7},{7,6},{8,9},{9,8},{10,11... | collective-permute-start | bytes 368648 | tf_op jit(solution)/shard_map/ppermute | solution.py:531
  93.1 4.2 %collective-permute-done.10.other_ref = f32[3,40,256]{2,1,0:T(8,128)S(1)} collective-permute-done((f32[3,40,256]{2,1,0:T(8,128)S(1)}, f32[3,40,256]{2,1,0:T(8,128)S(1)}, u32[]{:S(2)}, u32[]{:S(2)}) %collective-permute-start.10) | collective-permute-done | bytes 122912 | tf_op jit(solution)/shard_map/ppermute | solution.py:531
  97.3 0.0 collective-permute-done.8.low_ref
  97.3 0.0 collective-permute-done.9.high_ref
  97.3 24.6 %shard_map.52 = f32[3,8,32,128]{3,2,1,0:T(8,128)} custom-call(s32[1]{0:T(128)} %bitcast.gz_ref, f32[7,4,40,128]{3,2,1,0:T(8,128)S(1)} %get-tuple-element.30.ext_ref, f32[7,40,128]{2,1,0:T(8,128)S(1)} %collective-permute-done.8.low_ref, f32[7,40,128]{2,1,0:T(8,128)S(1)} %collective-permute-done.9.high_ref, ...), custom_call_target="tpu_custom_call" | custom-call | tf_op jit(solution)/shard_map/pallas_call | solution.py:145
  (1 shorter events, 0.0 us)
Async XLA Ops:
  0.0 1.0 copy-start
  1.0 1.0 copy-start.1
  2.0 1.0 copy-start.2
  3.0 0.9 copy-start.3
  4.0 12.7 %collective-permute-start = (f32[24,32,128]{2,1,0:T(8,128)S(1)}, f32[24,32,128]{2,1,0:T(8,128)S(1)}, u32[]{:S(2)}, u32[]{:S(2)}) collective-permute-start(f32[24,32,128]{2,1,0:T(8,128)S(1)} %get-tuple-element.21), channel_id=1, source_target_pairs={{0,1},{1,0},{2,3},{3,2},{4,5},{5,4},{6,7},{7,6},{8,9},{9,8},{10,11... | collective-permute-start | bytes 1179656 | tf_op jit(solution)/shard_map/ppermute | solution.py:531
  16.8 8.7 %collective-permute-start.1 = (f32[416,128]{1,0:T(8,128)S(1)}, f32[416,128]{1,0:T(8,128)S(1)}, u32[]{:S(2)}, u32[]{:S(2)}) collective-permute-start(f32[416,128]{1,0:T(8,128)S(1)} %get-tuple-element.22), channel_id=1, source_target_pairs={{0,32},{32,64},{64,96},{96,128},{128,160},{160,192},{192,224},{224... | collective-permute-start | bytes 638984 | tf_op jit(solution)/shard_map/ppermute | solution.py:523
  21.9 9.0 %collective-permute-start.2 = (f32[416,128]{1,0:T(8,128)S(1)}, f32[416,128]{1,0:T(8,128)S(1)}, u32[]{:S(2)}, u32[]{:S(2)}) collective-permute-start(f32[416,128]{1,0:T(8,128)S(1)} %get-tuple-element.23), channel_id=1, source_target_pairs={{32,0},{64,32},{96,64},{128,96},{160,128},{192,160},{224,192},{256... | collective-permute-start | bytes 638984 | tf_op jit(solution)/shard_map/ppermute | solution.py:527
  31.6 5.4 %collective-permute-start.4 = (f32[7,40,128]{2,1,0:T(8,128)S(1)}, f32[7,40,128]{2,1,0:T(8,128)S(1)}, u32[]{:S(2)}, u32[]{:S(2)}) collective-permute-start(f32[7,40,128]{2,1,0:T(8,128)S(1)} %get-tuple-element.25), channel_id=1, source_target_pairs={{2,0},{4,2},{6,4},{8,6},{10,8},{12,10},{14,12},{16,14},{18,16},{20... | collective-permute-start | bytes 430088 | tf_op jit(solution)/shard_map/ppermute | solution.py:527
  34.4 8.8 %collective-permute-start.3 = (f32[7,40,128]{2,1,0:T(8,128)S(1)}, f32[7,40,128]{2,1,0:T(8,128)S(1)}, u32[]{:S(2)}, u32[]{:S(2)}) collective-permute-start(f32[7,40,128]{2,1,0:T(8,128)S(1)} %get-tuple-element.25), channel_id=1, source_target_pairs={{0,2},{2,4},{4,6},{6,8},{8,10},{10,12},{12,14},{14,16},{16,18},{18... | collective-permute-start | bytes 430088 | tf_op jit(solution)/shard_map/ppermute | solution.py:523
  64.1 6.7 %collective-permute-start.5 = (f32[7,2,16,128]{3,2,1,0:T(8,128)S(1)}, f32[7,2,16,128]{3,2,1,0:T(8,128)S(1)}, u32[]{:S(2)}, u32[]{:S(2)}) collective-permute-start(f32[7,2,16,128]{3,2,1,0:T(8,128)S(1)} %get-tuple-element.26.own_ref), channel_id=1, source_target_pairs={{0,1},{1,0},{2,3},{3,2},{4,5},{5,4},{6,7},{7,6},{8,9},{9,8},{10,11... | collective-permute-start | bytes 344072 | tf_op jit(solution)/shard_map/ppermute | solution.py:531
  70.8 7.3 %collective-permute-start.6 = (f32[336,128]{1,0:T(8,128)S(1)}, f32[336,128]{1,0:T(8,128)S(1)}, u32[]{:S(2)}, u32[]{:S(2)}) collective-permute-start(f32[336,128]{1,0:T(8,128)S(1)} %get-tuple-element.28), channel_id=1, source_target_pairs={{0,32},{32,64},{64,96},{96,128},{128,160},{160,192},{192,224},{224... | collective-permute-start | bytes 516104 | tf_op jit(solution)/shard_map/ppermute | solution.py:523
  73.8 8.5 %collective-permute-start.7 = (f32[336,128]{1,0:T(8,128)S(1)}, f32[336,128]{1,0:T(8,128)S(1)}, u32[]{:S(2)}, u32[]{:S(2)}) collective-permute-start(f32[336,128]{1,0:T(8,128)S(1)} %get-tuple-element.29), channel_id=1, source_target_pairs={{32,0},{64,32},{96,64},{128,96},{160,128},{192,160},{224,192},{256... | collective-permute-start | bytes 516104 | tf_op jit(solution)/shard_map/ppermute | solution.py:527
  82.5 14.8 %collective-permute-start.8 = (f32[7,40,128]{2,1,0:T(8,128)S(1)}, f32[7,40,128]{2,1,0:T(8,128)S(1)}, u32[]{:S(2)}, u32[]{:S(2)}) collective-permute-start(f32[7,40,128]{2,1,0:T(8,128)S(1)} %get-tuple-element.31), channel_id=1, source_target_pairs={{0,2},{2,4},{4,6},{6,8},{8,10},{10,12},{12,14},{14,16},{16,18},{18... | collective-permute-start | bytes 430088 | tf_op jit(solution)/shard_map/ppermute | solution.py:523
  84.4 12.8 %collective-permute-start.9 = (f32[7,40,128]{2,1,0:T(8,128)S(1)}, f32[7,40,128]{2,1,0:T(8,128)S(1)}, u32[]{:S(2)}, u32[]{:S(2)}) collective-permute-start(f32[7,40,128]{2,1,0:T(8,128)S(1)} %get-tuple-element.32), channel_id=1, source_target_pairs={{2,0},{4,2},{6,4},{8,6},{10,8},{12,10},{14,12},{16,14},{18,16},{20... | collective-permute-start | bytes 430088 | tf_op jit(solution)/shard_map/ppermute | solution.py:527
  90.5 6.8 %collective-permute-start.10 = (f32[3,40,256]{2,1,0:T(8,128)S(1)}, f32[3,40,256]{2,1,0:T(8,128)S(1)}, u32[]{:S(2)}, u32[]{:S(2)}) collective-permute-start(f32[3,40,256]{2,1,0:T(8,128)S(1)} %get-tuple-element.34), channel_id=1, source_target_pairs={{0,1},{1,0},{2,3},{3,2},{4,5},{5,4},{6,7},{7,6},{8,9},{9,8},{10,11... | collective-permute-start | bytes 368648 | tf_op jit(solution)/shard_map/ppermute | solution.py:531

commit v2 on v1

v2 whole, which is shorter than its diff:
```python
import jax
import jax.numpy as jnp
from jax import lax
from jax.experimental import pallas as pl
from jax.experimental.pallas import tpu as pltpu
from jax.sharding import PartitionSpec as P

LEVELS = 16
COARSE = 4
EMIN = 0.001
OMEGA = 0.5

POISSON = 0.3
LAME = POISSON / ((1 + POISSON) * (1 - 2 * POISSON))
SHEAR = 1 / (2 * (1 + POISSON))
KDIAG = (LAME + 4 * SHEAR) / 16 + 2 * (LAME + 3 * SHEAR) / 48 + 2 * SHEAR / 48 + (LAME + 4 * SHEAR) / 144

PLANES, ROWS, LANES = 14, 40, 256
OWN = 3
EDGE = 4
EDGE1 = 12

F32 = jnp.float32


def element(c, s):
    s16l, s16m = s * (LAME / 16), s * (SHEAR / 16)
    s16n = s * (2 * SHEAR / 16)
    s48l, s48m, s48n = s * (LAME / 48), s * (SHEAR / 48), s * ((LAME + 3 * SHEAR) / 48)
    s144 = s * ((LAME + 4 * SHEAR) / 144)

    def at(*dims):
        return tuple(1 if d in dims else 0 for d in range(3))

    g = {}
    trace = s16l * (c[0, at(0)] + c[1, at(1)] + c[2, at(2)])
    for i in range(3):
        g[i, at(i)] = s16n * c[i, at(i)] + trace
    for i, j in ((0, 1), (0, 2), (1, 2)):
        force = s16m * (c[i, at(j)] + c[j, at(i)])
        g[i, at(j)] = force
        g[j, at(i)] = force
    for j in range(3):
        i, k = [d for d in range(3) if d != j]
        first, second = c[i, at(i, j)], c[k, at(k, j)]
        g[i, at(i, j)] = s48n * first + s48l * second
        g[k, at(k, j)] = s48n * second + s48l * first
    twists = [c[i, at(*[d for d in range(3) if d != i])] for i in range(3)]
    total = twists[0] + twists[1] + twists[2]
    for i in range(3):
        g[i, at(*[d for d in range(3) if d != i])] = s48m * (twists[i] + total)
        g[i, (1, 1, 1)] = s144 * c[i, (1, 1, 1)]
    return g


def stencil(u_ref, s_ref, emit, first, count, tiles, y_ref, x_ref, hi_ref, q_ref, r_ref):
    width = u_ref.shape[-1]
    parts = width // 128

    def split(value):
        return [value[:, 128 * part: 128 * part + 128] for part in range(parts)]

    def join(values):
        return jnp.concatenate(values, 1) if parts > 1 else values[0]

    for j in range(count + 2):
        for t in tiles:
            rows = pl.ds(8 * t, 8)
            for c in range(3):
                u = u_ref[c, first - 1 + j, rows, :]
                after = pltpu.roll(u, width - 1, 1)
                for k, value in enumerate((u + after, after - u)):
                    for part, piece in enumerate(split(value)):
                        y_ref[j, 2 * c + k, part, rows, :] = piece

    def spread_x(j, t, part):
        out = []
        for k in range(6):
            here = y_ref[j, k, part, pl.ds(8 * t, 8), :]
            after = y_ref[j, k, part, pl.ds(8 * t + 1, 8), :]
            out += [here + after, after - here]
        return out

    for t in tiles:
        for part in range(parts):
            for i, value in enumerate(spread_x(0, t, part)):
                x_ref[i, part, pl.ds(8 * t, 8), :] = value

    def layer(step, carry):
        e = first - 1 + step
        for t in tiles:
            rows = pl.ds(8 * t, 8)
            for part in range(parts):
                c = {}
                for i, now in enumerate(spread_x(step + 1, t, part)):
                    comp, yt, xt = i // 4, i // 2 % 2, i % 2
                    before = x_ref[i, part, rows, :]
                    x_ref[i, part, rows, :] = now
                    c[comp, (0, xt, yt)] = now + before
                    c[comp, (1, xt, yt)] = now - before
                g = element(c, s_ref[e, rows, pl.ds(128 * part, 128)])
                for comp in range(3):
                    ends = []
                    for yt in range(2):
                        node = []
                        for xt in range(2):
                            i = 4 * comp + 2 * yt + xt
                            d = g[comp, (1, xt, yt)]
                            a = g.get((comp, (0, xt, yt)))
                            low = hi_ref[i, part, rows, :]
                            if a is None:
                                node.append(low - d)
                                hi_ref[i, part, rows, :] = d
                            else:
                                node.append(low + (a - d))
                                hi_ref[i, part, rows, :] = a + d
                        k = 2 * comp + yt
                        q_ref[k, part, pl.ds(8 * t + 1, 8), :] = node[0] + node[1]
                        ends.append(node[0] - node[1] + q_ref[k, part, rows, :])
                    r_ref[step, 2 * comp, part, rows, :] = ends[0] - ends[1]
                    r_ref[step, 2 * comp + 1, part, rows, :] = ends[0] + ends[1]
        return carry

    lax.fori_loop(0, count + 1, layer, 0)

    for j in range(count):
        for t in tiles:
            rows = pl.ds(8 * t, 8)
            forces = []
            for comp in range(3):
                low = join([r_ref[j + 1, 2 * comp, part, rows, :] for part in range(parts)])
                high = join([r_ref[j + 1, 2 * comp + 1, part, rows, :] for part in range(parts)])
                forces.append(low + pltpu.roll(high, 1, 1))
            emit(first + j, t, forces)


def smoother(u_ref, rhs_ref, weight_ref):
    def sweep(z, t, forces):
        rows = pl.ds(8 * t, 8)
        for c in range(3):
            u = u_ref[c, z, rows, :]
            u_ref[c, z, rows, :] = u + weight_ref[c, z, rows, :] * (rhs_ref[c, z, rows, :] - forces[c])

    return sweep


def box_inverse(total, factor):
    positive = total > 0
    return jnp.where(positive, OMEGA / (factor * jnp.where(positive, total, 1.0)), 0.0)


def clear(*refs):
    for ref in refs:
        for k in range(ref.shape[0]):
            ref[k] = jnp.zeros(ref.shape[1:], F32)


def clear_work(y_ref, x_ref, hi_ref, q_ref, r_ref):
    planes, six, parts, rows, _ = y_ref.shape
    for j in range(planes):
        y_ref[j, :, :, pl.ds(rows - 8, 8), :] = jnp.zeros((six, parts, 8, 128), F32)
    clear(hi_ref, q_ref)


def lane_index(shape):
    return lax.broadcasted_iota(jnp.int32, shape, len(shape) - 1)


def call(body, outs, args, scratch=(), inputs="vmem", output="vmem"):
    whole = pl.BlockSpec(memory_space=pltpu.VMEM)
    rest = pl.BlockSpec(memory_space=pltpu.HBM) if inputs == "any" else whole
    values = args[1:]
    if inputs == "vmem":
        values = [pltpu.with_memory_space_constraint(value, pltpu.VMEM) for value in values]
    shape = pltpu.VMEM if output == "vmem" else jax.ShapeDtypeStruct
    return pl.pallas_call(
        body,
        out_shape=tuple(shape(out, F32) for out in outs),
        in_specs=[pl.BlockSpec(memory_space=pltpu.SMEM)] + [rest] * len(values),
        out_specs=tuple(whole for _ in outs),
        scratch_shapes=list(scratch),
        compiler_params=pltpu.CompilerParams(vmem_limit_bytes=24 * 1024 * 1024),
    )(args[0], *values)


def scale_of(code):
    level = code.astype(F32) / (LEVELS - 1)
    return EMIN + (1.0 - EMIN) * level * level * level


def boundary(gz_ref, disp_ref, load_ref, code_ref, fixed_ref, send_ref, disp, load, code, fixed, sems):
    gz = gz_ref[0]
    three, two = 5 * (1 - gz), 6 * (1 - gz)
    copies = [
        pltpu.make_async_copy(code_ref.at[pl.ds(three, 3)], code, sems.at[0]),
        pltpu.make_async_copy(fixed_ref.at[:, pl.ds(three, 3)], fixed, sems.at[1]),
        pltpu.make_async_copy(disp_ref.at[:, pl.ds(three, 3)], disp, sems.at[2]),
        pltpu.make_async_copy(load_ref.at[:, pl.ds(two, 2)], load, sems.at[3]),
    ]
    for copy in copies:
        copy.start()
    for copy in copies:
        copy.wait()
    for j in range(3):
        send_ref[21 + j] = scale_of(code[j])
        for c in range(3):
            send_ref[3 * c + j] = (1.0 - fixed[c, j].astype(F32)) * disp[c, j]
    for c in range(3):
        for j in range(2):
            send_ref[9 + 2 * c + j] = load[c, j]
            send_ref[15 + 2 * c + j] = 1.0 - fixed[c, j + 1 - gz].astype(F32)


def prepare(gz_ref, disp_ref, load_ref, code_ref, fixed_ref, base_ref, right_ref, left_ref):
    for z in range(8):
        base_ref[9, z] = scale_of(code_ref[z])
        for c in range(3):
            free = 1.0 - fixed_ref[c, z].astype(F32)
            base_ref[c, z] = free * disp_ref[c, z]
            base_ref[3 + c, z] = load_ref[c, z]
            base_ref[6 + c, z] = free
    for k in range(80):
        right_ref[pl.ds(4 * k, 4)] = base_ref[k // 8, k % 8, pl.ds(28, 4)]
        left_ref[pl.ds(4 * k, 4)] = base_ref[k // 8, k % 8, pl.ds(0, 4)]


def boundary_rows(gz_ref, low_ref, high_ref, send_ref):
    lower = gz_ref[0] == 0

    def send(k, f, below, above):
        for i, ref in enumerate((low_ref, high_ref)):
            first, second = 4 * (8 * f + below), 4 * (8 * f + above)
            send_ref[pl.ds(8 * k + 4 * i, 4)] = jnp.where(lower, ref[pl.ds(first, 4)], ref[pl.ds(second, 4)])

    for j in range(3):
        send(21 + j, 9, 5 + j, j)
        for c in range(3):
            send(3 * c + j, c, 5 + j, j)
    for c in range(3):
        for j in range(2):
            send(9 + 2 * c + j, 3 + c, 6 + j, j)
            send(15 + 2 * c + j, 6 + c, 6 + j, j)


def fine_places(gz):
    places = [(f, OWN + z) for f in range(10) for z in range(8)]
    three, two = 11 * (1 - gz), 11 - 10 * gz
    places += [(c, three + j) for c in range(3) for j in range(3)]
    places += [(3 + c, two + j) for c in range(3) for j in range(2)]
    places += [(6 + c, two + j) for c in range(3) for j in range(2)]
    places += [(9, three + j) for j in range(3)]
    return places


def edge_lanes(gz_ref, base_ref, zrecv_ref, low_ref, high_ref, beside_ref, ext_ref, send_ref):
    gz = gz_ref[0]
    blank = jnp.zeros((ROWS, 128), F32)
    for f in range(10):
        for z in list(range(OWN)) + list(range(OWN + 8, PLANES)):
            ext_ref[f, z] = blank
    lane = lane_index((ROWS, 128))
    packed = None
    for k, (f, z) in enumerate(fine_places(gz)):
        beside = 8 * (k - 80)
        ext_ref[f, z, pl.ds(0, 4)] = low_ref[pl.ds(4 * k, 4)] if k < 80 else beside_ref[pl.ds(beside, 4)]
        ext_ref[f, z, pl.ds(4, 32)] = base_ref[k // 8, k % 8] if k < 80 else zrecv_ref[k - 80]
        ext_ref[f, z, pl.ds(36, 4)] = high_ref[pl.ds(4 * k, 4)] if k < 80 else beside_ref[pl.ds(beside + 4, 4)]
        group = k % 16
        value = ext_ref[f, z]
        if group == 0:
            packed = value
        else:
            packed = jnp.where((lane >= 8 * group - 4) & (lane < 8 * group + 4), pltpu.roll(value, 8 * group, 1), packed)
        if group == 15 or k == 103:
            send_ref[k // 16] = packed


def fine_down(gz_ref, ext_ref, low_ref, high_ref,
              u_ref, load_ref, weight_ref, s_ref, send_ref, plane_ref,
              y_ref, x_ref, hi_ref, q_ref, r_ref, rest_ref, pair_ref, rows_ref):
    gz = gz_ref[0]
    blank = jnp.zeros((ROWS, 128), F32)
    fields = [ref.at[c] for ref in (u_ref, load_ref, weight_ref) for c in range(3)] + [s_ref]
    for f in range(10):
        for z in range(PLANES):
            fields[f][z, :, pl.ds(0, 128)] = ext_ref[f, z]
        for z in list(range(OWN)) + list(range(OWN + 8, PLANES)):
            fields[f][z, :, pl.ds(128, 128)] = blank
    lane = lane_index((ROWS, 128))
    merged = None
    for k, (f, z) in enumerate(fine_places(gz)):
        group = k % 16
        if group == 0:
            merged = jnp.where(lane % 8 < 4, high_ref[k // 16], low_ref[k // 16])
        value = merged if group == 0 else pltpu.roll(merged, 128 - 8 * group, 1)
        fields[f][z, :, pl.ds(128, 128)] = jnp.where((lane < EDGE) | (lane >= 128 - EDGE), value, 0.0)
    clear_work(y_ref, x_ref, hi_ref, q_ref, r_ref)

    for c in range(3):
        for z1 in range(4):
            z = OWN + 2 * z1
            pair_ref[0] = jnp.minimum(
                weight_ref[c, z, :, pl.ds(0, 128)], weight_ref[c, z + 1, :, pl.ds(0, 128)]
            )
            least = jnp.minimum(pair_ref[0, pl.ds(4, 16, 2), :], pair_ref[0, pl.ds(5, 16, 2), :])
            rows_ref[pl.ds(32 * (4 + c) + 16 * (z1 // 2), 16), pl.ds(128 * (z1 % 2), 128)] = least

    for z in range(1, PLANES - 1):
        for t in range(5):
            rows = pl.ds(8 * t, 8)
            s = s_ref[z, rows, :] + s_ref[z - 1, rows, :]
            for part in range(2):
                r_ref[0, z % 6, part, rows, :] = s[:, 128 * part: 128 * part + 128]
        for t in range(5):
            rows = pl.ds(8 * t, 8)
            s = s_ref[z, rows, :] + s_ref[z - 1, rows, :]
            before = [
                r_ref[0, z % 6, part, pl.ds(8 * t - 1, 8), :] if t else pltpu.roll(s[:, 128 * part: 128 * part + 128], 1, 0)
                for part in range(2)
            ]
            s = s + jnp.concatenate(before, 1)
            inverse = box_inverse(s + pltpu.roll(s, 1, 1), KDIAG)
            for c in range(3):
                weight_ref[c, z, rows, :] = weight_ref[c, z, rows, :] * inverse

    sweep = smoother(u_ref, load_ref, weight_ref)
    tiles = range(5)
    work = (y_ref, x_ref, hi_ref, q_ref, r_ref)
    for k in range(2):
        stencil(u_ref, s_ref, sweep, 3 - 2 * gz + k * gz, 10 - k, tiles, *work)

    def remain(z, t, forces):
        rows = pl.ds(8 * t, 8)
        here = pl.ds(0, 128)
        for c in range(3):
            rest = load_ref[c, z, rows, here] - forces[c][:, :128]
            rest_ref[c, z - OWN, rows, :] = jnp.where(weight_ref[c, z, rows, here] > 0, rest, 0.0)

    stencil(u_ref, s_ref, remain, OWN, 8, tiles, *work)

    for c in range(3):
        for z1 in range(4):
            pair_ref[0] = rest_ref[c, 2 * z1] + rest_ref[c, 2 * z1 + 1]
            total = pair_ref[0, pl.ds(4, 16, 2), :] + pair_ref[0, pl.ds(5, 16, 2), :]
            rows_ref[pl.ds(32 * c + 16 * (z1 // 2), 16), pl.ds(128 * (z1 % 2), 128)] = total
    for z1 in range(4):
        z = OWN + 2 * z1
        pair_ref[0] = s_ref[z, :, pl.ds(0, 128)] + s_ref[z + 1, :, pl.ds(0, 128)]
        total = pair_ref[0, pl.ds(4, 16, 2), :] + pair_ref[0, pl.ds(5, 16, 2), :]
        rows_ref[pl.ds(32 * 3 + 16 * (z1 // 2), 16), pl.ds(128 * (z1 % 2), 128)] = total
        box = []
        for k in range(2):
            here = pl.ds(128 * k, 128)
            pair_ref[k] = (s_ref[z - 2, :, here] + s_ref[z - 1, :, here]) + (
                s_ref[z, :, here] + s_ref[z + 1, :, here]
            )
            box.append(
                (pair_ref[k, pl.ds(2, 16, 2), :] + pair_ref[k, pl.ds(3, 16, 2), :])
                + (pair_ref[k, pl.ds(4, 16, 2), :] + pair_ref[k, pl.ds(5, 16, 2), :])
            )
        lane16 = lane_index((16, 128))
        back = jnp.where(lane16 < 2, pltpu.roll(box[1], 2, 1), pltpu.roll(box[0], 2, 1))
        rows_ref[pl.ds(32 * 7 + 16 * (z1 // 2), 16), pl.ds(128 * (z1 % 2), 128)] = box[0] + back

    source = lax.broadcasted_iota(jnp.int32, (256, 128), 0)
    target = lax.broadcasted_iota(jnp.int32, (256, 128), 1)
    join = jnp.where(source // 2 == target, 1.0, 0.0).astype(F32)
    level1 = jnp.dot(rows_ref[...], join, precision=lax.Precision.HIGHEST, preferred_element_type=F32)

    def part(k):
        return level1[32 * k: 32 * k + 32]

    inverse = box_inverse(part(7), 2.0 * KDIAG / 8)
    results = [part(0), part(1), part(2), part(3) * (2.0 / 8)]
    results += [jnp.where(part(4 + c) > 1.5, inverse, 0.0) for c in range(3)]
    for k in range(7):
        for pair in range(2):
            send_ref[k, pair] = results[k][16 * pair: 16 * pair + 16]
    away = OWN + 6 - 5 * gz
    for c in range(3):
        plane_ref[c] = u_ref[c, away]


def edge_rows1(gz_ref, own_ref, other_ref, full_ref, right_ref, left_ref):
    gz = gz_ref[0]
    for f in range(7):
        full_ref[f, pl.ds(2 * gz, 2)] = own_ref[f]
        full_ref[f, pl.ds(2 - 2 * gz, 2)] = other_ref[f]
    for f in range(7):
        for pair in range(4):
            k = 4 * f + pair
            right_ref[pl.ds(12 * k, 12)] = full_ref[f, pair, pl.ds(4, 12)]
            left_ref[pl.ds(12 * k, 12)] = full_ref[f, pair, pl.ds(0, 12)]


def edge_lanes1(gz_ref, full_ref, low_ref, high_ref, ext_ref, right_ref, left_ref):
    lane = lane_index((ROWS, 128))
    for f in range(7):
        right = left = None
        for pair in range(4):
            k = 4 * f + pair
            ext_ref[f, pair, pl.ds(0, 12)] = low_ref[pl.ds(12 * k, 12)]
            ext_ref[f, pair, pl.ds(12, 16)] = full_ref[f, pair]
            ext_ref[f, pair, pl.ds(28, 12)] = high_ref[pl.ds(12 * k, 12)]
            value = ext_ref[f, pair]
            moved = pltpu.roll(value, 16 * pair, 1) if pair else value
            place = (lane + (128 - 16 * pair)) % 64
            right = moved if right is None else jnp.where(place >= 52, moved, right)
            left = moved if left is None else jnp.where(place < 12, moved, left)
        right_ref[f] = right
        left_ref[f] = left


def coarse(gz_ref, ext_ref, low_ref, high_ref, old_ref, load_ref, weight_ref, s_ref, other_ref, out_ref,
           u1_ref, v1_ref, u2_ref, v2_ref, state_ref, rest_ref, rows_ref, pair_ref, *work):
    work, fine_work = work[:5], work[5:]
    gz = gz_ref[0]
    lane = lane_index((ROWS, 128))
    clear_work(*work)
    clear_work(*fine_work)
    clear(u2_ref, v2_ref)
    for f in range(7):
        for z in (0, 9):
            v1_ref[f, z] = jnp.zeros((ROWS, 128), F32)
    for f in range(7):
        low, high = low_ref[f], high_ref[f]
        for pair in range(4):
            value = ext_ref[f, pair]
            for half in range(2):
                own = value if half == 0 else pltpu.roll(value, 64, 1)
                turn = (64 - 16 * pair - 64 * half) % 128
                below = pltpu.roll(low, turn, 1) if turn else low
                above = pltpu.roll(high, turn, 1) if turn else high
                whole = jnp.where(
                    lane < 64, own, jnp.where(lane < 64 + EDGE1, above, jnp.where(lane >= 128 - EDGE1, below, 0.0))
                )
                v1_ref[f, 1 + 2 * pair + half] = whole
    for c in range(3):
        for z in range(10):
            u1_ref[c, z] = v1_ref[4 + c, z] * v1_ref[c, z]

    s1_ref = v1_ref.at[3]
    sweep1 = smoother(u1_ref, v1_ref, v1_ref.at[pl.ds(4, 3)])
    stencil(u1_ref, s1_ref, sweep1, 1, 8, range(5), *work)

    def remain(z, t, forces):
        rows = pl.ds(8 * t, 8)
        for c in range(3):
            rest = v1_ref[c, z, rows, :] - forces[c]
            rest_ref[c, z, rows, :] = jnp.where(v1_ref[4 + c, z, rows, :] > 0, rest, 0.0)

    stencil(u1_ref, s1_ref, remain, 1, 8, range(5), *work)

    for z2 in range(4):
        z = 1 + 2 * z2
        for c in range(3):
            rest_ref[c, z] = rest_ref[c, z] + rest_ref[c, z + 1]
            rows_ref[pl.ds(24 * (4 * c + z2), 20)] = rest_ref[c, z, pl.ds(0, 20, 2), :] + rest_ref[c, z, pl.ds(1, 20, 2), :]
            rest_ref[c, 9] = jnp.where((v1_ref[4 + c, z] > 0) & (v1_ref[4 + c, z + 1] > 0), 1.0, 0.0)
            rows_ref[pl.ds(24 * (16 + 4 * c + z2), 20)] = jnp.minimum(
                rest_ref[c, 9, pl.ds(0, 20, 2), :], rest_ref[c, 9, pl.ds(1, 20, 2), :]
            )
        rest_ref[0, 9] = v1_ref[3, z] + v1_ref[3, z + 1]
        rows_ref[pl.ds(24 * (12 + z2), 20)] = rest_ref[0, 9, pl.ds(0, 20, 2), :] + rest_ref[0, 9, pl.ds(1, 20, 2), :]
    for k in range(28):
        rows_ref[pl.ds(24 * k + 20, 4)] = jnp.zeros((4, 128), F32)
    source = lax.broadcasted_iota(jnp.int32, (128, 128), 0)
    target = lax.broadcasted_iota(jnp.int32, (128, 128), 1)
    used = (target < 40) | (target >= 120)
    fold = (source // 2 + jnp.where(target < 64, 0, 64) == target) & used
    join = jnp.where(fold, 1.0, 0.0).astype(F32)
    level2 = jnp.dot(rows_ref[...], join, precision=lax.Precision.HIGHEST, preferred_element_type=F32)

    def part(k, z2):
        return level2[24 * (4 * k + z2): 24 * (4 * k + z2) + 24]

    for z2 in range(4):
        for c in range(3):
            v2_ref[c, 1 + z2] = part(c, z2)
            v2_ref[4 + c, 1 + z2] = jnp.where(part(4 + c, z2) > 1.5, 1.0, 0.0)
        v2_ref[3, 1 + z2] = part(3, z2) * (4.0 / 2.0 / 8.0)
    for z in range(1, 5):
        for t in range(3):
            rows = pl.ds(8 * t, 8)
            s = v2_ref[3, z, rows, :] + v2_ref[3, z - 1, rows, :]
            if t:
                before = pl.ds(8 * t - 1, 8)
                back = v2_ref[3, z, before, :] + v2_ref[3, z - 1, before, :]
            else:
                back = pltpu.roll(s, 1, 0)
            s = s + back
            inverse = box_inverse(s + pltpu.roll(s, 1, 1), KDIAG)
            for c in range(3):
                weight = v2_ref[4 + c, z, rows, :] * inverse
                v2_ref[4 + c, z, rows, :] = weight
                u2_ref[c, z, rows, :] = weight * v2_ref[c, z, rows, :]

    sweep2 = smoother(u2_ref, v2_ref, v2_ref.at[pl.ds(4, 3)])

    def again(k, carry):
        stencil(u2_ref, v2_ref.at[3], sweep2, 1, 4, range(3), *work)
        return carry

    lax.fori_loop(0, COARSE - 1, again, 0)

    part_of = jnp.where(
        (source == jnp.where(target < 96, target // 2, target // 2 + 64)), 1.0, 0.0
    ).astype(F32)
    for c in range(3):
        for z2 in range(4):
            rows_ref[pl.ds(24 * (4 * c + z2), 24)] = u2_ref[c, 1 + z2]
    spread = jnp.dot(rows_ref[pl.ds(0, 288)], part_of, precision=lax.Precision.HIGHEST, preferred_element_type=F32)
    for c in range(3):
        for z2 in range(4):
            k = 24 * (4 * c + z2)
            value = spread[k: k + 24][:20]
            rest_ref[c, 9, pl.ds(0, 20, 2), :] = value
            rest_ref[c, 9, pl.ds(1, 20, 2), :] = value
            for z in (1 + 2 * z2, 2 + 2 * z2):
                u1_ref[c, z] = u1_ref[c, z] + jnp.where(v1_ref[4 + c, z] > 0, rest_ref[c, 9], 0.0)

    for k in range(2):
        stencil(u1_ref, s1_ref, sweep1, 1 + 2 * gz + k * gz, 6 - k, range(1, 4), *work)

    start = 4 * gz
    for c in range(3):
        for j in range(6):
            rows_ref[pl.ds(24 * (6 * c + j), 24)] = u1_ref[c, start + j, pl.ds(8, 24), :]
    target2 = lax.broadcasted_iota(jnp.int32, (128, 256), 1)
    source2 = lax.broadcasted_iota(jnp.int32, (128, 256), 0)
    copies = jnp.where(source2 == target2 // 2, 1.0, 0.0).astype(F32)
    fine = jnp.dot(rows_ref[pl.ds(0, 432)], copies, precision=lax.Precision.HIGHEST, preferred_element_type=F32)
    for c in range(3):
        for z in range(PLANES):
            state_ref[c, z] = old_ref[c, z]
        state_ref[c, 12 - 11 * gz] = other_ref[c]
        for j in range(6):
            k = 24 * (6 * c + j)
            value = fine[k: k + 24][2:22]
            for k in range(2):
                here = pl.ds(128 * k, 128)
                pair_ref[k, pl.ds(0, 20, 2), :] = value[:, 128 * k: 128 * k + 128]
                pair_ref[k, pl.ds(1, 20, 2), :] = value[:, 128 * k: 128 * k + 128]
                for half in range(2):
                    z = 1 + 2 * j + half
                    state_ref[c, z, :, here] = state_ref[c, z, :, here] + jnp.where(
                        weight_ref[c, z, :, here] > 0, pair_ref[k], 0.0
                    )

    sweep = smoother(state_ref, load_ref, weight_ref)
    for k in range(2):
        stencil(state_ref, s_ref, sweep, 3 - gz + k * gz, 9 - k, range(5), *fine_work)
    for c in range(3):
        for z in range(8):
            out_ref[c, z] = state_ref[c, OWN + z, pl.ds(4, 32), pl.ds(0, 128)]


def up(value, axis):
    return lax.ppermute(value, axis, [(i, i + 1) for i in range(lax.axis_size(axis) - 1)])


def down(value, axis):
    return lax.ppermute(value, axis, [(i + 1, i) for i in range(lax.axis_size(axis) - 1)])


def swap(value):
    return lax.ppermute(value, "gz", [(0, 1), (1, 0)])


def scratch_of(rows, width, planes):
    parts = width // 128
    return [
        pltpu.VMEM((planes + 2, 6, parts, rows + 8, 128), F32),
        pltpu.VMEM((12, parts, rows, 128), F32),
        pltpu.VMEM((12, parts, rows, 128), F32),
        pltpu.VMEM((6, parts, rows + 8, 128), F32),
        pltpu.VMEM((planes + 1, 6, parts, rows, 128), F32),
    ]


def on_device(displacement, load, density_code, fixed_mask):
    gz = lax.axis_index("gz").astype(jnp.int32).reshape(1)
    inputs = [gz, displacement, load, density_code, fixed_mask]
    (zsend,) = call(
        boundary,
        [(24, 32, 128)],
        inputs,
        [
            pltpu.VMEM((3, 3, 32, 128), F32),
            pltpu.VMEM((3, 2, 32, 128), F32),
            pltpu.VMEM((3, 32, 128), jnp.int32),
            pltpu.VMEM((3, 3, 32, 128), jnp.int32),
            pltpu.SemaphoreType.DMA((4,)),
        ],
        inputs="any",
    )
    zrecv = swap(zsend)
    base, right, left = call(prepare, [(10, 8, 32, 128), (320, 128), (320, 128)], inputs, inputs="plain")
    low, high = up(right, "gx"), down(left, "gx")
    (zsend,) = call(boundary_rows, [(192, 128)], [gz, low, high])
    beside = swap(zsend)
    ext, ysend = call(
        edge_lanes, [(10, PLANES, ROWS, 128), (7, ROWS, 128)], [gz, base, zrecv, low, high, beside]
    )
    low, high = up(ysend, "gy"), down(ysend, "gy")
    wide = (3, PLANES, ROWS, LANES)
    u, loads, weights, scales, send1, plane = call(
        fine_down,
        [wide, wide, wide, (PLANES, ROWS, LANES), (7, 2, 16, 128), (3, ROWS, LANES)],
        [gz, ext, low, high],
        scratch_of(ROWS, LANES, 10)
        + [pltpu.VMEM((3, 8, ROWS, 128), F32), pltpu.VMEM((2, ROWS, 128), F32), pltpu.VMEM((256, 256), F32)],
    )
    other1 = swap(send1)
    other_plane = swap(plane)
    full, right, left = call(edge_rows1, [(7, 4, 16, 128), (336, 128), (336, 128)], [gz, send1, other1])
    low, high = up(right, "gx"), down(left, "gx")
    full, low, high, other_plane = lax.optimization_barrier((full, low, high, other_plane))
    ext1, right, left = call(
        edge_lanes1, [(7, 4, ROWS, 128), (7, ROWS, 128), (7, ROWS, 128)], [gz, full, low, high]
    )
    low, high = up(right, "gy"), down(left, "gy")
    (out,) = call(
        coarse,
        [(3, 8, 32, 128)],
        [gz, ext1, low, high, u, loads, weights, scales, other_plane],
        [
            pltpu.VMEM((3, 10, ROWS, 128), F32),
            pltpu.VMEM((7, 10, ROWS, 128), F32),
            pltpu.VMEM((3, 6, 24, 128), F32),
            pltpu.VMEM((7, 6, 24, 128), F32),
            pltpu.VMEM(wide, F32),
            pltpu.VMEM((3, 10, ROWS, 128), F32),
            pltpu.VMEM((672, 128), F32),
            pltpu.VMEM((2, ROWS, 128), F32),
        ]
        + scratch_of(ROWS, 128, 8)
        + scratch_of(ROWS, LANES, 9),
        output="plain",
    )
    return out


def solution(mesh):
    return jax.shard_map(
        on_device,
        mesh=mesh,
        in_specs=(
            P(None, "gz", "gx", "gy"),
            P(None, "gz", "gx", "gy"),
            P("gz", "gx", "gy"),
            P(None, "gz", "gx", "gy"),
        ),
        out_specs=P(None, "gz", "gx", "gy"),
        check_vma=False,
    )
```

time: 122 us -> 99.8 us (0.82)
  the two profiles are of different devices: /device:TPU:102 before, /device:TPU:113 now
where the time goes in v2:
time: 99.8 us; the launch traced here: 99.3 us
  starting transfers between devices  42.5 us (43%)
  Pallas kernels  29.5 us (30%)
  waiting for transfers between devices  23.2 us (23%)
  local copies, waits for them, and re-layouts  3.89 us (4%)
    pallas_call x8, Pallas kernels, call(): pl.pallas_call(body, out_shape=tuple((shape(out, F32) for out in outs)),...  29.5 us
    ppermute x4, starting transfers between devices, up(): lax.ppermute(value, axis, [(i, i + 1) for i in range(lax.axis_size(axis)...  20 us
    ppermute x4, waiting for transfers between devices, down(): lax.ppermute(value, axis, [(i + 1, i) for i in range(lax.axis_size(axis)...  12.6 us
    ppermute x4, starting transfers between devices, down(): lax.ppermute(value, axis, [(i + 1, i) for i in range(lax.axis_size(axis)...  11.9 us
    ppermute x4, starting transfers between devices, swap(): return lax.ppermute(value, 'gz', [(0, 1), (1, 0)])  10.6 us
    ppermute x4, waiting for transfers between devices, swap(): return lax.ppermute(value, 'gz', [(0, 1), (1, 0)])  8.79 us
    unnamed x8, local copies, waits for them, and re-layouts  3.89 us
  transfers between devices with their start and end apart: 12, of which 8 were waited for; matrix products, arithmetic and copies ran while one was open for 0% of the time, Pallas kernels for 0%

profile of v2, /device:TPU:113, one launch (start us, length us, event | category | flops | bytes accessed | tf_op | source)
XLA Modules:
  0.0 99.3 jit_solution(16458182516718510764)
XLA Ops:
  0.0 0.0 copy-start
  0.0 1.0 %copy-done = f32[3,8,32,128]{3,2,1,0:T(8,128)S(1)} copy-done((f32[3,8,32,128]{3,2,1,0:T(8,128)S(1)}, f32[3,8,32,128]{3,2,1,0:T(8,128)}, u32[]{:S(2)}) %copy-start) | copy-done | bytes 393240
  1.0 0.0 copy-start.1
  1.0 1.0 %copy-done.1 = f32[3,8,32,128]{3,2,1,0:T(8,128)S(1)} copy-done((f32[3,8,32,128]{3,2,1,0:T(8,128)S(1)}, f32[3,8,32,128]{3,2,1,0:T(8,128)}, u32[]{:S(2)}) %copy-start.1) | copy-done | bytes 393240
  2.0 0.0 copy-start.2
  2.0 1.0 %copy-done.2 = s32[3,8,32,128]{3,2,1,0:T(8,128)S(1)} copy-done((s32[3,8,32,128]{3,2,1,0:T(8,128)S(1)}, s32[3,8,32,128]{3,2,1,0:T(8,128)}, u32[]{:S(2)}) %copy-start.2) | copy-done | bytes 393240
  3.0 0.0 copy-start.3
  3.0 0.9 copy-done.3
  3.9 0.3 shard_map.47
  4.2 2.9 %collective-permute-start = (f32[24,32,128]{2,1,0:T(8,128)S(1)}, f32[24,32,128]{2,1,0:T(8,128)S(1)}, u32[]{:S(2)}, u32[]{:S(2)}) collective-permute-start(f32[24,32,128]{2,1,0:T(8,128)S(1)} %shard_map.47), channel_id=1, source_target_pairs={{0,1},{1,0},{2,3},{3,2},{4,5},{5,4},{6,7},{7,6},{8,9},{9,8},{10,11... | collective-permute-start | bytes 1179656 | tf_op jit(solution)/shard_map/ppermute | solution.py:567
  7.1 0.2 shard_map.46
  7.3 4.8 %collective-permute-start.1 = (f32[320,128]{1,0:T(8,128)S(1)}, f32[320,128]{1,0:T(8,128)S(1)}, u32[]{:S(2)}, u32[]{:S(2)}) collective-permute-start(f32[320,128]{1,0:T(8,128)S(1)} %get-tuple-element.27), channel_id=1, source_target_pairs={{0,32},{32,64},{64,96},{96,128},{128,160},{160,192},{192,224},{224... | collective-permute-start | bytes 491528 | tf_op jit(solution)/shard_map/ppermute | solution.py:559
  12.0 1.9 %collective-permute-start.2 = (f32[320,128]{1,0:T(8,128)S(1)}, f32[320,128]{1,0:T(8,128)S(1)}, u32[]{:S(2)}, u32[]{:S(2)}) collective-permute-start(f32[320,128]{1,0:T(8,128)S(1)} %get-tuple-element.28), channel_id=1, source_target_pairs={{32,0},{64,32},{96,64},{128,96},{160,128},{192,160},{224,192},{256... | collective-permute-start | bytes 491528 | tf_op jit(solution)/shard_map/ppermute | solution.py:563
  14.0 0.7 collective-permute-done.1.low_ref
  14.6 5.0 %collective-permute-done.2.high_ref = f32[320,128]{1,0:T(8,128)S(1)} collective-permute-done((f32[320,128]{1,0:T(8,128)S(1)}, f32[320,128]{1,0:T(8,128)S(1)}, u32[]{:S(2)}, u32[]{:S(2)}) %collective-permute-start.2) | collective-permute-done | bytes 163872 | tf_op jit(solution)/shard_map/ppermute | solution.py:563
  19.7 2.4 %collective-permute-start.3 = (f32[192,128]{1,0:T(8,128)S(1)}, f32[192,128]{1,0:T(8,128)S(1)}, u32[]{:S(2)}, u32[]{:S(2)}) collective-permute-start(f32[192,128]{1,0:T(8,128)S(1)} %shard_map.48), channel_id=1, source_target_pairs={{0,1},{1,0},{2,3},{3,2},{4,5},{5,4},{6,7},{7,6},{8,9},{9,8},{10,11... | collective-permute-start | bytes 294920 | tf_op jit(solution)/shard_map/ppermute | solution.py:567
  22.1 3.0 %collective-permute-done.3.beside_ref = f32[192,128]{1,0:T(8,128)S(1)} collective-permute-done((f32[192,128]{1,0:T(8,128)S(1)}, f32[192,128]{1,0:T(8,128)S(1)}, u32[]{:S(2)}, u32[]{:S(2)}) %collective-permute-start.3) | collective-permute-done | bytes 98336 | tf_op jit(solution)/shard_map/ppermute | solution.py:567
  25.0 0.0 collective-permute-done.zrecv_ref
  25.0 0.7 shard_map.49
  25.8 5.2 %collective-permute-start.5 = (f32[7,40,128]{2,1,0:T(8,128)S(1)}, f32[7,40,128]{2,1,0:T(8,128)S(1)}, u32[]{:S(2)}, u32[]{:S(2)}) collective-permute-start(f32[7,40,128]{2,1,0:T(8,128)S(1)} %get-tuple-element.30), channel_id=1, source_target_pairs={{2,0},{4,2},{6,4},{8,6},{10,8},{12,10},{14,12},{16,14},{18,16},{20... | collective-permute-start | bytes 430088 | tf_op jit(solution)/shard_map/ppermute | solution.py:563
  30.9 3.1 %collective-permute-start.4 = (f32[7,40,128]{2,1,0:T(8,128)S(1)}, f32[7,40,128]{2,1,0:T(8,128)S(1)}, u32[]{:S(2)}, u32[]{:S(2)}) collective-permute-start(f32[7,40,128]{2,1,0:T(8,128)S(1)} %get-tuple-element.30), channel_id=1, source_target_pairs={{0,2},{2,4},{4,6},{6,8},{8,10},{10,12},{12,14},{14,16},{16,18},{18... | collective-permute-start | bytes 430088 | tf_op jit(solution)/shard_map/ppermute | solution.py:559
  34.0 0.8 collective-permute-done.5.high_ref
  34.9 1.2 %collective-permute-done.4.low_ref = f32[7,40,128]{2,1,0:T(8,128)S(1)} collective-permute-done((f32[7,40,128]{2,1,0:T(8,128)S(1)}, f32[7,40,128]{2,1,0:T(8,128)S(1)}, u32[]{:S(2)}, u32[]{:S(2)}) %collective-permute-start.4) | collective-permute-done | bytes 143392 | tf_op jit(solution)/shard_map/ppermute | solution.py:559
  36.1 11.3 %shard_map.50 = (f32[3,14,40,256]{3,2,1,0:T(8,128)S(1)}, f32[3,14,40,256]{3,2,1,0:T(8,128)S(1)}, f32[3,14,40,256]{3,2,1,0:T(8,128)S(1)}, f32[14,40,256]{2,1,0:T(...) custom-call(s32[1]{0:T(128)} %bitcast.gz_ref, f32[10,14,40,128]{3,2,1,0:T(8,128)S(1)} %get-tuple-element.29.ext_ref, ...), custom_call_target="tpu_custom_call" | custom-call | tf_op jit(solution)/shard_map/pallas_call | solution.py:176
  47.4 2.7 %collective-permute-start.6 = (f32[7,2,16,128]{3,2,1,0:T(8,128)S(1)}, f32[7,2,16,128]{3,2,1,0:T(8,128)S(1)}, u32[]{:S(2)}, u32[]{:S(2)}) collective-permute-start(f32[7,2,16,128]{3,2,1,0:T(8,128)S(1)} %get-tuple-element.31.own_ref), channel_id=1, source_target_pairs={{0,1},{1,0},{2,3},{3,2},{4,5},{5,4},{6,7},{7,6},{8,9},{9,8},{10,11... | collective-permute-start | bytes 344072 | tf_op jit(solution)/shard_map/ppermute | solution.py:567
  50.1 2.9 %collective-permute-done.6.other_ref = f32[7,2,16,128]{3,2,1,0:T(8,128)S(1)} collective-permute-done((f32[7,2,16,128]{3,2,1,0:T(8,128)S(1)}, f32[7,2,16,128]{3,2,1,0:T(8,128)S(1)}, u32[]{:S(2)}, u32[]{:S(2)}) %collective-permute-start.6) | collective-permute-done | bytes 114720 | tf_op jit(solution)/shard_map/ppermute | solution.py:567
  53.0 2.5 %collective-permute-start.7 = (f32[336,128]{1,0:T(8,128)S(1)}, f32[336,128]{1,0:T(8,128)S(1)}, u32[]{:S(2)}, u32[]{:S(2)}) collective-permute-start(f32[336,128]{1,0:T(8,128)S(1)} %get-tuple-element.33), channel_id=1, source_target_pairs={{0,32},{32,64},{64,96},{96,128},{128,160},{160,192},{192,224},{224... | collective-permute-start | bytes 516104 | tf_op jit(solution)/shard_map/ppermute | solution.py:559
  55.5 2.8 %collective-permute-start.8 = (f32[336,128]{1,0:T(8,128)S(1)}, f32[336,128]{1,0:T(8,128)S(1)}, u32[]{:S(2)}, u32[]{:S(2)}) collective-permute-start(f32[336,128]{1,0:T(8,128)S(1)} %get-tuple-element.34), channel_id=1, source_target_pairs={{32,0},{64,32},{96,64},{128,96},{160,128},{192,160},{224,192},{256... | collective-permute-start | bytes 516104 | tf_op jit(solution)/shard_map/ppermute | solution.py:563
  58.3 2.7 %collective-permute-start.9 = (f32[3,40,256]{2,1,0:T(8,128)S(1)}, f32[3,40,256]{2,1,0:T(8,128)S(1)}, u32[]{:S(2)}, u32[]{:S(2)}) collective-permute-start(f32[3,40,256]{2,1,0:T(8,128)S(1)} %get-tuple-element.35), channel_id=1, source_target_pairs={{0,1},{1,0},{2,3},{3,2},{4,5},{5,4},{6,7},{7,6},{8,9},{9,8},{10,11... | collective-permute-start | bytes 368648 | tf_op jit(solution)/shard_map/ppermute | solution.py:567
  61.0 2.9 %collective-permute-done.9.other_ref = f32[3,40,256]{2,1,0:T(8,128)S(1)} collective-permute-done((f32[3,40,256]{2,1,0:T(8,128)S(1)}, f32[3,40,256]{2,1,0:T(8,128)S(1)}, u32[]{:S(2)}, u32[]{:S(2)}) %collective-permute-start.9) | collective-permute-done | bytes 122912 | tf_op jit(solution)/shard_map/ppermute | solution.py:567
  63.9 0.0 collective-permute-done.7.low_ref
  63.9 0.0 collective-permute-done.8.high_ref
  63.9 0.2 shard_map.52
  64.1 9.6 %collective-permute-start.10 = (f32[7,40,128]{2,1,0:T(8,128)S(1)}, f32[7,40,128]{2,1,0:T(8,128)S(1)}, u32[]{:S(2)}, u32[]{:S(2)}) collective-permute-start(f32[7,40,128]{2,1,0:T(8,128)S(1)} %get-tuple-element.40), channel_id=1, source_target_pairs={{0,2},{2,4},{4,6},{6,8},{8,10},{10,12},{12,14},{14,16},{16,18},{18... | collective-permute-start | bytes 430088 | tf_op jit(solution)/shard_map/ppermute | solution.py:559
  73.8 2.1 %collective-permute-start.11 = (f32[7,40,128]{2,1,0:T(8,128)S(1)}, f32[7,40,128]{2,1,0:T(8,128)S(1)}, u32[]{:S(2)}, u32[]{:S(2)}) collective-permute-start(f32[7,40,128]{2,1,0:T(8,128)S(1)} %get-tuple-element.41), channel_id=1, source_target_pairs={{2,0},{4,2},{6,4},{8,6},{10,8},{12,10},{14,12},{16,14},{18,16},{20... | collective-permute-start | bytes 430088 | tf_op jit(solution)/shard_map/ppermute | solution.py:563
  75.9 0.0 collective-permute-done.10.low_ref
  75.9 6.7 %collective-permute-done.11.high_ref = f32[7,40,128]{2,1,0:T(8,128)S(1)} collective-permute-done((f32[7,40,128]{2,1,0:T(8,128)S(1)}, f32[7,40,128]{2,1,0:T(8,128)S(1)}, u32[]{:S(2)}, u32[]{:S(2)}) %collective-permute-start.11) | collective-permute-done | bytes 143392 | tf_op jit(solution)/shard_map/ppermute | solution.py:563
  82.6 16.7 %shard_map.53 = f32[3,8,32,128]{3,2,1,0:T(8,128)} custom-call(s32[1]{0:T(128)} %bitcast.gz_ref, f32[7,4,40,128]{3,2,1,0:T(8,128)S(1)} %get-tuple-element.39.ext_ref, f32[7,40,128]{2,1,0:T(8,128)S(1)} %collective-permute-done.10.low_ref, f32[7,40,128]{2,1,0:T(8,128)S(1)} %collective-permute-done.11.high_ref, ...), custom_call_target="tpu_custom_call" | custom-call | tf_op jit(solution)/shard_map/pallas_call | solution.py:176
  (2 shorter events, 0.1 us)
Async XLA Ops:
  0.0 1.0 %copy-start = (f32[3,8,32,128]{3,2,1,0:T(8,128)S(1)}, f32[3,8,32,128]{3,2,1,0:T(8,128)}, u32[]{:S(2)}) copy-start(f32[3,8,32,128]{3,2,1,0:T(8,128)} %disp_ref.3) | copy-start | bytes 1179652
  1.0 1.0 %copy-start.1 = (f32[3,8,32,128]{3,2,1,0:T(8,128)S(1)}, f32[3,8,32,128]{3,2,1,0:T(8,128)}, u32[]{:S(2)}) copy-start(f32[3,8,32,128]{3,2,1,0:T(8,128)} %load_ref.3) | copy-start | bytes 1179652
  2.0 1.0 %copy-start.2 = (s32[3,8,32,128]{3,2,1,0:T(8,128)S(1)}, s32[3,8,32,128]{3,2,1,0:T(8,128)}, u32[]{:S(2)}) copy-start(s32[3,8,32,128]{3,2,1,0:T(8,128)} %fixed_ref.3) | copy-start | bytes 1179652
  3.0 0.9 copy-start.3
  4.2 20.9 %collective-permute-start = (f32[24,32,128]{2,1,0:T(8,128)S(1)}, f32[24,32,128]{2,1,0:T(8,128)S(1)}, u32[]{:S(2)}, u32[]{:S(2)}) collective-permute-start(f32[24,32,128]{2,1,0:T(8,128)S(1)} %shard_map.47), channel_id=1, source_target_pairs={{0,1},{1,0},{2,3},{3,2},{4,5},{5,4},{6,7},{7,6},{8,9},{9,8},{10,11... | collective-permute-start | bytes 1179656 | tf_op jit(solution)/shard_map/ppermute | solution.py:567
  7.3 7.3 %collective-permute-start.1 = (f32[320,128]{1,0:T(8,128)S(1)}, f32[320,128]{1,0:T(8,128)S(1)}, u32[]{:S(2)}, u32[]{:S(2)}) collective-permute-start(f32[320,128]{1,0:T(8,128)S(1)} %get-tuple-element.27), channel_id=1, source_target_pairs={{0,32},{32,64},{64,96},{96,128},{128,160},{160,192},{192,224},{224... | collective-permute-start | bytes 491528 | tf_op jit(solution)/shard_map/ppermute | solution.py:559
  12.0 7.6 %collective-permute-start.2 = (f32[320,128]{1,0:T(8,128)S(1)}, f32[320,128]{1,0:T(8,128)S(1)}, u32[]{:S(2)}, u32[]{:S(2)}) collective-permute-start(f32[320,128]{1,0:T(8,128)S(1)} %get-tuple-element.28), channel_id=1, source_target_pairs={{32,0},{64,32},{96,64},{128,96},{160,128},{192,160},{224,192},{256... | collective-permute-start | bytes 491528 | tf_op jit(solution)/shard_map/ppermute | solution.py:563
  19.7 5.4 %collective-permute-start.3 = (f32[192,128]{1,0:T(8,128)S(1)}, f32[192,128]{1,0:T(8,128)S(1)}, u32[]{:S(2)}, u32[]{:S(2)}) collective-permute-start(f32[192,128]{1,0:T(8,128)S(1)} %shard_map.48), channel_id=1, source_target_pairs={{0,1},{1,0},{2,3},{3,2},{4,5},{5,4},{6,7},{7,6},{8,9},{9,8},{10,11... | collective-permute-start | bytes 294920 | tf_op jit(solution)/shard_map/ppermute | solution.py:567
  25.8 9.1 %collective-permute-start.5 = (f32[7,40,128]{2,1,0:T(8,128)S(1)}, f32[7,40,128]{2,1,0:T(8,128)S(1)}, u32[]{:S(2)}, u32[]{:S(2)}) collective-permute-start(f32[7,40,128]{2,1,0:T(8,128)S(1)} %get-tuple-element.30), channel_id=1, source_target_pairs={{2,0},{4,2},{6,4},{8,6},{10,8},{12,10},{14,12},{16,14},{18,16},{20... | collective-permute-start | bytes 430088 | tf_op jit(solution)/shard_map/ppermute | solution.py:563
  30.9 5.1 %collective-permute-start.4 = (f32[7,40,128]{2,1,0:T(8,128)S(1)}, f32[7,40,128]{2,1,0:T(8,128)S(1)}, u32[]{:S(2)}, u32[]{:S(2)}) collective-permute-start(f32[7,40,128]{2,1,0:T(8,128)S(1)} %get-tuple-element.30), channel_id=1, source_target_pairs={{0,2},{2,4},{4,6},{6,8},{8,10},{10,12},{12,14},{14,16},{16,18},{18... | collective-permute-start | bytes 430088 | tf_op jit(solution)/shard_map/ppermute | solution.py:559
  47.4 5.5 %collective-permute-start.6 = (f32[7,2,16,128]{3,2,1,0:T(8,128)S(1)}, f32[7,2,16,128]{3,2,1,0:T(8,128)S(1)}, u32[]{:S(2)}, u32[]{:S(2)}) collective-permute-start(f32[7,2,16,128]{3,2,1,0:T(8,128)S(1)} %get-tuple-element.31.own_ref), channel_id=1, source_target_pairs={{0,1},{1,0},{2,3},{3,2},{4,5},{5,4},{6,7},{7,6},{8,9},{9,8},{10,11... | collective-permute-start | bytes 344072 | tf_op jit(solution)/shard_map/ppermute | solution.py:567
  53.0 10.9 %collective-permute-start.7 = (f32[336,128]{1,0:T(8,128)S(1)}, f32[336,128]{1,0:T(8,128)S(1)}, u32[]{:S(2)}, u32[]{:S(2)}) collective-permute-start(f32[336,128]{1,0:T(8,128)S(1)} %get-tuple-element.33), channel_id=1, source_target_pairs={{0,32},{32,64},{64,96},{96,128},{128,160},{160,192},{192,224},{224... | collective-permute-start | bytes 516104 | tf_op jit(solution)/shard_map/ppermute | solution.py:559
  55.5 8.4 %collective-permute-start.8 = (f32[336,128]{1,0:T(8,128)S(1)}, f32[336,128]{1,0:T(8,128)S(1)}, u32[]{:S(2)}, u32[]{:S(2)}) collective-permute-start(f32[336,128]{1,0:T(8,128)S(1)} %get-tuple-element.34), channel_id=1, source_target_pairs={{32,0},{64,32},{96,64},{128,96},{160,128},{192,160},{224,192},{256... | collective-permute-start | bytes 516104 | tf_op jit(solution)/shard_map/ppermute | solution.py:563
  58.3 5.6 %collective-permute-start.9 = (f32[3,40,256]{2,1,0:T(8,128)S(1)}, f32[3,40,256]{2,1,0:T(8,128)S(1)}, u32[]{:S(2)}, u32[]{:S(2)}) collective-permute-start(f32[3,40,256]{2,1,0:T(8,128)S(1)} %get-tuple-element.35), channel_id=1, source_target_pairs={{0,1},{1,0},{2,3},{3,2},{4,5},{5,4},{6,7},{7,6},{8,9},{9,8},{10,11... | collective-permute-start | bytes 368648 | tf_op jit(solution)/shard_map/ppermute | solution.py:567
  64.1 11.8 %collective-permute-start.10 = (f32[7,40,128]{2,1,0:T(8,128)S(1)}, f32[7,40,128]{2,1,0:T(8,128)S(1)}, u32[]{:S(2)}, u32[]{:S(2)}) collective-permute-start(f32[7,40,128]{2,1,0:T(8,128)S(1)} %get-tuple-element.40), channel_id=1, source_target_pairs={{0,2},{2,4},{4,6},{6,8},{8,10},{10,12},{12,14},{14,16},{16,18},{18... | collective-permute-start | bytes 430088 | tf_op jit(solution)/shard_map/ppermute | solution.py:559
  73.8 8.8 %collective-permute-start.11 = (f32[7,40,128]{2,1,0:T(8,128)S(1)}, f32[7,40,128]{2,1,0:T(8,128)S(1)}, u32[]{:S(2)}, u32[]{:S(2)}) collective-permute-start(f32[7,40,128]{2,1,0:T(8,128)S(1)} %get-tuple-element.41), channel_id=1, source_target_pairs={{2,0},{4,2},{6,4},{8,6},{10,8},{12,10},{14,12},{16,14},{18,16},{20... | collective-permute-start | bytes 430088 | tf_op jit(solution)/shard_map/ppermute | solution.py:563

commit v3 on v2

--- a/solution.py
+++ b/solution.py
@@ -168,10 +168,9 @@
 
 def call(body, outs, args, scratch=(), inputs="vmem", output="vmem"):
     whole = pl.BlockSpec(memory_space=pltpu.VMEM)
-    rest = pl.BlockSpec(memory_space=pltpu.HBM) if inputs == "any" else whole
-    values = args[1:]
-    if inputs == "vmem":
-        values = [pltpu.with_memory_space_constraint(value, pltpu.VMEM) for value in values]
+    space = pltpu.VMEM if inputs == "vmem" else pltpu.HBM
+    rest = pl.BlockSpec(memory_space=space)
+    values = [pltpu.with_memory_space_constraint(value, space) for value in args[1:]]
     shape = pltpu.VMEM if output == "vmem" else jax.ShapeDtypeStruct
     return pl.pallas_call(
         body,
@@ -188,30 +187,22 @@
     return EMIN + (1.0 - EMIN) * level * level * level
 
 
-def boundary(gz_ref, disp_ref, load_ref, code_ref, fixed_ref, send_ref, disp, load, code, fixed, sems):
+def prepare(gz_ref, disp_hbm, load_hbm, code_hbm, fixed_hbm, send_ref, base_ref, right_ref, left_ref,
+            disp_ref, load_ref, code_ref, fixed_ref, sems):
     gz = gz_ref[0]
-    three, two = 5 * (1 - gz), 6 * (1 - gz)
-    copies = [
-        pltpu.make_async_copy(code_ref.at[pl.ds(three, 3)], code, sems.at[0]),
-        pltpu.make_async_copy(fixed_ref.at[:, pl.ds(three, 3)], fixed, sems.at[1]),
-        pltpu.make_async_copy(disp_ref.at[:, pl.ds(three, 3)], disp, sems.at[2]),
-        pltpu.make_async_copy(load_ref.at[:, pl.ds(two, 2)], load, sems.at[3]),
-    ]
+    copies = []
+    for half in range(2):
+        planes = pl.ds(4 * half, 4)
+        pairs = [(code_hbm.at[planes], code_ref.at[planes])]
+        for c in range(3):
+            for source, target in ((fixed_hbm, fixed_ref), (disp_hbm, disp_ref), (load_hbm, load_ref)):
+                pairs.append((source.at[c, planes], target.at[c, planes]))
+        for source, target in pairs:
+            copies.append(pltpu.make_async_copy(source, target, sems.at[len(copies)]))
     for copy in copies:
         copy.start()
     for copy in copies:
         copy.wait()
-    for j in range(3):
-        send_ref[21 + j] = scale_of(code[j])
-        for c in range(3):
-            send_ref[3 * c + j] = (1.0 - fixed[c, j].astype(F32)) * disp[c, j]
-    for c in range(3):
-        for j in range(2):
-            send_ref[9 + 2 * c + j] = load[c, j]
-            send_ref[15 + 2 * c + j] = 1.0 - fixed[c, j + 1 - gz].astype(F32)
-
-
-def prepare(gz_ref, disp_ref, load_ref, code_ref, fixed_ref, base_ref, right_ref, left_ref):
     for z in range(8):
         base_ref[9, z] = scale_of(code_ref[z])
         for c in range(3):
@@ -219,6 +210,15 @@
             base_ref[c, z] = free * disp_ref[c, z]
             base_ref[3 + c, z] = load_ref[c, z]
             base_ref[6 + c, z] = free
+    three, two = 5 * (1 - gz), 6 * (1 - gz)
+    for j in range(3):
+        send_ref[21 + j] = base_ref[9, three + j]
+        for c in range(3):
+            send_ref[3 * c + j] = base_ref[c, three + j]
+    for c in range(3):
+        for j in range(2):
+            send_ref[9 + 2 * c + j] = base_ref[3 + c, two + j]
+            send_ref[15 + 2 * c + j] = base_ref[6 + c, two + j]
     for k in range(80):
         right_ref[pl.ds(4 * k, 4)] = base_ref[k // 8, k % 8, pl.ds(28, 4)]
         left_ref[pl.ds(4 * k, 4)] = base_ref[k // 8, k % 8, pl.ds(0, 4)]
@@ -252,31 +252,33 @@
     return places
 
 
-def edge_lanes(gz_ref, base_ref, zrecv_ref, low_ref, high_ref, beside_ref, ext_ref, send_ref):
+def edge_lanes(gz_ref, base_ref, zrecv_ref, low_ref, high_ref, beside_ref, ext_ref, up_ref, down_ref):
     gz = gz_ref[0]
     blank = jnp.zeros((ROWS, 128), F32)
     for f in range(10):
         for z in list(range(OWN)) + list(range(OWN + 8, PLANES)):
             ext_ref[f, z] = blank
     lane = lane_index((ROWS, 128))
-    packed = None
+    rising = falling = None
     for k, (f, z) in enumerate(fine_places(gz)):
-        beside = 8 * (k - 80)
-        ext_ref[f, z, pl.ds(0, 4)] = low_ref[pl.ds(4 * k, 4)] if k < 80 else beside_ref[pl.ds(beside, 4)]
+        beside, other = 8 * (k - 80), 1 - gz
+        ext_ref[f, z, pl.ds(0, 4)] = low_ref[pl.ds(4 * k, 4)] if k < 80 else beside_ref[other, pl.ds(beside, 4)]
         ext_ref[f, z, pl.ds(4, 32)] = base_ref[k // 8, k % 8] if k < 80 else zrecv_ref[k - 80]
-        ext_ref[f, z, pl.ds(36, 4)] = high_ref[pl.ds(4 * k, 4)] if k < 80 else beside_ref[pl.ds(beside + 4, 4)]
-        group = k % 16
-        value = ext_ref[f, z]
+        ext_ref[f, z, pl.ds(36, 4)] = high_ref[pl.ds(4 * k, 4)] if k < 80 else beside_ref[other, pl.ds(beside + 4, 4)]
+        group = k % 32
+        moved = pltpu.roll(ext_ref[f, z], (4 * group + 4) % 128, 1)
         if group == 0:
-            packed = value
+            rising = falling = moved
         else:
-            packed = jnp.where((lane >= 8 * group - 4) & (lane < 8 * group + 4), pltpu.roll(value, 8 * group, 1), packed)
-        if group == 15 or k == 103:
-            send_ref[k // 16] = packed
+            rising = jnp.where(lane // 4 == group, moved, rising)
+            falling = jnp.where(lane // 4 == (group + 1) % 32, moved, falling)
+        if group == 31 or k == 103:
+            up_ref[k // 32] = rising
+            down_ref[k // 32] = falling
 
 
 def fine_down(gz_ref, ext_ref, low_ref, high_ref,
-              u_ref, load_ref, weight_ref, s_ref, send_ref, plane_ref,
+              u_ref, load_ref, weight_ref, s_ref, send_ref,
               y_ref, x_ref, hi_ref, q_ref, r_ref, rest_ref, pair_ref, rows_ref):
     gz = gz_ref[0]
     blank = jnp.zeros((ROWS, 128), F32)
@@ -287,12 +289,13 @@
         for z in list(range(OWN)) + list(range(OWN + 8, PLANES)):
             fields[f][z, :, pl.ds(128, 128)] = blank
     lane = lane_index((ROWS, 128))
-    merged = None
+    merged = [None, None]
     for k, (f, z) in enumerate(fine_places(gz)):
-        group = k % 16
+        group = k % 32
         if group == 0:
-            merged = jnp.where(lane % 8 < 4, high_ref[k // 16], low_ref[k // 16])
-        value = merged if group == 0 else pltpu.roll(merged, 128 - 8 * group, 1)
+            for odd in range(2):
+                merged[odd] = jnp.where(lane // 4 % 2 == odd, low_ref[k // 32], high_ref[k // 32])
+        value = pltpu.roll(merged[group % 2], 124 - 4 * group, 1) if group < 31 else merged[1]
         fields[f][z, :, pl.ds(128, 128)] = jnp.where((lane < EDGE) | (lane >= 128 - EDGE), value, 0.0)
     clear_work(y_ref, x_ref, hi_ref, q_ref, r_ref)
 
@@ -374,18 +377,26 @@
     results = [part(0), part(1), part(2), part(3) * (2.0 / 8)]
     results += [jnp.where(part(4 + c) > 1.5, inverse, 0.0) for c in range(3)]
     for k in range(7):
-        for pair in range(2):
-            send_ref[k, pair] = results[k][16 * pair: 16 * pair + 16]
+        for i in range(4):
+            send_ref[4 * k + i] = results[k][8 * i: 8 * i + 8]
     away = OWN + 6 - 5 * gz
-    for c in range(3):
-        plane_ref[c] = u_ref[c, away]
-
-
-def edge_rows1(gz_ref, own_ref, other_ref, full_ref, right_ref, left_ref):
-    gz = gz_ref[0]
+    lane8 = lane_index((8, 128))
+    for t in range(5):
+        rows = pl.ds(8 * t, 8)
+        edges = u_ref[0, away, rows, pl.ds(128, 128)]
+        for c in range(3):
+            send_ref[28 + 5 * c + t] = u_ref[c, away, rows, pl.ds(0, 128)]
+            if c:
+                moved = pltpu.roll(u_ref[c, away, rows, pl.ds(128, 128)], 8 * c, 1)
+                edges = jnp.where((lane8 >= 8 * c - 4) & (lane8 < 8 * c + 4), moved, edges)
+        send_ref[43 + t] = edges
+
+
+def edge_rows1(gz_ref, both_ref, full_ref, right_ref, left_ref):
     for f in range(7):
-        full_ref[f, pl.ds(2 * gz, 2)] = own_ref[f]
-        full_ref[f, pl.ds(2 - 2 * gz, 2)] = other_ref[f]
+        for pair in range(4):
+            for i in range(2):
+                full_ref[f, pair, pl.ds(8 * i, 8)] = both_ref[pair // 2, 4 * f + 2 * (pair % 2) + i]
     for f in range(7):
         for pair in range(4):
             k = 4 * f + pair
@@ -411,7 +422,7 @@
         left_ref[f] = left
 
 
-def coarse(gz_ref, ext_ref, low_ref, high_ref, old_ref, load_ref, weight_ref, s_ref, other_ref, out_ref,
+def coarse(gz_ref, ext_ref, low_ref, high_ref, old_ref, load_ref, weight_ref, s_ref, both_ref, out_ref,
            u1_ref, v1_ref, u2_ref, v2_ref, state_ref, rest_ref, rows_ref, pair_ref, *work):
     work, fine_work = work[:5], work[5:]
     gz = gz_ref[0]
@@ -523,6 +534,7 @@
         stencil(u1_ref, s1_ref, sweep1, 1 + 2 * gz + k * gz, 6 - k, range(1, 4), *work)
 
     start = 4 * gz
+    lane8 = lane_index((8, 128))
     for c in range(3):
         for j in range(6):
             rows_ref[pl.ds(24 * (6 * c + j), 24)] = u1_ref[c, start + j, pl.ds(8, 24), :]
@@ -531,9 +543,14 @@
     copies = jnp.where(source2 == target2 // 2, 1.0, 0.0).astype(F32)
     fine = jnp.dot(rows_ref[pl.ds(0, 432)], copies, precision=lax.Precision.HIGHEST, preferred_element_type=F32)
     for c in range(3):
-        for z in range(PLANES):
+        for z in range(1, PLANES - 1):
             state_ref[c, z] = old_ref[c, z]
-        state_ref[c, 12 - 11 * gz] = other_ref[c]
+        for t in range(5):
+            edges = both_ref[1 - gz, 43 + t]
+            edges = pltpu.roll(edges, 128 - 8 * c, 1) if c else edges
+            edges = jnp.where((lane8 < 4) | (lane8 >= 124), edges, 0.0)
+            state_ref[c, 12 - 11 * gz, pl.ds(8 * t, 8), pl.ds(0, 128)] = both_ref[1 - gz, 28 + 5 * c + t]
+            state_ref[c, 12 - 11 * gz, pl.ds(8 * t, 8), pl.ds(128, 128)] = edges
         for j in range(6):
             k = 24 * (6 * c + j)
             value = fine[k: k + 24][2:22]
@@ -580,42 +597,41 @@
 
 def on_device(displacement, load, density_code, fixed_mask):
     gz = lax.axis_index("gz").astype(jnp.int32).reshape(1)
-    inputs = [gz, displacement, load, density_code, fixed_mask]
-    (zsend,) = call(
-        boundary,
-        [(24, 32, 128)],
-        inputs,
+    block = (3, 8, 32, 128)
+    zsend, base, right, left = call(
+        prepare,
+        [(24, 32, 128), (10, 8, 32, 128), (320, 128), (320, 128)],
+        [gz, displacement, load, density_code, fixed_mask],
         [
-            pltpu.VMEM((3, 3, 32, 128), F32),
-            pltpu.VMEM((3, 2, 32, 128), F32),
-            pltpu.VMEM((3, 32, 128), jnp.int32),
-            pltpu.VMEM((3, 3, 32, 128), jnp.int32),
-            pltpu.SemaphoreType.DMA((4,)),
+            pltpu.VMEM(block, F32),
+            pltpu.VMEM(block, F32),
+            pltpu.VMEM(block[1:], jnp.int32),
+            pltpu.VMEM(block, jnp.int32),
+            pltpu.SemaphoreType.DMA((20,)),
         ],
-        inputs="any",
+        inputs="hbm",
     )
     zrecv = swap(zsend)
-    base, right, left = call(prepare, [(10, 8, 32, 128), (320, 128), (320, 128)], inputs, inputs="plain")
     low, high = up(right, "gx"), down(left, "gx")
     (zsend,) = call(boundary_rows, [(192, 128)], [gz, low, high])
-    beside = swap(zsend)
-    ext, ysend = call(
-        edge_lanes, [(10, PLANES, ROWS, 128), (7, ROWS, 128)], [gz, base, zrecv, low, high, beside]
+    beside = lax.all_gather(zsend, "gz")
+    ext, rising, falling = call(
+        edge_lanes,
+        [(10, PLANES, ROWS, 128), (4, ROWS, 128), (4, ROWS, 128)],
+        [gz, base, zrecv, low, high, beside],
     )
-    low, high = up(ysend, "gy"), down(ysend, "gy")
+    low, high = up(rising, "gy"), down(falling, "gy")
     wide = (3, PLANES, ROWS, LANES)
-    u, loads, weights, scales, send1, plane = call(
+    u, loads, weights, scales, send1 = call(
         fine_down,
-        [wide, wide, wide, (PLANES, ROWS, LANES), (7, 2, 16, 128), (3, ROWS, LANES)],
+        [wide, wide, wide, (PLANES, ROWS, LANES), (48, 8, 128)],
         [gz, ext, low, high],
         scratch_of(ROWS, LANES, 10)
         + [pltpu.VMEM((3, 8, ROWS, 128), F32), pltpu.VMEM((2, ROWS, 128), F32), pltpu.VMEM((256, 256), F32)],
     )
-    other1 = swap(send1)
-    other_plane = swap(plane)
-    full, right, left = call(edge_rows1, [(7, 4, 16, 128), (336, 128), (336, 128)], [gz, send1, other1])
+    both = lax.all_gather(send1, "gz")
+    full, right, left = call(edge_rows1, [(7, 4, 16, 128), (336, 128), (336, 128)], [gz, both])
     low, high = up(right, "gx"), down(left, "gx")
-    full, low, high, other_plane = lax.optimization_barrier((full, low, high, other_plane))
     ext1, right, left = call(
         edge_lanes1, [(7, 4, ROWS, 128), (7, ROWS, 128), (7, ROWS, 128)], [gz, full, low, high]
     )
@@ -623,7 +639,7 @@
     (out,) = call(
         coarse,
         [(3, 8, 32, 128)],
-        [gz, ext1, low, high, u, loads, weights, scales, other_plane],
+        [gz, ext1, low, high, u, loads, weights, scales, both],
         [
             pltpu.VMEM((3, 10, ROWS, 128), F32),
             pltpu.VMEM((7, 10, ROWS, 128), F32),

time: 99.8 us -> 96 us (0.962)
  the two profiles are of different devices: /device:TPU:113 before, /device:TPU:115 now
where the time goes in v3:
time: 96 us; the launch traced here: 95.6 us
  Pallas kernels  30.7 us (32%)
  starting transfers between devices  30 us (31%)
  waiting for transfers between devices  24.9 us (26%)
  blocking collectives  9.77 us (10%)
    pallas_call x7, Pallas kernels, call(): pl.pallas_call(body, out_shape=tuple((shape(out, F32) for out in outs)),...  30.7 us
    ppermute x4, waiting for transfers between devices, down(): lax.ppermute(value, axis, [(i + 1, i) for i in range(lax.axis_size(axis)...  22 us
    ppermute x4, starting transfers between devices, up(): lax.ppermute(value, axis, [(i, i + 1) for i in range(lax.axis_size(axis)...  18.4 us
    ppermute x4, starting transfers between devices, down(): lax.ppermute(value, axis, [(i + 1, i) for i in range(lax.axis_size(axis)...  8.71 us
    all_gather x1, blocking collectives, on_device(): both = lax.all_gather(send1, 'gz')  5.63 us
    all_gather x1, blocking collectives, on_device(): beside = lax.all_gather(zsend, 'gz')  4.13 us
    ppermute x1, starting transfers between devices, swap(): return lax.ppermute(value, 'gz', [(0, 1), (1, 0)])  2.91 us
    ppermute x4, waiting for transfers between devices, up(): lax.ppermute(value, axis, [(i, i + 1) for i in range(lax.axis_size(axis)...  2.84 us
  transfers between devices with their start and end apart: 9, of which 6 were waited for; matrix products, arithmetic and copies ran while one was open for 0% of the time, Pallas kernels for 0%

profile of v3, /device:TPU:115, one launch (start us, length us, event | category | flops | bytes accessed | tf_op | source)
XLA Modules:
  0.0 95.6 jit_solution(7831507189596194780)
XLA Ops:
  0.0 1.7 %shard_map.46 = (f32[24,32,128]{2,1,0:T(8,128)S(1)}, f32[10,8,32,128]{3,2,1,0:T(8,128)S(1)}, f32[320,128]{1,0:T(8,128)S(1)}, f32[320,128]{1,0:T(8,128)S(1)}) custom-call(s32[1]{0:T(128)} %bitcast.gz_ref, f32[3,8,32,128]{3,2,1,0:T(8,128)} %disp_hbm.1, f32[3,8,32,128]{3,2,1,0:T(8,128)} %load_hbm.1, s32[8,32,128]{2,1,0:T(8,128)} %code_hbm.1, ...), custom_call_target="tpu_custom_call" | custom-call | tf_op jit(solution)/shard_map/pallas_call | solution.py:175
  1.7 2.9 %collective-permute-start = (f32[24,32,128]{2,1,0:T(8,128)S(1)}, f32[24,32,128]{2,1,0:T(8,128)S(1)}, u32[]{:S(2)}, u32[]{:S(2)}) collective-permute-start(f32[24,32,128]{2,1,0:T(8,128)S(1)} %get-tuple-element.24), channel_id=1, source_target_pairs={{0,1},{1,0},{2,3},{3,2},{4,5},{5,4},{6,7},{7,6},{8,9},{9,8},{10,11... | collective-permute-start | bytes 1179656 | tf_op jit(solution)/shard_map/ppermute | solution.py:584
  4.6 4.8 %collective-permute-start.1 = (f32[320,128]{1,0:T(8,128)S(1)}, f32[320,128]{1,0:T(8,128)S(1)}, u32[]{:S(2)}, u32[]{:S(2)}) collective-permute-start(f32[320,128]{1,0:T(8,128)S(1)} %get-tuple-element.25), channel_id=1, source_target_pairs={{0,32},{32,64},{64,96},{96,128},{128,160},{160,192},{192,224},{224... | collective-permute-start | bytes 491528 | tf_op jit(solution)/shard_map/ppermute | solution.py:576
  9.4 1.9 %collective-permute-start.2 = (f32[320,128]{1,0:T(8,128)S(1)}, f32[320,128]{1,0:T(8,128)S(1)}, u32[]{:S(2)}, u32[]{:S(2)}) collective-permute-start(f32[320,128]{1,0:T(8,128)S(1)} %get-tuple-element.26), channel_id=1, source_target_pairs={{32,0},{64,32},{96,64},{128,96},{160,128},{192,160},{224,192},{256... | collective-permute-start | bytes 491528 | tf_op jit(solution)/shard_map/ppermute | solution.py:580
  11.3 0.7 collective-permute-done.1.low_ref
  11.9 5.0 %collective-permute-done.2.high_ref = f32[320,128]{1,0:T(8,128)S(1)} collective-permute-done((f32[320,128]{1,0:T(8,128)S(1)}, f32[320,128]{1,0:T(8,128)S(1)}, u32[]{:S(2)}, u32[]{:S(2)}) %collective-permute-start.2) | collective-permute-done | bytes 163872 | tf_op jit(solution)/shard_map/ppermute | solution.py:580
  17.0 4.1 %all-gather = f32[384,128]{1,0:T(8,128)S(1)} all-gather(f32[192,128]{1,0:T(8,128)S(1)} %shard_map.47), channel_id=2, replica_groups=mesh['gx'=16,'gy'=16,'gz'=2] {'gz'}, dimensions={0}, use_global_device_ids=true | all-gather | bytes 294912 | tf_op jit(solution)/shard_map/all_gather | solution.py:617
  21.1 0.0 collective-permute-done.zrecv_ref
  21.1 0.8 shard_map.48
  22.0 6.3 %collective-permute-start.3 = (f32[4,40,128]{2,1,0:T(8,128)S(1)}, f32[4,40,128]{2,1,0:T(8,128)S(1)}, u32[]{:S(2)}, u32[]{:S(2)}) collective-permute-start(f32[4,40,128]{2,1,0:T(8,128)S(1)} %get-tuple-element.28), channel_id=1, source_target_pairs={{0,2},{2,4},{4,6},{6,8},{8,10},{10,12},{12,14},{14,16},{16,18},{18... | collective-permute-start | bytes 245768 | tf_op jit(solution)/shard_map/ppermute | solution.py:576
  28.3 1.9 %collective-permute-start.4 = (f32[4,40,128]{2,1,0:T(8,128)S(1)}, f32[4,40,128]{2,1,0:T(8,128)S(1)}, u32[]{:S(2)}, u32[]{:S(2)}) collective-permute-start(f32[4,40,128]{2,1,0:T(8,128)S(1)} %get-tuple-element.29), channel_id=1, source_target_pairs={{2,0},{4,2},{6,4},{8,6},{10,8},{12,10},{14,12},{16,14},{18,16},{20... | collective-permute-start | bytes 245768 | tf_op jit(solution)/shard_map/ppermute | solution.py:580
  30.2 0.0 collective-permute-done.3.low_ref
  30.2 6.2 %collective-permute-done.4.high_ref = f32[4,40,128]{2,1,0:T(8,128)S(1)} collective-permute-done((f32[4,40,128]{2,1,0:T(8,128)S(1)}, f32[4,40,128]{2,1,0:T(8,128)S(1)}, u32[]{:S(2)}, u32[]{:S(2)}) %collective-permute-start.4) | collective-permute-done | bytes 81952 | tf_op jit(solution)/shard_map/ppermute | solution.py:580
  36.5 11.3 %shard_map.49 = (f32[3,14,40,256]{3,2,1,0:T(8,128)S(1)}, f32[3,14,40,256]{3,2,1,0:T(8,128)S(1)}, f32[3,14,40,256]{3,2,1,0:T(8,128)S(1)}, f32[14,40,256]{2,1,0:T(8,128)S(1)}, f32[48,8,128]{2,1,0:T(8,128)S(1)}) custom-call(s32[1]{0:T(128)} %bitcast.gz_ref, f32[10,14,40,128]{3,2,1,0:T(8,128)S(1)} %get-tuple-element.27.ext_ref, ...), custom_call_target="tpu_custom_call" | custom-call | tf_op jit(solution)/shard_map/pallas_call | solution.py:175
  47.8 5.6 %all-gather.1 = f32[96,8,128]{2,1,0:T(8,128)S(1)} all-gather(f32[48,8,128]{2,1,0:T(8,128)S(1)} %get-tuple-element.30), channel_id=3, replica_groups=mesh['gx'=16,'gy'=16,'gz'=2] {'gz'}, dimensions={0}, use_global_device_ids=true | all-gather | bytes 589824 | tf_op jit(solution)/shard_map/all_gather | solution.py:632
  53.5 2.5 %collective-permute-start.5 = (f32[336,128]{1,0:T(8,128)S(1)}, f32[336,128]{1,0:T(8,128)S(1)}, u32[]{:S(2)}, u32[]{:S(2)}) collective-permute-start(f32[336,128]{1,0:T(8,128)S(1)} %get-tuple-element.32), channel_id=1, source_target_pairs={{0,32},{32,64},{64,96},{96,128},{128,160},{160,192},{192,224},{224... | collective-permute-start | bytes 516104 | tf_op jit(solution)/shard_map/ppermute | solution.py:576
  56.0 2.8 %collective-permute-start.6 = (f32[336,128]{1,0:T(8,128)S(1)}, f32[336,128]{1,0:T(8,128)S(1)}, u32[]{:S(2)}, u32[]{:S(2)}) collective-permute-start(f32[336,128]{1,0:T(8,128)S(1)} %get-tuple-element.33), channel_id=1, source_target_pairs={{32,0},{64,32},{96,64},{128,96},{160,128},{192,160},{224,192},{256... | collective-permute-start | bytes 516104 | tf_op jit(solution)/shard_map/ppermute | solution.py:580
  58.8 2.2 %collective-permute-done.5.low_ref = f32[336,128]{1,0:T(8,128)S(1)} collective-permute-done((f32[336,128]{1,0:T(8,128)S(1)}, f32[336,128]{1,0:T(8,128)S(1)}, u32[]{:S(2)}, u32[]{:S(2)}) %collective-permute-start.5) | collective-permute-done | bytes 172064 | tf_op jit(solution)/shard_map/ppermute | solution.py:576
  60.9 4.1 %collective-permute-done.6.high_ref = f32[336,128]{1,0:T(8,128)S(1)} collective-permute-done((f32[336,128]{1,0:T(8,128)S(1)}, f32[336,128]{1,0:T(8,128)S(1)}, u32[]{:S(2)}, u32[]{:S(2)}) %collective-permute-start.6) | collective-permute-done | bytes 172064 | tf_op jit(solution)/shard_map/ppermute | solution.py:580
  65.0 0.2 shard_map.51
  65.2 4.8 %collective-permute-start.7 = (f32[7,40,128]{2,1,0:T(8,128)S(1)}, f32[7,40,128]{2,1,0:T(8,128)S(1)}, u32[]{:S(2)}, u32[]{:S(2)}) collective-permute-start(f32[7,40,128]{2,1,0:T(8,128)S(1)} %get-tuple-element.35), channel_id=1, source_target_pairs={{0,2},{2,4},{4,6},{6,8},{8,10},{10,12},{12,14},{14,16},{16,18},{18... | collective-permute-start | bytes 430088 | tf_op jit(solution)/shard_map/ppermute | solution.py:576
  70.1 2.1 %collective-permute-start.8 = (f32[7,40,128]{2,1,0:T(8,128)S(1)}, f32[7,40,128]{2,1,0:T(8,128)S(1)}, u32[]{:S(2)}, u32[]{:S(2)}) collective-permute-start(f32[7,40,128]{2,1,0:T(8,128)S(1)} %get-tuple-element.36), channel_id=1, source_target_pairs={{2,0},{4,2},{6,4},{8,6},{10,8},{12,10},{14,12},{16,14},{18,16},{20... | collective-permute-start | bytes 430088 | tf_op jit(solution)/shard_map/ppermute | solution.py:580
  72.2 0.0 collective-permute-done.7.low_ref
  72.2 6.7 %collective-permute-done.8.high_ref = f32[7,40,128]{2,1,0:T(8,128)S(1)} collective-permute-done((f32[7,40,128]{2,1,0:T(8,128)S(1)}, f32[7,40,128]{2,1,0:T(8,128)S(1)}, u32[]{:S(2)}, u32[]{:S(2)}) %collective-permute-start.8) | collective-permute-done | bytes 143392 | tf_op jit(solution)/shard_map/ppermute | solution.py:580
  78.9 16.7 %shard_map.52 = f32[3,8,32,128]{3,2,1,0:T(8,128)} custom-call(s32[1]{0:T(128)} %bitcast.gz_ref, f32[7,4,40,128]{3,2,1,0:T(8,128)S(1)} %get-tuple-element.34.ext_ref, f32[7,40,128]{2,1,0:T(8,128)S(1)} %collective-permute-done.7.low_ref, f32[7,40,128]{2,1,0:T(8,128)S(1)} %collective-permute-done.8.high_ref, f32[3,14,40,256]{3,2,1,0:T(8,128)S(1)} %get-tuple-element.37.old_ref, ...), custom_call_target="tpu_custom_call" | custom-call | tf_op jit(solution)/shard_map/pallas_call | solution.py:175
  (2 shorter events, 0.1 us)
Async XLA Ops:
  1.7 19.5 %collective-permute-start = (f32[24,32,128]{2,1,0:T(8,128)S(1)}, f32[24,32,128]{2,1,0:T(8,128)S(1)}, u32[]{:S(2)}, u32[]{:S(2)}) collective-permute-start(f32[24,32,128]{2,1,0:T(8,128)S(1)} %get-tuple-element.24), channel_id=1, source_target_pairs={{0,1},{1,0},{2,3},{3,2},{4,5},{5,4},{6,7},{7,6},{8,9},{9,8},{10,11... | collective-permute-start | bytes 1179656 | tf_op jit(solution)/shard_map/ppermute | solution.py:584
  4.6 7.3 %collective-permute-start.1 = (f32[320,128]{1,0:T(8,128)S(1)}, f32[320,128]{1,0:T(8,128)S(1)}, u32[]{:S(2)}, u32[]{:S(2)}) collective-permute-start(f32[320,128]{1,0:T(8,128)S(1)} %get-tuple-element.25), channel_id=1, source_target_pairs={{0,32},{32,64},{64,96},{96,128},{128,160},{160,192},{192,224},{224... | collective-permute-start | bytes 491528 | tf_op jit(solution)/shard_map/ppermute | solution.py:576
  9.4 7.6 %collective-permute-start.2 = (f32[320,128]{1,0:T(8,128)S(1)}, f32[320,128]{1,0:T(8,128)S(1)}, u32[]{:S(2)}, u32[]{:S(2)}) collective-permute-start(f32[320,128]{1,0:T(8,128)S(1)} %get-tuple-element.26), channel_id=1, source_target_pairs={{32,0},{64,32},{96,64},{128,96},{160,128},{192,160},{224,192},{256... | collective-permute-start | bytes 491528 | tf_op jit(solution)/shard_map/ppermute | solution.py:580
  22.0 8.3 %collective-permute-start.3 = (f32[4,40,128]{2,1,0:T(8,128)S(1)}, f32[4,40,128]{2,1,0:T(8,128)S(1)}, u32[]{:S(2)}, u32[]{:S(2)}) collective-permute-start(f32[4,40,128]{2,1,0:T(8,128)S(1)} %get-tuple-element.28), channel_id=1, source_target_pairs={{0,2},{2,4},{4,6},{6,8},{8,10},{10,12},{12,14},{14,16},{16,18},{18... | collective-permute-start | bytes 245768 | tf_op jit(solution)/shard_map/ppermute | solution.py:576
  28.3 8.2 %collective-permute-start.4 = (f32[4,40,128]{2,1,0:T(8,128)S(1)}, f32[4,40,128]{2,1,0:T(8,128)S(1)}, u32[]{:S(2)}, u32[]{:S(2)}) collective-permute-start(f32[4,40,128]{2,1,0:T(8,128)S(1)} %get-tuple-element.29), channel_id=1, source_target_pairs={{2,0},{4,2},{6,4},{8,6},{10,8},{12,10},{14,12},{16,14},{18,16},{20... | collective-permute-start | bytes 245768 | tf_op jit(solution)/shard_map/ppermute | solution.py:580
  53.5 7.5 %collective-permute-start.5 = (f32[336,128]{1,0:T(8,128)S(1)}, f32[336,128]{1,0:T(8,128)S(1)}, u32[]{:S(2)}, u32[]{:S(2)}) collective-permute-start(f32[336,128]{1,0:T(8,128)S(1)} %get-tuple-element.32), channel_id=1, source_target_pairs={{0,32},{32,64},{64,96},{96,128},{128,160},{160,192},{192,224},{224... | collective-permute-start | bytes 516104 | tf_op jit(solution)/shard_map/ppermute | solution.py:576
  56.0 9.0 %collective-permute-start.6 = (f32[336,128]{1,0:T(8,128)S(1)}, f32[336,128]{1,0:T(8,128)S(1)}, u32[]{:S(2)}, u32[]{:S(2)}) collective-permute-start(f32[336,128]{1,0:T(8,128)S(1)} %get-tuple-element.33), channel_id=1, source_target_pairs={{32,0},{64,32},{96,64},{128,96},{160,128},{192,160},{224,192},{256... | collective-permute-start | bytes 516104 | tf_op jit(solution)/shard_map/ppermute | solution.py:580
  65.2 7.0 %collective-permute-start.7 = (f32[7,40,128]{2,1,0:T(8,128)S(1)}, f32[7,40,128]{2,1,0:T(8,128)S(1)}, u32[]{:S(2)}, u32[]{:S(2)}) collective-permute-start(f32[7,40,128]{2,1,0:T(8,128)S(1)} %get-tuple-element.35), channel_id=1, source_target_pairs={{0,2},{2,4},{4,6},{6,8},{8,10},{10,12},{12,14},{14,16},{16,18},{18... | collective-permute-start | bytes 430088 | tf_op jit(solution)/shard_map/ppermute | solution.py:576
  70.1 8.8 %collective-permute-start.8 = (f32[7,40,128]{2,1,0:T(8,128)S(1)}, f32[7,40,128]{2,1,0:T(8,128)S(1)}, u32[]{:S(2)}, u32[]{:S(2)}) collective-permute-start(f32[7,40,128]{2,1,0:T(8,128)S(1)} %get-tuple-element.36), channel_id=1, source_target_pairs={{2,0},{4,2},{6,4},{8,6},{10,8},{12,10},{14,12},{16,14},{18,16},{20... | collective-permute-start | bytes 430088 | tf_op jit(solution)/shard_map/ppermute | solution.py:580

commit v4 on v3

--- a/solution.py
+++ b/solution.py
@@ -277,69 +277,107 @@
             down_ref[k // 32] = falling
 
 
-def fine_down(gz_ref, ext_ref, low_ref, high_ref,
-              u_ref, load_ref, weight_ref, s_ref, send_ref,
-              y_ref, x_ref, hi_ref, q_ref, r_ref, rest_ref, pair_ref, rows_ref):
+def weigh(s_ref, weight_ref, planes, tiles):
+    for z in planes:
+        for t in tiles:
+            rows = pl.ds(8 * t, 8)
+            s = s_ref[z, rows, :] + s_ref[z - 1, rows, :]
+            if t:
+                before = pl.ds(8 * t - 1, 8)
+                back = s_ref[z, before, :] + s_ref[z - 1, before, :]
+            else:
+                back = pltpu.roll(s, 1, 0)
+            s = s + back
+            inverse = box_inverse(s + pltpu.roll(s, 1, 1), KDIAG)
+            for c in range(3):
+                weight_ref[c, z, rows, :] = weight_ref[c, z, rows, :] * inverse
+
+
+def down_stroke(gz, u_ref, load_ref, weight_ref, s_ref, rest_ref, work):
+    clear_work(*work)
+    weigh(s_ref, weight_ref, range(1, PLANES - 1), range(5))
+    sweep = smoother(u_ref, load_ref, weight_ref)
+    for k in range(2):
+        stencil(u_ref, s_ref, sweep, 3 - 2 * gz + k * gz, 10 - k, range(5), *work)
+
+    def remain(z, t, forces):
+        rows = pl.ds(8 * t, 8)
+        for c in range(3):
+            rest = load_ref[c, z, rows, :] - forces[c]
+            rest_ref[c, z - OWN, rows, :] = jnp.where(weight_ref[c, z, rows, :] > 0, rest, 0.0)
+
+    stencil(u_ref, s_ref, remain, OWN, 8, range(5), *work)
+
+
+def fine_main(gz_ref, ext_ref, u_ref, weight_ref, rest_ref, *work):
+    for z in range(PLANES):
+        for c in range(3):
+            u_ref[c, z] = ext_ref[c, z]
+            weight_ref[c, z] = ext_ref[6 + c, z]
+    down_stroke(gz_ref[0], u_ref, ext_ref.at[pl.ds(3, 3)], weight_ref, ext_ref.at[9], rest_ref, work)
+
+
+def fine_edges(gz_ref, ext_ref, low_ref, high_ref, main_u_ref, main_weight_ref, main_rest_ref,
+               u_ref, load_ref, weight_ref, s_ref, send_ref,
+               strip_u_ref, strip_load_ref, strip_weight_ref, strip_s_ref, strip_rest_ref,
+               rest_ref, pair_ref, rows_ref, halo_ref, *work):
     gz = gz_ref[0]
     blank = jnp.zeros((ROWS, 128), F32)
-    fields = [ref.at[c] for ref in (u_ref, load_ref, weight_ref) for c in range(3)] + [s_ref]
+    halos = {3: load_ref.at[0], 4: load_ref.at[1], 5: load_ref.at[2], 9: s_ref}
+    outer = list(range(OWN)) + list(range(OWN + 8, PLANES))
+    strips = [ref.at[c] for ref in (strip_u_ref, strip_load_ref, strip_weight_ref) for c in range(3)] + [strip_s_ref]
     for f in range(10):
+        for z in outer:
+            strips[f][z] = blank
+    for f, ref in halos.items():
         for z in range(PLANES):
-            fields[f][z, :, pl.ds(0, 128)] = ext_ref[f, z]
-        for z in list(range(OWN)) + list(range(OWN + 8, PLANES)):
-            fields[f][z, :, pl.ds(128, 128)] = blank
+            ref[z, :, pl.ds(0, 128)] = ext_ref[f, z]
+        for z in outer:
+            ref[z, :, pl.ds(128, 128)] = blank
     lane = lane_index((ROWS, 128))
+    left = (lane >= 60) & (lane < 72)
+    right = (lane < EDGE) | (lane >= 120)
     merged = [None, None]
     for k, (f, z) in enumerate(fine_places(gz)):
         group = k % 32
         if group == 0:
             for odd in range(2):
                 merged[odd] = jnp.where(lane // 4 % 2 == odd, low_ref[k // 32], high_ref[k // 32])
-        value = pltpu.roll(merged[group % 2], 124 - 4 * group, 1) if group < 31 else merged[1]
-        fields[f][z, :, pl.ds(128, 128)] = jnp.where((lane < EDGE) | (lane >= 128 - EDGE), value, 0.0)
-    clear_work(y_ref, x_ref, hi_ref, q_ref, r_ref)
+        halo_ref[k] = pltpu.roll(merged[group % 2], 124 - 4 * group, 1) if group < 31 else merged[1]
+    for k, (f, z) in enumerate(fine_places(gz)):
+        halo = halo_ref[k]
+        own = ext_ref[f, z]
+        turned = pltpu.roll(jnp.where(lane < 8, own, halo), 64, 1)
+        straight = jnp.where(lane < EDGE, halo, own)
+        strips[f][z] = jnp.where(left, turned, jnp.where(right, straight, 0.0))
+        if f in halos:
+            halos[f][z, :, pl.ds(128, 128)] = jnp.where((lane < EDGE) | (lane >= 128 - EDGE), halo, 0.0)
 
     for c in range(3):
         for z1 in range(4):
             z = OWN + 2 * z1
             pair_ref[0] = jnp.minimum(
-                weight_ref[c, z, :, pl.ds(0, 128)], weight_ref[c, z + 1, :, pl.ds(0, 128)]
+                ext_ref[6 + c, z], ext_ref[6 + c, z + 1]
             )
             least = jnp.minimum(pair_ref[0, pl.ds(4, 16, 2), :], pair_ref[0, pl.ds(5, 16, 2), :])
             rows_ref[pl.ds(32 * (4 + c) + 16 * (z1 // 2), 16), pl.ds(128 * (z1 % 2), 128)] = least
 
-    for z in range(1, PLANES - 1):
-        for t in range(5):
-            rows = pl.ds(8 * t, 8)
-            s = s_ref[z, rows, :] + s_ref[z - 1, rows, :]
-            for part in range(2):
-                r_ref[0, z % 6, part, rows, :] = s[:, 128 * part: 128 * part + 128]
-        for t in range(5):
-            rows = pl.ds(8 * t, 8)
-            s = s_ref[z, rows, :] + s_ref[z - 1, rows, :]
-            before = [
-                r_ref[0, z % 6, part, pl.ds(8 * t - 1, 8), :] if t else pltpu.roll(s[:, 128 * part: 128 * part + 128], 1, 0)
-                for part in range(2)
-            ]
-            s = s + jnp.concatenate(before, 1)
-            inverse = box_inverse(s + pltpu.roll(s, 1, 1), KDIAG)
-            for c in range(3):
-                weight_ref[c, z, rows, :] = weight_ref[c, z, rows, :] * inverse
-
-    sweep = smoother(u_ref, load_ref, weight_ref)
-    tiles = range(5)
-    work = (y_ref, x_ref, hi_ref, q_ref, r_ref)
-    for k in range(2):
-        stencil(u_ref, s_ref, sweep, 3 - 2 * gz + k * gz, 10 - k, tiles, *work)
-
-    def remain(z, t, forces):
-        rows = pl.ds(8 * t, 8)
-        here = pl.ds(0, 128)
-        for c in range(3):
-            rest = load_ref[c, z, rows, here] - forces[c][:, :128]
-            rest_ref[c, z - OWN, rows, :] = jnp.where(weight_ref[c, z, rows, here] > 0, rest, 0.0)
-
-    stencil(u_ref, s_ref, remain, OWN, 8, tiles, *work)
+    down_stroke(gz, strip_u_ref, strip_load_ref, strip_weight_ref, strip_s_ref, strip_rest_ref, work)
+
+    below, above = lane < EDGE, lane >= 128 - EDGE
+    for c in range(3):
+        for z in range(1, PLANES - 1):
+            for out_ref, main, strip in (
+                (u_ref, main_u_ref[c, z], strip_u_ref[c, z]),
+                (weight_ref, main_weight_ref[c, z], strip_weight_ref[c, z]),
+            ):
+                turned = pltpu.roll(strip, 64, 1)
+                out_ref[c, z, :, pl.ds(0, 128)] = jnp.where(below, turned, jnp.where(above, strip, main))
+                out_ref[c, z, :, pl.ds(128, 128)] = jnp.where(below, strip, jnp.where(above, turned, 0.0))
+        for z in range(8):
+            strip = strip_rest_ref[c, z]
+            turned = pltpu.roll(strip, 64, 1)
+            rest_ref[c, z] = jnp.where(below, turned, jnp.where(above, strip, main_rest_ref[c, z]))
 
     for c in range(3):
         for z1 in range(4):
@@ -423,13 +461,14 @@
 
 
 def coarse(gz_ref, ext_ref, low_ref, high_ref, old_ref, load_ref, weight_ref, s_ref, both_ref, out_ref,
-           u1_ref, v1_ref, u2_ref, v2_ref, state_ref, rest_ref, rows_ref, pair_ref, *work):
+           u1_ref, v1_ref, u2_ref, v2_ref, s2_ref, weight2_ref, state_ref, rest_ref, rows_ref, pair_ref, *work):
     work, fine_work = work[:5], work[5:]
     gz = gz_ref[0]
     lane = lane_index((ROWS, 128))
     clear_work(*work)
     clear_work(*fine_work)
-    clear(u2_ref, v2_ref)
+    clear(u2_ref, v2_ref, weight2_ref)
+    s2_ref[...] = jnp.zeros(s2_ref.shape, F32)
     for f in range(7):
         for z in (0, 9):
             v1_ref[f, z] = jnp.zeros((ROWS, 128), F32)
@@ -488,28 +527,17 @@
     for z2 in range(4):
         for c in range(3):
             v2_ref[c, 1 + z2] = part(c, z2)
-            v2_ref[4 + c, 1 + z2] = jnp.where(part(4 + c, z2) > 1.5, 1.0, 0.0)
-        v2_ref[3, 1 + z2] = part(3, z2) * (4.0 / 2.0 / 8.0)
+            weight2_ref[c, 1 + z2] = jnp.where(part(4 + c, z2) > 1.5, 1.0, 0.0)
+        s2_ref[1 + z2] = part(3, z2) * (4.0 / 2.0 / 8.0)
+    weigh(s2_ref, weight2_ref, range(1, 5), range(3))
     for z in range(1, 5):
-        for t in range(3):
-            rows = pl.ds(8 * t, 8)
-            s = v2_ref[3, z, rows, :] + v2_ref[3, z - 1, rows, :]
-            if t:
-                before = pl.ds(8 * t - 1, 8)
-                back = v2_ref[3, z, before, :] + v2_ref[3, z - 1, before, :]
-            else:
-                back = pltpu.roll(s, 1, 0)
-            s = s + back
-            inverse = box_inverse(s + pltpu.roll(s, 1, 1), KDIAG)
-            for c in range(3):
-                weight = v2_ref[4 + c, z, rows, :] * inverse
-                v2_ref[4 + c, z, rows, :] = weight
-                u2_ref[c, z, rows, :] = weight * v2_ref[c, z, rows, :]
-
-    sweep2 = smoother(u2_ref, v2_ref, v2_ref.at[pl.ds(4, 3)])
+        for c in range(3):
+            u2_ref[c, z] = weight2_ref[c, z] * v2_ref[c, z]
+
+    sweep2 = smoother(u2_ref, v2_ref, weight2_ref)
 
     def again(k, carry):
-        stencil(u2_ref, v2_ref.at[3], sweep2, 1, 4, range(3), *work)
+        stencil(u2_ref, s2_ref, sweep2, 1, 4, range(3), *work)
         return carry
 
     lax.fori_loop(0, COARSE - 1, again, 0)
@@ -622,12 +650,24 @@
     )
     low, high = up(rising, "gy"), down(falling, "gy")
     wide = (3, PLANES, ROWS, LANES)
+    tile, rest = (3, PLANES, ROWS, 128), (3, 8, ROWS, 128)
+    main = call(fine_main, [tile, tile, rest], [gz, ext], scratch_of(ROWS, 128, 10))
     u, loads, weights, scales, send1 = call(
-        fine_down,
+        fine_edges,
         [wide, wide, wide, (PLANES, ROWS, LANES), (48, 8, 128)],
-        [gz, ext, low, high],
-        scratch_of(ROWS, LANES, 10)
-        + [pltpu.VMEM((3, 8, ROWS, 128), F32), pltpu.VMEM((2, ROWS, 128), F32), pltpu.VMEM((256, 256), F32)],
+        [gz, ext, low, high, *main],
+        [
+            pltpu.VMEM(tile, F32),
+            pltpu.VMEM(tile, F32),
+            pltpu.VMEM(tile, F32),
+            pltpu.VMEM(tile[1:], F32),
+            pltpu.VMEM(rest, F32),
+            pltpu.VMEM(rest, F32),
+            pltpu.VMEM((2, ROWS, 128), F32),
+            pltpu.VMEM((256, 256), F32),
+            pltpu.VMEM((104, ROWS, 128), F32),
+        ]
+        + scratch_of(ROWS, 128, 10),
     )
     both = lax.all_gather(send1, "gz")
     full, right, left = call(edge_rows1, [(7, 4, 16, 128), (336, 128), (336, 128)], [gz, both])
@@ -644,7 +684,9 @@
             pltpu.VMEM((3, 10, ROWS, 128), F32),
             pltpu.VMEM((7, 10, ROWS, 128), F32),
             pltpu.VMEM((3, 6, 24, 128), F32),
-            pltpu.VMEM((7, 6, 24, 128), F32),
+            pltpu.VMEM((3, 6, 24, 128), F32),
+            pltpu.VMEM((6, 24, 128), F32),
+            pltpu.VMEM((3, 6, 24, 128), F32),
             pltpu.VMEM(wide, F32),
             pltpu.VMEM((3, 10, ROWS, 128), F32),
             pltpu.VMEM((672, 128), F32),

time: 96 us -> 93.6 us (0.975)
  the two profiles are of different devices: /device:TPU:115 before, /device:TPU:99 now
where the time goes in v4:
time: 93.6 us; the launch traced here: 93.2 us
  starting transfers between devices  34.7 us (37%)
  Pallas kernels  32.7 us (35%)
  waiting for transfers between devices  16.1 us (17%)
  blocking collectives  9.62 us (10%)
    pallas_call x8, Pallas kernels, call(): pl.pallas_call(body, out_shape=tuple((shape(out, F32) for out in outs)),...  32.7 us
    ppermute x4, starting transfers between devices, up(): lax.ppermute(value, axis, [(i, i + 1) for i in range(lax.axis_size(axis)...  22.8 us
    ppermute x4, waiting for transfers between devices, down(): lax.ppermute(value, axis, [(i + 1, i) for i in range(lax.axis_size(axis)...  14.6 us
    ppermute x4, starting transfers between devices, down(): lax.ppermute(value, axis, [(i + 1, i) for i in range(lax.axis_size(axis)...  8.71 us
    all_gather x1, blocking collectives, on_device(): both = lax.all_gather(send1, 'gz')  5.49 us
    all_gather x1, blocking collectives, on_device(): beside = lax.all_gather(zsend, 'gz')  4.13 us
    ppermute x1, starting transfers between devices, swap(): return lax.ppermute(value, 'gz', [(0, 1), (1, 0)])  3.2 us
  transfers between devices with their start and end apart: 9, of which 5 were waited for; matrix products, arithmetic and copies ran while one was open for 0% of the time, Pallas kernels for 6%

profile of v4, /device:TPU:99, one launch (start us, length us, event | category | flops | bytes accessed | tf_op | source)
XLA Modules:
  0.0 93.2 jit_solution(3029561812631275172)
XLA Ops:
  0.0 1.7 %shard_map.46 = (f32[24,32,128]{2,1,0:T(8,128)S(1)}, f32[10,8,32,128]{3,2,1,0:T(8,128)S(1)}, f32[320,128]{1,0:T(8,128)S(1)}, f32[320,128]{1,0:T(8,128)S(1)}) custom-call(s32[1]{0:T(128)} %bitcast.gz_ref, f32[3,8,32,128]{3,2,1,0:T(8,128)} %disp_hbm.1, f32[3,8,32,128]{3,2,1,0:T(8,128)} %load_hbm.1, s32[8,32,128]{2,1,0:T(8,128)} %code_hbm.1, ...), custom_call_target="tpu_custom_call" | custom-call | tf_op jit(solution)/shard_map/pallas_call | solution.py:175
  1.7 3.2 %collective-permute-start = (f32[24,32,128]{2,1,0:T(8,128)S(1)}, f32[24,32,128]{2,1,0:T(8,128)S(1)}, u32[]{:S(2)}, u32[]{:S(2)}) collective-permute-start(f32[24,32,128]{2,1,0:T(8,128)S(1)} %get-tuple-element.27), channel_id=1, source_target_pairs={{0,1},{1,0},{2,3},{3,2},{4,5},{5,4},{6,7},{7,6},{8,9},{9,8},{10,11... | collective-permute-start | bytes 1179656 | tf_op jit(solution)/shard_map/ppermute | solution.py:612
  4.9 4.8 %collective-permute-start.1 = (f32[320,128]{1,0:T(8,128)S(1)}, f32[320,128]{1,0:T(8,128)S(1)}, u32[]{:S(2)}, u32[]{:S(2)}) collective-permute-start(f32[320,128]{1,0:T(8,128)S(1)} %get-tuple-element.28), channel_id=1, source_target_pairs={{0,32},{32,64},{64,96},{96,128},{128,160},{160,192},{192,224},{224... | collective-permute-start | bytes 491528 | tf_op jit(solution)/shard_map/ppermute | solution.py:604
  9.6 1.9 %collective-permute-start.2 = (f32[320,128]{1,0:T(8,128)S(1)}, f32[320,128]{1,0:T(8,128)S(1)}, u32[]{:S(2)}, u32[]{:S(2)}) collective-permute-start(f32[320,128]{1,0:T(8,128)S(1)} %get-tuple-element.29), channel_id=1, source_target_pairs={{32,0},{64,32},{96,64},{128,96},{160,128},{192,160},{224,192},{256... | collective-permute-start | bytes 491528 | tf_op jit(solution)/shard_map/ppermute | solution.py:608
  11.6 0.7 collective-permute-done.1.low_ref
  12.2 5.0 %collective-permute-done.2.high_ref = f32[320,128]{1,0:T(8,128)S(1)} collective-permute-done((f32[320,128]{1,0:T(8,128)S(1)}, f32[320,128]{1,0:T(8,128)S(1)}, u32[]{:S(2)}, u32[]{:S(2)}) %collective-permute-start.2) | collective-permute-done | bytes 163872 | tf_op jit(solution)/shard_map/ppermute | solution.py:608
  17.3 4.1 %all-gather = f32[384,128]{1,0:T(8,128)S(1)} all-gather(f32[192,128]{1,0:T(8,128)S(1)} %shard_map.47), channel_id=2, replica_groups=mesh['gx'=16,'gy'=16,'gz'=2] {'gz'}, dimensions={0}, use_global_device_ids=true | all-gather | bytes 294912 | tf_op jit(solution)/shard_map/all_gather | solution.py:645
  21.4 0.0 collective-permute-done.zrecv_ref
  21.4 0.8 shard_map.48
  22.3 7.7 %collective-permute-start.3 = (f32[4,40,128]{2,1,0:T(8,128)S(1)}, f32[4,40,128]{2,1,0:T(8,128)S(1)}, u32[]{:S(2)}, u32[]{:S(2)}) collective-permute-start(f32[4,40,128]{2,1,0:T(8,128)S(1)} %get-tuple-element.31), channel_id=1, source_target_pairs={{0,2},{2,4},{4,6},{6,8},{8,10},{10,12},{12,14},{14,16},{16,18},{18... | collective-permute-start | bytes 245768 | tf_op jit(solution)/shard_map/ppermute | solution.py:604
  29.9 1.9 %collective-permute-start.4 = (f32[4,40,128]{2,1,0:T(8,128)S(1)}, f32[4,40,128]{2,1,0:T(8,128)S(1)}, u32[]{:S(2)}, u32[]{:S(2)}) collective-permute-start(f32[4,40,128]{2,1,0:T(8,128)S(1)} %get-tuple-element.32), channel_id=1, source_target_pairs={{2,0},{4,2},{6,4},{8,6},{10,8},{12,10},{14,12},{16,14},{18,16},{20... | collective-permute-start | bytes 245768 | tf_op jit(solution)/shard_map/ppermute | solution.py:608
  31.9 5.3 %shard_map.49 = (f32[3,14,40,128]{3,2,1,0:T(8,128)S(1)}, f32[3,14,40,128]{3,2,1,0:T(8,128)S(1)}, f32[3,8,40,128]{3,2,1,0:T(8,128)S(1)}) custom-call(s32[1]{0:T(128)} %bitcast.gz_ref, f32[10,14,40,128]{3,2,1,0:T(8,128)S(1)} %get-tuple-element.30.ext_ref), custom_call_target="tpu_custom_call" | custom-call | tf_op jit(solution)/shard_map/pallas_call | solution.py:175
  37.2 0.0 collective-permute-done.3.low_ref
  37.2 0.0 collective-permute-done.4.high_ref
  37.2 7.9 %shard_map.50 = (f32[3,14,40,256]{3,2,1,0:T(8,128)S(1)}, f32[3,14,40,256]{3,2,1,0:T(8,128)S(1)}, f32[3,14,40,256]{3,2,1,0:T(8,128)S(1)}, f32[14,40,256]{2,1,0:T(8,128)S(1)}, f32[48,8,128]{2,1,0:T(8,128)S(1)}) custom-call(s32[1]{0:T(128)} %bitcast.gz_ref, f32[10,14,40,128]{3,2,1,0:T(8,128)S(1)} %get-tuple-element.30.ext_ref, ...), custom_call_target="tpu_custom_call" | custom-call | tf_op jit(solution)/shard_map/pallas_call | solution.py:175
  45.1 5.5 %all-gather.1 = f32[96,8,128]{2,1,0:T(8,128)S(1)} all-gather(f32[48,8,128]{2,1,0:T(8,128)S(1)} %get-tuple-element.36), channel_id=3, replica_groups=mesh['gx'=16,'gy'=16,'gz'=2] {'gz'}, dimensions={0}, use_global_device_ids=true | all-gather | bytes 589824 | tf_op jit(solution)/shard_map/all_gather | solution.py:672
  50.7 2.5 %collective-permute-start.5 = (f32[336,128]{1,0:T(8,128)S(1)}, f32[336,128]{1,0:T(8,128)S(1)}, u32[]{:S(2)}, u32[]{:S(2)}) collective-permute-start(f32[336,128]{1,0:T(8,128)S(1)} %get-tuple-element.38), channel_id=1, source_target_pairs={{0,32},{32,64},{64,96},{96,128},{128,160},{160,192},{192,224},{224... | collective-permute-start | bytes 516104 | tf_op jit(solution)/shard_map/ppermute | solution.py:604
  53.2 2.8 %collective-permute-start.6 = (f32[336,128]{1,0:T(8,128)S(1)}, f32[336,128]{1,0:T(8,128)S(1)}, u32[]{:S(2)}, u32[]{:S(2)}) collective-permute-start(f32[336,128]{1,0:T(8,128)S(1)} %get-tuple-element.39), channel_id=1, source_target_pairs={{32,0},{64,32},{96,64},{128,96},{160,128},{192,160},{224,192},{256... | collective-permute-start | bytes 516104 | tf_op jit(solution)/shard_map/ppermute | solution.py:608
  56.0 0.9 collective-permute-done.5.low_ref
  56.8 3.7 %collective-permute-done.6.high_ref = f32[336,128]{1,0:T(8,128)S(1)} collective-permute-done((f32[336,128]{1,0:T(8,128)S(1)}, f32[336,128]{1,0:T(8,128)S(1)}, u32[]{:S(2)}, u32[]{:S(2)}) %collective-permute-start.6) | collective-permute-done | bytes 172064 | tf_op jit(solution)/shard_map/ppermute | solution.py:608
  60.6 0.2 shard_map.52
  60.8 7.8 %collective-permute-start.7 = (f32[7,40,128]{2,1,0:T(8,128)S(1)}, f32[7,40,128]{2,1,0:T(8,128)S(1)}, u32[]{:S(2)}, u32[]{:S(2)}) collective-permute-start(f32[7,40,128]{2,1,0:T(8,128)S(1)} %get-tuple-element.41), channel_id=1, source_target_pairs={{0,2},{2,4},{4,6},{6,8},{8,10},{10,12},{12,14},{14,16},{16,18},{18... | collective-permute-start | bytes 430088 | tf_op jit(solution)/shard_map/ppermute | solution.py:604
  68.6 2.1 %collective-permute-start.8 = (f32[7,40,128]{2,1,0:T(8,128)S(1)}, f32[7,40,128]{2,1,0:T(8,128)S(1)}, u32[]{:S(2)}, u32[]{:S(2)}) collective-permute-start(f32[7,40,128]{2,1,0:T(8,128)S(1)} %get-tuple-element.42), channel_id=1, source_target_pairs={{2,0},{4,2},{6,4},{8,6},{10,8},{12,10},{14,12},{16,14},{18,16},{20... | collective-permute-start | bytes 430088 | tf_op jit(solution)/shard_map/ppermute | solution.py:608
  70.7 0.0 collective-permute-done.7.low_ref
  70.7 5.8 %collective-permute-done.8.high_ref = f32[7,40,128]{2,1,0:T(8,128)S(1)} collective-permute-done((f32[7,40,128]{2,1,0:T(8,128)S(1)}, f32[7,40,128]{2,1,0:T(8,128)S(1)}, u32[]{:S(2)}, u32[]{:S(2)}) %collective-permute-start.8) | collective-permute-done | bytes 143392 | tf_op jit(solution)/shard_map/ppermute | solution.py:608
  76.5 16.7 %shard_map.53 = f32[3,8,32,128]{3,2,1,0:T(8,128)} custom-call(s32[1]{0:T(128)} %bitcast.gz_ref, f32[7,4,40,128]{3,2,1,0:T(8,128)S(1)} %get-tuple-element.40.ext_ref, f32[7,40,128]{2,1,0:T(8,128)S(1)} %collective-permute-done.7.low_ref, f32[7,40,128]{2,1,0:T(8,128)S(1)} %collective-permute-done.8.high_ref, f32[3,14,40,256]{3,2,1,0:T(8,128)S(1)} %get-tuple-element.43.old_ref, ...), custom_call_target="tpu_custom_call" | custom-call | tf_op jit(solution)/shard_map/pallas_call | solution.py:175
  (2 shorter events, 0.1 us)
Async XLA Ops:
  1.7 19.8 %collective-permute-start = (f32[24,32,128]{2,1,0:T(8,128)S(1)}, f32[24,32,128]{2,1,0:T(8,128)S(1)}, u32[]{:S(2)}, u32[]{:S(2)}) collective-permute-start(f32[24,32,128]{2,1,0:T(8,128)S(1)} %get-tuple-element.27), channel_id=1, source_target_pairs={{0,1},{1,0},{2,3},{3,2},{4,5},{5,4},{6,7},{7,6},{8,9},{9,8},{10,11... | collective-permute-start | bytes 1179656 | tf_op jit(solution)/shard_map/ppermute | solution.py:612
  4.9 7.3 %collective-permute-start.1 = (f32[320,128]{1,0:T(8,128)S(1)}, f32[320,128]{1,0:T(8,128)S(1)}, u32[]{:S(2)}, u32[]{:S(2)}) collective-permute-start(f32[320,128]{1,0:T(8,128)S(1)} %get-tuple-element.28), channel_id=1, source_target_pairs={{0,32},{32,64},{64,96},{96,128},{128,160},{160,192},{192,224},{224... | collective-permute-start | bytes 491528 | tf_op jit(solution)/shard_map/ppermute | solution.py:604
  9.6 7.6 %collective-permute-start.2 = (f32[320,128]{1,0:T(8,128)S(1)}, f32[320,128]{1,0:T(8,128)S(1)}, u32[]{:S(2)}, u32[]{:S(2)}) collective-permute-start(f32[320,128]{1,0:T(8,128)S(1)} %get-tuple-element.29), channel_id=1, source_target_pairs={{32,0},{64,32},{96,64},{128,96},{160,128},{192,160},{224,192},{256... | collective-permute-start | bytes 491528 | tf_op jit(solution)/shard_map/ppermute | solution.py:608
  22.3 15.0 %collective-permute-start.3 = (f32[4,40,128]{2,1,0:T(8,128)S(1)}, f32[4,40,128]{2,1,0:T(8,128)S(1)}, u32[]{:S(2)}, u32[]{:S(2)}) collective-permute-start(f32[4,40,128]{2,1,0:T(8,128)S(1)} %get-tuple-element.31), channel_id=1, source_target_pairs={{0,2},{2,4},{4,6},{6,8},{8,10},{10,12},{12,14},{14,16},{16,18},{18... | collective-permute-start | bytes 245768 | tf_op jit(solution)/shard_map/ppermute | solution.py:604
  29.9 7.3 %collective-permute-start.4 = (f32[4,40,128]{2,1,0:T(8,128)S(1)}, f32[4,40,128]{2,1,0:T(8,128)S(1)}, u32[]{:S(2)}, u32[]{:S(2)}) collective-permute-start(f32[4,40,128]{2,1,0:T(8,128)S(1)} %get-tuple-element.32), channel_id=1, source_target_pairs={{2,0},{4,2},{6,4},{8,6},{10,8},{12,10},{14,12},{16,14},{18,16},{20... | collective-permute-start | bytes 245768 | tf_op jit(solution)/shard_map/ppermute | solution.py:608
  50.7 6.2 %collective-permute-start.5 = (f32[336,128]{1,0:T(8,128)S(1)}, f32[336,128]{1,0:T(8,128)S(1)}, u32[]{:S(2)}, u32[]{:S(2)}) collective-permute-start(f32[336,128]{1,0:T(8,128)S(1)} %get-tuple-element.38), channel_id=1, source_target_pairs={{0,32},{32,64},{64,96},{96,128},{128,160},{160,192},{192,224},{224... | collective-permute-start | bytes 516104 | tf_op jit(solution)/shard_map/ppermute | solution.py:604
  53.2 7.4 %collective-permute-start.6 = (f32[336,128]{1,0:T(8,128)S(1)}, f32[336,128]{1,0:T(8,128)S(1)}, u32[]{:S(2)}, u32[]{:S(2)}) collective-permute-start(f32[336,128]{1,0:T(8,128)S(1)} %get-tuple-element.39), channel_id=1, source_target_pairs={{32,0},{64,32},{96,64},{128,96},{160,128},{192,160},{224,192},{256... | collective-permute-start | bytes 516104 | tf_op jit(solution)/shard_map/ppermute | solution.py:608
  60.8 10.0 %collective-permute-start.7 = (f32[7,40,128]{2,1,0:T(8,128)S(1)}, f32[7,40,128]{2,1,0:T(8,128)S(1)}, u32[]{:S(2)}, u32[]{:S(2)}) collective-permute-start(f32[7,40,128]{2,1,0:T(8,128)S(1)} %get-tuple-element.41), channel_id=1, source_target_pairs={{0,2},{2,4},{4,6},{6,8},{8,10},{10,12},{12,14},{14,16},{16,18},{18... | collective-permute-start | bytes 430088 | tf_op jit(solution)/shard_map/ppermute | solution.py:604
  68.6 7.9 %collective-permute-start.8 = (f32[7,40,128]{2,1,0:T(8,128)S(1)}, f32[7,40,128]{2,1,0:T(8,128)S(1)}, u32[]{:S(2)}, u32[]{:S(2)}) collective-permute-start(f32[7,40,128]{2,1,0:T(8,128)S(1)} %get-tuple-element.42), channel_id=1, source_target_pairs={{2,0},{4,2},{6,4},{8,6},{10,8},{12,10},{14,12},{16,14},{18,16},{20... | collective-permute-start | bytes 430088 | tf_op jit(solution)/shard_map/ppermute | solution.py:608
